TPU v7x, 512 devices: a whole 4x8x8 slice. The times are simulated.
512 devices in a mesh: cons: 16 (over y, x_lo), blk: 32 (over x_hi, z, core).
Axes of the slice: x: 4 (x_hi: 2, x_lo: 2; x = x_hi * 2 + x_lo), y: 8, z: 8, core: 2. Of those that a mesh axis runs over, the one named last changes fastest.
Arguments:
- elevation: bfloat16 [16, 1280, 6144], P('cons', 'blk'), may hold values from -6 to 6
- legendre: bfloat16 [1280, 768, 768], P('blk', 'cons'), may hold values from -5 to 5, as said below
- cycle_weight: float32 [1280], P('blk'), may hold values from 0.0001782951 to 0.0014263608
- love_factor: float32 [768], replicated, may hold values from 0.000390625 to 0.0052083335
- assignment: int32 [16], replicated, may hold values from 0 to 15, each once
Outputs:
- loading: float32 [16, 1280, 6144], P('cons', 'blk')
Inputs may be any that keep to these rules, and one draw needn't show every extreme that they name: `legendre`: fully normalized associated Legendre functions (the square integrates to 1 over [-1, 1]) of each cycle's latitude, every cycle within 26 degrees of the equator; zero where the degree is below the order.
All inputs are finite; a program needn't handle non-finite values.
Results may differ from a plain program's by a relative error of at most 0.02.
Values may be sent and summed in bfloat16 or wider, within the bound.
No kernel may reach another device: no remote copies, remote signals or barrier semaphores. Data moves between devices by JAX's collectives and lax.ppermute only.
A program may use at most 128 MiB of HBM per device.

v0:
```python
import jax
import jax.numpy as jnp
import numpy as np
from jax import lax
from jax.experimental import pallas as pl
from jax.experimental.pallas import tpu as pltpu
from jax.sharding import Mesh
from jax.sharding import PartitionSpec as P

BLK = ("blk_0", "blk_1", "blk_2", "blk_3")
NEAR = ("blk_0", "blk_2", "blk_3")
FAR = "blk_1"
TEAM = ("cons", *NEAR)
FINE = 16
INNER = FINE * FINE
LANES = 128
NEAR_SIZE = 8
SHARE = 6
EARLY = (6, 7)
LATE = (4, 2, 5, 3, 1)
ROOM = 24 << 20
SCALARS = pl.BlockSpec(memory_space=pltpu.SMEM)
NEARBY = pl.BlockSpec(memory_space=pltpu.VMEM)


def angle_tables(steps, stride, period, orders):
    phases = (np.arange(steps)[:, None] * stride * np.arange(orders)[None, :]) % period
    angles = phases * (2.0 * np.pi / period)
    return np.stack([np.cos(angles), np.sin(angles)]).astype(np.float32)


def inner_table(coarse_ref, fine_ref, table_ref, lanes):
    fine_cos, fine_sin = fine_ref[0, :, lanes], fine_ref[1, :, lanes]
    for step in range(FINE):
        rows = slice(step * FINE, (step + 1) * FINE)
        coarse_cos = coarse_ref[0, step : step + 1, lanes]
        coarse_sin = coarse_ref[1, step : step + 1, lanes]
        cosine = coarse_cos * fine_cos - coarse_sin * fine_sin
        sine = coarse_sin * fine_cos + coarse_cos * fine_sin
        table_ref[0, rows, lanes] = cosine.astype(jnp.bfloat16)
        table_ref[1, rows, lanes] = (-sine).astype(jnp.bfloat16)


def shift(values, amount):
    amount %= LANES
    return values if amount == 0 else pltpu.roll(values, amount, values.ndim - 1)


def side_by_side(pieces, width):
    lane = lax.broadcasted_iota(jnp.int32, pieces[0].shape, pieces[0].ndim - 1)
    joined = jnp.zeros_like(pieces[0])
    for index, piece in reversed(list(enumerate(pieces))):
        joined = jnp.where(lane < (index + 1) * width, shift(piece, index * width), joined)
    return jnp.where(lane < len(pieces) * width, joined, 0.0)


def forward_kernel(
    elevation_ref,
    weight_ref,
    coarse_ref,
    fine_ref,
    turn_ref,
    out_ref,
    rows_ref,
    table_ref,
    flip_ref,
    pack_ref,
):
    cycles = elevation_ref.shape[0]
    turns = turn_ref.shape[1]
    orders = flip_ref.shape[1]
    for turn in range(turns):
        rows_ref[turn * cycles : (turn + 1) * cycles, :] = elevation_ref[
            :, turn * INNER : (turn + 1) * INNER
        ]
    weight = weight_ref[...]
    inner_table(coarse_ref, fine_ref, table_ref, slice(None))
    for part in range(orders // INNER):
        lanes = slice(part * INNER, (part + 1) * INNER)
        even = jnp.dot(rows_ref[...], table_ref[0, :, lanes], preferred_element_type=jnp.float32)
        odd = jnp.dot(rows_ref[...], table_ref[1, :, lanes], preferred_element_type=jnp.float32)
        first = second = None
        for turn in range(turns):
            rows = slice(turn * cycles, (turn + 1) * cycles)
            cosine, sine = turn_ref[0, turn : turn + 1, lanes], turn_ref[1, turn : turn + 1, lanes]
            one = even[rows] * cosine + odd[rows] * sine
            two = odd[rows] * cosine - even[rows] * sine
            first = one if first is None else first + one
            second = two if second is None else second + two
        flip_ref[0, lanes, :cycles] = jnp.transpose(first * weight)
        flip_ref[1, lanes, :cycles] = jnp.transpose(second * weight)

    beside = LANES // cycles
    peers = orders // SHARE
    deep = out_ref.shape[0] // peers
    for row in range(deep):
        pieces = []
        for column in range(beside):
            which, order = divmod(deep * column + row, SHARE)
            pieces.append(flip_ref[which, pl.ds(order, peers, stride=SHARE), :])
        pack_ref[pl.ds(row, peers, stride=deep), :] = side_by_side(pieces, cycles)
    out_ref[...] = pack_ref[...].astype(jnp.bfloat16)


def forward(elevation, weight, coarse, fine, turn, lines):
    cycles, longitudes = elevation.shape
    orders = coarse.shape[2]
    turns = longitudes // INNER
    return pl.pallas_call(
        forward_kernel,
        in_specs=[NEARBY] * 5,
        out_specs=NEARBY,
        out_shape=jax.ShapeDtypeStruct((lines, LANES), jnp.bfloat16),
        scratch_shapes=[
            pltpu.VMEM((turns * cycles, INNER), jnp.bfloat16),
            pltpu.VMEM((2, INNER, orders), jnp.bfloat16),
            pltpu.VMEM((2, orders, LANES), jnp.float32),
            pltpu.VMEM((lines, LANES), jnp.float32),
        ],
        cost_estimate=pl.CostEstimate(
            flops=4 * cycles * longitudes * orders, bytes_accessed=1 << 20, transcendentals=0
        ),
        compiler_params=pltpu.CompilerParams(vmem_limit_bytes=ROOM),
        name="forward_dft",
    )(elevation, weight, coarse, fine, turn)


def analysis_kernel(spot_ref, *refs):
    near = NEAR_SIZE
    assignment_ref, moved_ref, *value_refs = refs[: near + 2]
    out_ref, row_ref, left_ref, joined_ref = refs[near + 2 :]
    share, _, two_fields, _ = left_ref.shape
    fields = two_fields // 2
    cycles = value_refs[0].shape[1]
    beside = LANES // cycles
    lines = moved_ref.shape[0]
    block = lines // fields
    deep = block // near
    spot = spot_ref[0]

    for slot in range(fields):
        source = pl.multiple_of(assignment_ref[slot] * block, block)
        row_ref[slot * block : (slot + 1) * block, :] = moved_ref[
            pl.ds(source, block), :
        ].astype(jnp.float32)
    for other in range(near):
        peer = jnp.bitwise_xor(spot, other)
        for row in range(deep):
            taken = row_ref[pl.ds(peer * deep + row, fields, stride=block), :]
            for column in range(beside):
                which, order = divmod(deep * column + row, share)
                left_ref[order, other, which * fields : (which + 1) * fields, :] = shift(
                    taken, -column * cycles
                ).astype(jnp.bfloat16)

    for order in range(share):
        for other in range(near):
            joined_ref[order % 2, other * cycles : (other + 1) * cycles, :] = value_refs[other][
                order
            ]
        left = jnp.concatenate(
            [left_ref[order, other][:, :cycles] for other in range(near)], axis=1
        )
        out_ref[2 * fields * order : 2 * fields * (order + 1), :] = jnp.dot(
            left, joined_ref[order % 2], preferred_element_type=jnp.float32
        ).astype(jnp.bfloat16)


def analyse(spot, assignment, moved, values):
    share, cycles, degrees = values[0].shape
    fields = assignment.shape[0]
    return pl.pallas_call(
        analysis_kernel,
        in_specs=[SCALARS] * 2 + [NEARBY] * (1 + len(values)),
        out_specs=NEARBY,
        scratch_shapes=[
            pltpu.VMEM(moved.shape, jnp.float32),
            pltpu.VMEM((share, len(values), 2 * fields, LANES), jnp.bfloat16),
            pltpu.VMEM((2, len(values) * cycles, degrees), jnp.bfloat16),
        ],
        out_shape=jax.ShapeDtypeStruct((share * 2 * fields, degrees), jnp.bfloat16),
        cost_estimate=pl.CostEstimate(
            flops=4 * fields * share * cycles * degrees * len(values),
            bytes_accessed=4 << 20,
            transcendentals=0,
        ),
        compiler_params=pltpu.CompilerParams(vmem_limit_bytes=ROOM),
        name="analysis",
    )(spot, assignment, moved, *values)


def synthesis_kernel(spot_ref, first_ref, *refs):
    near = NEAR_SIZE
    coefficient_ref, *value_refs = refs[: near + 1]
    out_ref, right_ref, row_ref, joined_ref = refs[near + 1 :]
    share, _, two_fields, _ = right_ref.shape
    fields = two_fields // 2
    cycles = value_refs[0].shape[1]
    beside = LANES // cycles
    lines = out_ref.shape[0]
    block = lines // fields
    deep = block // near
    dims = (((1,), (1,)), ((), ()))
    for order in range(share):
        factor = jnp.where(first_ref[0] + order == 0, 1.0, 2.0).astype(jnp.float32)
        for other in range(near):
            joined_ref[order % 2, other * cycles : (other + 1) * cycles, :] = value_refs[other][
                order
            ]
        product = factor * lax.dot_general(
            coefficient_ref[2 * fields * order : 2 * fields * (order + 1), :],
            joined_ref[order % 2],
            dims,
            preferred_element_type=jnp.float32,
        )
        for other in range(near):
            right_ref[order, other, :, :cycles] = product[
                :, other * cycles : (other + 1) * cycles
            ]
    for other in range(near):
        peer = jnp.bitwise_xor(spot_ref[0], other)
        for row in range(deep):
            pieces = []
            for column in range(beside):
                which, own = divmod(deep * column + row, share)
                pieces.append(right_ref[own, other, which * fields : (which + 1) * fields, :])
            row_ref[pl.ds(peer * deep + row, fields, stride=block), :] = side_by_side(
                pieces, cycles
            )
    out_ref[...] = row_ref[...].astype(jnp.bfloat16)


def synthesise(spot, first, coefficients, values, lines):
    share, cycles, degrees = values[0].shape
    fields = coefficients.shape[0] // (2 * share)
    return pl.pallas_call(
        synthesis_kernel,
        in_specs=[SCALARS] * 2 + [NEARBY] * (1 + len(values)),
        out_specs=NEARBY,
        scratch_shapes=[
            pltpu.VMEM((share, len(values), 2 * fields, LANES), jnp.float32),
            pltpu.VMEM((lines, LANES), jnp.float32),
            pltpu.VMEM((2, len(values) * cycles, degrees), jnp.bfloat16),
        ],
        out_shape=jax.ShapeDtypeStruct((lines, LANES), jnp.bfloat16),
        cost_estimate=pl.CostEstimate(
            flops=4 * fields * share * cycles * degrees * len(values),
            bytes_accessed=4 << 20,
            transcendentals=0,
        ),
        compiler_params=pltpu.CompilerParams(vmem_limit_bytes=ROOM),
        name="synthesis",
    )(spot, first, coefficients, *values)


def inverse_kernel(
    moved_ref,
    coarse_ref,
    fine_ref,
    turn_ref,
    out_ref,
    rows_ref,
    table_ref,
    row_ref,
    flip_ref,
    part_ref,
    sems,
):
    parts, cycles, span = part_ref.shape
    count = span // INNER
    orders = flip_ref.shape[1]
    inner_table(coarse_ref, fine_ref, table_ref, slice(None))
    row_ref[...] = moved_ref[...].astype(jnp.float32)
    peers = orders // SHARE
    deep = moved_ref.shape[0] // peers
    for row in range(deep):
        taken = row_ref[pl.ds(row, peers, stride=deep), :]
        for column in range(LANES // cycles):
            which, order = divmod(deep * column + row, SHARE)
            flip_ref[which, pl.ds(order, peers, stride=SHARE), :] = shift(
                taken, -column * cycles
            )
    first = jnp.transpose(flip_ref[0])[:cycles]
    second = jnp.transpose(flip_ref[1])[:cycles]
    dims = (((1,), (1,)), ((), ()))
    copies = []
    for part in range(parts):
        for step in range(count):
            rows = slice(step * cycles, (step + 1) * cycles)
            turn = part * count + step
            cosine, sine = turn_ref[0, turn : turn + 1, :], turn_ref[1, turn : turn + 1, :]
            rows_ref[part % 2, 0, rows, :] = (first * cosine - second * sine).astype(jnp.bfloat16)
            rows_ref[part % 2, 1, rows, :] = (first * sine + second * cosine).astype(jnp.bfloat16)
        result = lax.dot_general(
            rows_ref[part % 2, 0], table_ref[0], dims, preferred_element_type=jnp.float32
        ) + lax.dot_general(
            rows_ref[part % 2, 1], table_ref[1], dims, preferred_element_type=jnp.float32
        )
        for step in range(count):
            part_ref[part, :, step * INNER : (step + 1) * INNER] = result[
                step * cycles : (step + 1) * cycles
            ]
        copy = pltpu.make_async_copy(
            part_ref.at[part], out_ref.at[:, part * span : (part + 1) * span], sems.at[part]
        )
        copy.start()
        copies.append(copy)
    for copy in copies:
        copy.wait()


def inverse(moved, coarse, fine, turn, cycles, longitudes):
    orders = coarse.shape[2]
    count = 6
    parts = longitudes // INNER // count
    return pl.pallas_call(
        inverse_kernel,
        in_specs=[NEARBY] * 4,
        out_specs=pl.BlockSpec(memory_space=pltpu.HBM),
        out_shape=jax.ShapeDtypeStruct((cycles, longitudes), jnp.float32),
        scratch_shapes=[
            pltpu.VMEM((2, 2, count * cycles, orders), jnp.bfloat16),
            pltpu.VMEM((2, INNER, orders), jnp.bfloat16),
            pltpu.VMEM(moved.shape, jnp.float32),
            pltpu.VMEM((2, orders, LANES), jnp.float32),
            pltpu.VMEM((parts, cycles, count * INNER), jnp.float32),
            pltpu.SemaphoreType.DMA((parts,)),
        ],
        cost_estimate=pl.CostEstimate(
            flops=4 * cycles * longitudes * orders, bytes_accessed=1 << 20, transcendentals=0
        ),
        compiler_params=pltpu.CompilerParams(vmem_limit_bytes=ROOM),
        name="inverse_dft",
    )(moved, coarse, fine, turn)


def local(elevation, legendre, cycle_weight, love_factor, assignment):
    _, cycle_dev, longitudes = elevation.shape
    orders_dev, degrees = legendre.shape[1:]
    groups = lax.axis_size("cons")
    near = lax.axis_size(NEAR)
    far = lax.axis_size(FAR)
    orders = orders_dev * groups
    share = orders_dev // near
    spot = lax.axis_index(NEAR)
    coarse = jnp.asarray(angle_tables(FINE, FINE, longitudes, orders))
    fine = jnp.asarray(angle_tables(FINE, 1, longitudes, orders))
    turn = jnp.asarray(angle_tables(longitudes // INNER, INNER, longitudes, orders))

    by_order = legendre.transpose(1, 0, 2).reshape(near, share, cycle_dev, degrees)

    def chunk(other):
        return lax.dynamic_index_in_dim(by_order, spot ^ other, 0, keepdims=False)

    values = [chunk(0)] + [None] * (near - 1)
    for other in (*EARLY, *LATE):
        values[other] = lax.ppermute(
            chunk(other), NEAR, [(index, index ^ other) for index in range(near)]
        )

    deep = 2 * share // (LANES // cycle_dev)
    peers = groups * near
    lines = peers * deep

    def exchanged(packed):
        tiles = packed.reshape(peers, deep, LANES)
        tiles = lax.all_to_all(tiles, TEAM, 0, 0, tiled=True)
        return tiles.reshape(lines, LANES)

    packed = forward(elevation[0], cycle_weight[:, None], coarse, fine, turn, lines)
    moved = exchanged(packed)
    spot_row = spot[None].astype(jnp.int32)
    partial = analyse(spot_row, assignment, moved, values)
    rows = partial.shape[0] // far
    arrived = lax.all_to_all(partial.reshape(far, rows, degrees), FAR, 0, 0, tiled=True)
    analysis = jnp.sum(arrived.astype(jnp.float32), axis=0)
    scaled = (analysis * love_factor[None, :]).astype(jnp.bfloat16)
    copies = jnp.broadcast_to(scaled[None], (far, rows, degrees))
    coefficients = lax.all_to_all(copies, FAR, 0, 0, tiled=True).reshape(-1, degrees)
    first = ((lax.axis_index("cons") * near + spot) * share)[None].astype(jnp.int32)
    synthesis = synthesise(spot_row, first, coefficients, values, lines)
    returned = exchanged(synthesis)
    return inverse(returned, coarse, fine, turn, cycle_dev, longitudes)[None]


def solution(mesh):
    torus = Mesh(
        mesh.devices.reshape(mesh.shape["cons"], 2, 4, 2, 2), ("cons", *BLK)
    )
    placed = (P("cons", BLK, None), P(BLK, "cons", None), P(BLK), P(), P())
    return jax.shard_map(
        local, mesh=torus, in_specs=placed, out_specs=P("cons", BLK, None), check_vma=False
    )
```

profile of v0, /device:TPU:1, one launch (start us, length us, event | category | flops | bytes accessed | tf_op | source)
XLA Modules:
  0.0 120.8 jit_solution(16162542910541367052)
XLA Ops:
  0.0 4.4 %copy.19 = bf16[40,48,768]{2,0,1:T(8,128)(2,1)} copy(bf16[40,48,768]{2,1,0:T(8,128)(2,1)} %param.9) | data formatting | bytes 5898240 | tf_op args[1]
  4.4 0.0 copy-start.9
  4.4 0.0 copy-start.1
  4.4 3.1 %dynamic-slice_bitcast_fusion = (bf16[6,40,768]{2,1,0:T(8,128)(2,1)}, bf16[6,40,768]{2,1,0:T(8,128)(2,1)}, bf16[6,40,768]{2,1,0:T(8,128)(2,1)}, bf16[6,40,768]{2...) fusion(bf16[8,6,40,768]{3,2,1,0:T(8,128)(2,1)} %bitcast.37, ...), kind=kLoop, calls=%fused_computation.1 | loop fusion | bytes 5898272 | tf_op jit(solution)/shard_map/jit(dynamic_index_in_dim)/squeeze | solution.py:353
  7.4 0.0 copy-start
  7.4 8.9 %collective-permute-start = (bf16[6,40,768]{2,1,0:T(8,128)(2,1)S(1)}, bf16[6,40,768]{2,1,0:T(8,128)(2,1)S(1)}, u32[]{:S(2)}, u32[]{:S(2)}) collective-permute-start(bf16[6,40,768]{2,1,0:T(8,128)(2,1)S(1)} %get-tuple-element.11), channel_id=1, source_target_pairs={{0,1},{1,0},{2,3},{3,2},{16,17},{17,16},{18,19},{19,18},{4,5},{5,4... | collective-permute-start | bytes 1105928 | tf_op jit(solution)/shard_map/ppermute | solution.py:357
  16.3 1.9 %collective-permute-start.1 = (bf16[6,40,768]{2,1,0:T(8,128)(2,1)S(1)}, bf16[6,40,768]{2,1,0:T(8,128)(2,1)S(1)}, u32[]{:S(2)}, u32[]{:S(2)}) collective-permute-start(bf16[6,40,768]{2,1,0:T(8,128)(2,1)S(1)} %get-tuple-element.10), channel_id=1, source_target_pairs={{0,2},{1,3},{2,0},{3,1},{16,18},{17,19},{18,16},{19,17},{4,6},{5,7... | collective-permute-start | bytes 1105928 | tf_op jit(solution)/shard_map/ppermute | solution.py:357
  18.2 3.5 %collective-permute-start.2 = (bf16[6,40,768]{2,1,0:T(8,128)(2,1)}, bf16[6,40,768]{2,1,0:T(8,128)(2,1)S(1)}, u32[]{:S(2)}, u32[]{:S(2)}) collective-permute-start(bf16[6,40,768]{2,1,0:T(8,128)(2,1)} %get-tuple-element.9), channel_id=1, source_target_pairs={{0,3},{1,2},{2,1},{3,0},{16,19},{17,18},{18,17},{19,16},{4,7},{5,6... | collective-permute-start | bytes 1105928 | tf_op jit(solution)/shard_map/ppermute | solution.py:357
  21.8 1.9 %collective-permute-start.3 = (bf16[6,40,768]{2,1,0:T(8,128)(2,1)}, bf16[6,40,768]{2,1,0:T(8,128)(2,1)S(1)}, u32[]{:S(2)}, u32[]{:S(2)}) collective-permute-start(bf16[6,40,768]{2,1,0:T(8,128)(2,1)} %get-tuple-element.8), channel_id=1, source_target_pairs={{0,16},{1,17},{2,18},{3,19},{16,0},{17,1},{18,2},{19,3},{4,20},{5,... | collective-permute-start | bytes 1105928 | tf_op jit(solution)/shard_map/ppermute | solution.py:357
  23.7 5.2 %collective-permute-start.4 = (bf16[6,40,768]{2,1,0:T(8,128)(2,1)}, bf16[6,40,768]{2,1,0:T(8,128)(2,1)S(1)}, u32[]{:S(2)}, u32[]{:S(2)}) collective-permute-start(bf16[6,40,768]{2,1,0:T(8,128)(2,1)} %get-tuple-element.7), channel_id=1, source_target_pairs={{0,17},{1,16},{2,19},{3,18},{16,1},{17,0},{18,3},{19,2},{4,21},{5,... | collective-permute-start | bytes 1105928 | tf_op jit(solution)/shard_map/ppermute | solution.py:357
  29.0 0.0 collective-permute-done.refs_3_.refs_2_
  29.0 1.9 %collective-permute-start.5 = (bf16[6,40,768]{2,1,0:T(8,128)(2,1)}, bf16[6,40,768]{2,1,0:T(8,128)(2,1)S(1)}, u32[]{:S(2)}, u32[]{:S(2)}) collective-permute-start(bf16[6,40,768]{2,1,0:T(8,128)(2,1)} %get-tuple-element.6), channel_id=1, source_target_pairs={{0,18},{1,19},{2,16},{3,17},{16,2},{17,3},{18,0},{19,1},{4,22},{5,... | collective-permute-start | bytes 1105928 | tf_op jit(solution)/shard_map/ppermute | solution.py:357
  30.9 0.0 collective-permute-done.1.refs_4_.refs_3_
  30.9 5.9 %collective-permute-start.6 = (bf16[6,40,768]{2,1,0:T(8,128)(2,1)}, bf16[6,40,768]{2,1,0:T(8,128)(2,1)S(1)}, u32[]{:S(2)}, u32[]{:S(2)}) collective-permute-start(bf16[6,40,768]{2,1,0:T(8,128)(2,1)} %get-tuple-element.5), channel_id=1, source_target_pairs={{0,19},{1,18},{2,17},{3,16},{16,3},{17,2},{18,1},{19,0},{4,23},{5,... | collective-permute-start | bytes 1105928 | tf_op jit(solution)/shard_map/ppermute | solution.py:357
  36.9 0.0 copy-done.9
  36.9 0.1 copy.18.weight_ref
  37.0 0.0 copy-done.1
  37.0 0.0 copy-start.2
  37.0 0.9 copy-done.2
  37.9 0.0 copy-start.4
  37.9 0.9 copy-done.4
  38.8 0.0 copy-start.6
  38.8 0.9 copy-done.6
  39.7 1.5 %forward_dft.1 = bf16[512,128]{1,0:T(8,128)(2,1)S(1)} custom-call(bf16[40,6144]{1,0:T(8,128)(2,1)S(1)} %bitcast.36, f32[40,1]{1,0:T(8,128)S(1)} %copy.18.weight_ref, f32[2,16,768]{2,1,0:T(8,128)S(1)} %copy-done.4, f32[2,16,768]{2,1,0:T(8,128)S(1)} %copy-done.6, f32[2,24,768]{2,1,0:T(8,128)S(1)} %copy-done.2), custom_call_target="tpu_custom_call" | custom-call | flops 754974720 | bytes 1048576 | tf_op jit(solution)/shard_map/forward_dft/pallas_call | solution.py:109
  41.2 0.0 copy-start.8
  41.2 19.9 %all_to_all.20 = bf16[128,4,128]{2,1,0:T(4,128)(2,1)S(1)} all-to-all(bf16[128,4,128]{2,1,0:T(4,128)(2,1)S(1)} %bitcast.35), channel_id=1, replica_groups=mesh['cons'=16,'blk_0'=2,'blk_1'=4,'blk_2'=2,'blk_3'=2] {'cons','blk_0',..., dimensions={0} | all-to-all | bytes 262144 | tf_op jit(solution)/shard_map/all_to_all | solution.py:367
  61.1 0.0 collective-permute-done.2.refs_5_.refs_4_
  61.1 0.0 collective-permute-done.3.refs_6_.refs_5_
  61.1 0.0 collective-permute-done.4.refs_7_.refs_6_
  61.1 0.0 collective-permute-done.5.refs_8_.refs_7_
  61.1 0.0 collective-permute-done.6.refs_9_.refs_8_
  61.1 0.0 copy-done
  61.1 1.5 %analysis.1 = bf16[192,768]{1,0:T(8,128)(2,1)S(1)} custom-call(s32[1]{0:T(128)} %bitcast.spot_ref, s32[16]{0:T(128)S(1)} %copy-done, bf16[512,128]{1,0:T(8,128)(2,1)S(1)} %bitcast.32, bf16[6,40,768]{2,1,0:T(8,128)(2,1)S(1)} %get-tuple-element.12.refs_2_.refs_1_, bf16[6,40,768]{2,1,0:T(8,128)(2,1)S(1)} %collective-permute-done.refs_3_.refs_2_, ...), custom_call_target="tpu_custom_call" | custom-call | flops 94371840 | bytes 4194304 | tf_op jit(solution)/shard_map/analysis/pallas_call | solution.py:172
  62.6 0.0 copy-start.3
  62.6 0.0 copy-start.5
  62.6 17.4 %all_to_all.21 = bf16[4,48,768]{2,1,0:T(8,128)(2,1)S(1)} all-to-all(bf16[4,48,768]{2,1,0:T(8,128)(2,1)S(1)} %bitcast.31), channel_id=1, replica_groups=mesh['cons'=16,'blk_0'=2,'blk_1'=4,'blk_2'=2,'blk_3'=2] {'blk_1'}, dimensions={0} | all-to-all | bytes 589824 | tf_op jit(solution)/shard_map/all_to_all | solution.py:375
  80.1 0.0 copy-done.8
  80.1 0.7 broadcast_in_dim.22
  80.9 3.9 %all-to-all-start.2 = ((bf16[4,48,768]{2,1,0:T(8,128)(2,1)}), bf16[4,48,768]{2,1,0:T(8,128)(2,1)S(1)}, u32[]{:S(2)}, u32[]{:S(2)}) async-start(bf16[4,48,768]{2,1,0:T(8,128)(2,1)} %broadcast_in_dim.22), calls=%async_computation.2 | async-start | bytes 589824 | tf_op jit(solution)/shard_map/all_to_all | solution.py:379
  84.8 9.0 %all-to-all-done.2 = bf16[4,48,768]{2,1,0:T(8,128)(2,1)S(1)} async-done(((bf16[4,48,768]{2,1,0:T(8,128)(2,1)}), bf16[4,48,768]{2,1,0:T(8,128)(2,1)S(1)}, u32[]{:S(2)}, u32[]{:S(2)}) %all-to-all-start.2) | async-done | bytes 294944 | tf_op jit(solution)/shard_map/all_to_all | solution.py:379
  93.8 0.0 copy-start.7
  93.8 1.3 %synthesis.1 = bf16[512,128]{1,0:T(8,128)(2,1)S(1)} custom-call(s32[1]{0:T(128)} %bitcast.spot_ref, s32[1]{0:T(128)} %bitcast.1.first_ref, bf16[192,768]{1,0:T(8,128)(2,1)S(1)} %bitcast.30, bf16[6,40,768]{2,1,0:T(8,128)(2,1)S(1)} %get-tuple-element.12.refs_2_.refs_1_, bf16[6,40,768]{2,1,0:T(8,128)(2,1)S(1)} %collective-permute-done.refs_3_.refs_2_, ...), custom_call_target="tpu_custom_call" | custom-call | flops 94371840 | bytes 4194304 | tf_op jit(solution)/shard_map/synthesis/pallas_call | solution.py:236
  95.1 23.5 %all_to_all.22 = bf16[128,4,128]{2,1,0:T(4,128)(2,1)S(1)} all-to-all(bf16[128,4,128]{2,1,0:T(4,128)(2,1)S(1)} %bitcast.33), channel_id=1, replica_groups=mesh['cons'=16,'blk_0'=2,'blk_1'=4,'blk_2'=2,'blk_3'=2] {'cons','blk_0',..., dimensions={0} | all-to-all | bytes 262144 | tf_op jit(solution)/shard_map/all_to_all | solution.py:367
  118.5 0.0 copy-done.3
  118.5 0.0 copy-done.5
  118.5 0.0 copy-done.7
  118.6 2.2 %inverse_dft.1 = f32[40,6144]{1,0:T(8,128)} custom-call(bf16[512,128]{1,0:T(8,128)(2,1)S(1)} %bitcast.34, f32[2,16,768]{2,1,0:T(8,128)S(1)} %copy-done.5, f32[2,16,768]{2,1,0:T(8,128)S(1)} %copy-done.7, f32[2,24,768]{2,1,0:T(8,128)S(1)} %copy-done.3), custom_call_target="tpu_custom_call" | custom-call | flops 754974720 | bytes 1048576 | tf_op jit(solution)/shard_map/inverse_dft/pallas_call | solution.py:316
  (2 shorter events, 0.1 us)
Async XLA Ops:
  4.4 32.5 %copy-start.9 = (f32[40]{0:T(128)S(1)}, f32[40]{0:T(128)}, u32[]{:S(2)}) copy-start(f32[40]{0:T(128)} %param.10) | copy-start | bytes 484
  4.4 32.6 %copy-start.1 = (bf16[1,40,6144]{2,1,0:T(8,128)(2,1)S(1)}, bf16[1,40,6144]{2,1,0:T(8,128)(2,1)}, u32[]{:S(2)}) copy-start(bf16[1,40,6144]{2,1,0:T(8,128)(2,1)} %param.8) | copy-start | bytes 1474564
  7.4 53.7 %copy-start = (s32[16]{0:T(128)S(1)}, s32[16]{0:T(128)}, u32[]{:S(2)}) copy-start(s32[16]{0:T(128)} %refs_0_.1) | copy-start | bytes 196
  7.4 21.5 %collective-permute-start = (bf16[6,40,768]{2,1,0:T(8,128)(2,1)S(1)}, bf16[6,40,768]{2,1,0:T(8,128)(2,1)S(1)}, u32[]{:S(2)}, u32[]{:S(2)}) collective-permute-start(bf16[6,40,768]{2,1,0:T(8,128)(2,1)S(1)} %get-tuple-element.11), channel_id=1, source_target_pairs={{0,1},{1,0},{2,3},{3,2},{16,17},{17,16},{18,19},{19,18},{4,5},{5,4... | collective-permute-start | bytes 1105928 | tf_op jit(solution)/shard_map/ppermute | solution.py:357
  16.3 14.6 %collective-permute-start.1 = (bf16[6,40,768]{2,1,0:T(8,128)(2,1)S(1)}, bf16[6,40,768]{2,1,0:T(8,128)(2,1)S(1)}, u32[]{:S(2)}, u32[]{:S(2)}) collective-permute-start(bf16[6,40,768]{2,1,0:T(8,128)(2,1)S(1)} %get-tuple-element.10), channel_id=1, source_target_pairs={{0,2},{1,3},{2,0},{3,1},{16,18},{17,19},{18,16},{19,17},{4,6},{5,7... | collective-permute-start | bytes 1105928 | tf_op jit(solution)/shard_map/ppermute | solution.py:357
  18.2 42.9 %collective-permute-start.2 = (bf16[6,40,768]{2,1,0:T(8,128)(2,1)}, bf16[6,40,768]{2,1,0:T(8,128)(2,1)S(1)}, u32[]{:S(2)}, u32[]{:S(2)}) collective-permute-start(bf16[6,40,768]{2,1,0:T(8,128)(2,1)} %get-tuple-element.9), channel_id=1, source_target_pairs={{0,3},{1,2},{2,1},{3,0},{16,19},{17,18},{18,17},{19,16},{4,7},{5,6... | collective-permute-start | bytes 1105928 | tf_op jit(solution)/shard_map/ppermute | solution.py:357
  21.8 39.3 %collective-permute-start.3 = (bf16[6,40,768]{2,1,0:T(8,128)(2,1)}, bf16[6,40,768]{2,1,0:T(8,128)(2,1)S(1)}, u32[]{:S(2)}, u32[]{:S(2)}) collective-permute-start(bf16[6,40,768]{2,1,0:T(8,128)(2,1)} %get-tuple-element.8), channel_id=1, source_target_pairs={{0,16},{1,17},{2,18},{3,19},{16,0},{17,1},{18,2},{19,3},{4,20},{5,... | collective-permute-start | bytes 1105928 | tf_op jit(solution)/shard_map/ppermute | solution.py:357
  23.7 37.4 %collective-permute-start.4 = (bf16[6,40,768]{2,1,0:T(8,128)(2,1)}, bf16[6,40,768]{2,1,0:T(8,128)(2,1)S(1)}, u32[]{:S(2)}, u32[]{:S(2)}) collective-permute-start(bf16[6,40,768]{2,1,0:T(8,128)(2,1)} %get-tuple-element.7), channel_id=1, source_target_pairs={{0,17},{1,16},{2,19},{3,18},{16,1},{17,0},{18,3},{19,2},{4,21},{5,... | collective-permute-start | bytes 1105928 | tf_op jit(solution)/shard_map/ppermute | solution.py:357
  29.0 32.1 %collective-permute-start.5 = (bf16[6,40,768]{2,1,0:T(8,128)(2,1)}, bf16[6,40,768]{2,1,0:T(8,128)(2,1)S(1)}, u32[]{:S(2)}, u32[]{:S(2)}) collective-permute-start(bf16[6,40,768]{2,1,0:T(8,128)(2,1)} %get-tuple-element.6), channel_id=1, source_target_pairs={{0,18},{1,19},{2,16},{3,17},{16,2},{17,3},{18,0},{19,1},{4,22},{5,... | collective-permute-start | bytes 1105928 | tf_op jit(solution)/shard_map/ppermute | solution.py:357
  30.9 30.2 %collective-permute-start.6 = (bf16[6,40,768]{2,1,0:T(8,128)(2,1)}, bf16[6,40,768]{2,1,0:T(8,128)(2,1)S(1)}, u32[]{:S(2)}, u32[]{:S(2)}) collective-permute-start(bf16[6,40,768]{2,1,0:T(8,128)(2,1)} %get-tuple-element.5), channel_id=1, source_target_pairs={{0,19},{1,18},{2,17},{3,16},{16,3},{17,2},{18,1},{19,0},{4,23},{5,... | collective-permute-start | bytes 1105928 | tf_op jit(solution)/shard_map/ppermute | solution.py:357
  37.0 0.9 copy-start.2
  37.9 0.9 copy-start.4
  38.8 0.9 copy-start.6
  41.2 38.9 %copy-start.8 = (f32[768]{0:T(1024)S(1)}, f32[768]{0:T(1024)}, u32[]{:S(2)}) copy-start(f32[768]{0:T(1024)} %param.11) | copy-start | bytes 9220
  62.6 55.9 %copy-start.3 = (f32[2,24,768]{2,1,0:T(8,128)S(1)}, f32[2,24,768]{2,1,0:T(8,128)}, u32[]{:S(2)}) copy-start(f32[2,24,768]{2,1,0:T(8,128)} %constant.60.clone.turn_ref) | copy-start | bytes 442372
  62.6 55.9 %copy-start.5 = (f32[2,16,768]{2,1,0:T(8,128)S(1)}, f32[2,16,768]{2,1,0:T(8,128)}, u32[]{:S(2)}) copy-start(f32[2,16,768]{2,1,0:T(8,128)} %constant.58.clone.coarse_ref) | copy-start | bytes 294916
  80.9 12.9 %all-to-all-start.2 = ((bf16[4,48,768]{2,1,0:T(8,128)(2,1)}), bf16[4,48,768]{2,1,0:T(8,128)(2,1)S(1)}, u32[]{:S(2)}, u32[]{:S(2)}) async-start(bf16[4,48,768]{2,1,0:T(8,128)(2,1)} %broadcast_in_dim.22), calls=%async_computation.2 | async-start | bytes 589824 | tf_op jit(solution)/shard_map/all_to_all | solution.py:379
  93.8 24.8 %copy-start.7 = (f32[2,16,768]{2,1,0:T(8,128)S(1)}, f32[2,16,768]{2,1,0:T(8,128)}, u32[]{:S(2)}) copy-start(f32[2,16,768]{2,1,0:T(8,128)} %constant.59.clone.fine_ref) | copy-start | bytes 294916
where the time goes:
time: 121 us
  blocking collectives  60.8 us (50%)
  starting transfers between devices  33.3 us (28%)
  local copies, waits for them, and re-layouts  11 us (9%)
  waiting for transfers between devices  8.99 us (7%)
  Pallas kernels  6.49 us (5%)
    all_to_all x2, blocking collectives, exchanged(): tiles = lax.all_to_all(tiles, TEAM, 0, 0, tiled=True)  43.4 us
    ppermute x7, starting transfers between devices, local(): lax.ppermute(chunk(other), NEAR, [(index, index ^ other) for index in ran...  29.4 us
    all_to_all x1, blocking collectives, local(): lax.all_to_all(partial.reshape(far, rows, degrees), FAR, 0, 0, tiled=True)  17.4 us
    all_to_all x1, waiting for transfers between devices, local(): lax.all_to_all(copies, FAR, 0, 0, tiled=True).reshape(-1, degrees)  8.97 us
    unnamed x21, local copies, waits for them, and re-layouts  7.1 us
    all_to_all x1, starting transfers between devices, local(): lax.all_to_all(copies, FAR, 0, 0, tiled=True).reshape(-1, degrees)  3.91 us
    squeeze x1, local copies, waits for them, and re-layouts, chunk(): return lax.dynamic_index_in_dim(by_order, spot ^ other, 0, keepdims=False)  3.07 us
  transfers between devices with their start and end apart: 8, of which 1 were waited for; matrix products, arithmetic and copies ran while one was open for 0% of the time, Pallas kernels for 1%

commit v1 on v0

--- a/solution.py
+++ b/solution.py
@@ -7,17 +7,17 @@
 from jax.sharding import Mesh
 from jax.sharding import PartitionSpec as P
 
-BLK = ("blk_0", "blk_1", "blk_2", "blk_3")
-NEAR = ("blk_0", "blk_2", "blk_3")
+BLK = ("blk_0", "blk_1", "blk_2")
+NEAR = ("blk_0", "blk_2")
 FAR = "blk_1"
 TEAM = ("cons", *NEAR)
 FINE = 16
 INNER = FINE * FINE
 LANES = 128
-NEAR_SIZE = 8
-SHARE = 6
-EARLY = (6, 7)
-LATE = (4, 2, 5, 3, 1)
+TILE = 8
+NEAR_SIZE = 4
+SHARE = 12
+SWAPS = (2, 3, 1)
 ROOM = 24 << 20
 SCALARS = pl.BlockSpec(memory_space=pltpu.SMEM)
 NEARBY = pl.BlockSpec(memory_space=pltpu.VMEM)
@@ -123,6 +123,36 @@
         compiler_params=pltpu.CompilerParams(vmem_limit_bytes=ROOM),
         name="forward_dft",
     )(elevation, weight, coarse, fine, turn)
+
+
+def split_kernel(spot_ref, legendre_ref, same_ref, other_ref, stage_ref):
+    flip_half, core = spot_ref[0], spot_ref[1]
+    share = same_ref.shape[0]
+    orders = stage_ref.shape[0]
+    for first in range(0, orders, TILE):
+        start = pl.multiple_of(flip_half * orders + first, TILE)
+        stage_ref[first : first + TILE] = jnp.swapaxes(
+            legendre_ref[:, pl.ds(start, TILE), :], 0, 1
+        )
+    same_ref[...] = stage_ref[pl.ds(core * share, share)]
+    other_ref[...] = stage_ref[pl.ds((1 - core) * share, share)]
+
+
+def split(spot, legendre):
+    cycles, _, degrees = legendre.shape
+    piece = jax.ShapeDtypeStruct((SHARE, cycles, degrees), legendre.dtype)
+    return pl.pallas_call(
+        split_kernel,
+        in_specs=[SCALARS, NEARBY],
+        out_specs=[NEARBY] * 2,
+        out_shape=[piece] * 2,
+        scratch_shapes=[pltpu.VMEM((2 * SHARE, cycles, degrees), legendre.dtype)],
+        cost_estimate=pl.CostEstimate(
+            flops=1 << 20, bytes_accessed=4 * cycles * SHARE * degrees * 2, transcendentals=0
+        ),
+        compiler_params=pltpu.CompilerParams(vmem_limit_bytes=ROOM),
+        name="split",
+    )(spot, legendre)
 
 
 def analysis_kernel(spot_ref, *refs):
@@ -347,15 +377,14 @@
     fine = jnp.asarray(angle_tables(FINE, 1, longitudes, orders))
     turn = jnp.asarray(angle_tables(longitudes // INNER, INNER, longitudes, orders))
 
-    by_order = legendre.transpose(1, 0, 2).reshape(near, share, cycle_dev, degrees)
-
-    def chunk(other):
-        return lax.dynamic_index_in_dim(by_order, spot ^ other, 0, keepdims=False)
-
-    values = [chunk(0)] + [None] * (near - 1)
-    for other in (*EARLY, *LATE):
+    far_half, core = lax.axis_index("blk_0"), lax.axis_index("blk_2")
+    values = [None] * near
+    for flip in (1, 0):
+        place = jnp.stack([far_half ^ flip, core]).astype(jnp.int32)
+        values[2 * flip], values[2 * flip + 1] = split(place, legendre)
+    for other in SWAPS:
         values[other] = lax.ppermute(
-            chunk(other), NEAR, [(index, index ^ other) for index in range(near)]
+            values[other], NEAR, [(index, index ^ other) for index in range(near)]
         )
 
     deep = 2 * share // (LANES // cycle_dev)
@@ -385,7 +414,7 @@
 
 def solution(mesh):
     torus = Mesh(
-        mesh.devices.reshape(mesh.shape["cons"], 2, 4, 2, 2), ("cons", *BLK)
+        mesh.devices.reshape(mesh.shape["cons"], 2, 8, 2), ("cons", *BLK)
     )
     placed = (P("cons", BLK, None), P(BLK, "cons", None), P(BLK), P(), P())
     return jax.shard_map(

time: 121 us -> 128 us (1.058)
  waiting for transfers between devices: 8.99 us -> 42 us
  blocking collectives: 60.8 us -> 45.9 us
  starting transfers between devices: 33.3 us -> 24.3 us
  local copies, waits for them, and re-layouts: 11 us -> 3.84 us
  Pallas kernels: 6.49 us -> 11.2 us
    all_to_all x0 -> x1, waiting for transfers between devices: none -> 23.9 us  [exchanged(): tiles = lax.all_to_all(tiles, TEAM, 0, 0, tiled=True)]
    all_to_all x2 -> x1, blocking collectives: 43.4 us -> 22.9 us  [exchanged(): tiles = lax.all_to_all(tiles, TEAM, 0, 0, tiled=True)]
    ppermute x7 -> x3, starting transfers between devices: 29.4 us -> 15.7 us  [local(): lax.ppermute(values[other], NEAR, [(index, index ^ other) for index in ra...]
    all_to_all x1, waiting for transfers between devices: 8.97 us -> 18.1 us  [local(): lax.all_to_all(copies, FAR, 0, 0, tiled=True).reshape(-1, degrees)]
    all_to_all x1, blocking collectives: 17.4 us -> 23 us  [local(): lax.all_to_all(partial.reshape(far, rows, degrees), FAR, 0, 0, tiled=True)]
    all_to_all x0 -> x1, starting transfers between devices: none -> 5.12 us  [exchanged(): tiles = lax.all_to_all(tiles, TEAM, 0, 0, tiled=True)]
    unnamed x21 -> x24, local copies, waits for them, and re-layouts: 7.1 us -> 2.9 us
    pallas_call x0 -> x2, Pallas kernels: none -> 3.97 us  [split(): pl.pallas_call(split_kernel, in_specs=[SCALARS, NEARBY], out_specs=[NEARB...]
  transfers between devices with their start and end apart: 8 -> 5, of which waited for: 1 -> 2; matrix products, arithmetic and copies ran while one was open for 0% -> 0% of each run, Pallas kernels for 1% -> 3%
where the time goes in v1:
time: 128 us
  blocking collectives  45.9 us (36%)
  waiting for transfers between devices  42 us (33%)
  starting transfers between devices  24.3 us (19%)
  Pallas kernels  11.2 us (9%)
  local copies, waits for them, and re-layouts  3.84 us (3%)
    all_to_all x1, waiting for transfers between devices, exchanged(): tiles = lax.all_to_all(tiles, TEAM, 0, 0, tiled=True)  23.9 us
    all_to_all x1, blocking collectives, local(): lax.all_to_all(partial.reshape(far, rows, degrees), FAR, 0, 0, tiled=True)  23 us
    all_to_all x1, blocking collectives, exchanged(): tiles = lax.all_to_all(tiles, TEAM, 0, 0, tiled=True)  22.9 us
    all_to_all x1, waiting for transfers between devices, local(): lax.all_to_all(copies, FAR, 0, 0, tiled=True).reshape(-1, degrees)  18.1 us
    ppermute x3, starting transfers between devices, local(): lax.ppermute(values[other], NEAR, [(index, index ^ other) for index in ra...  15.7 us
    all_to_all x1, starting transfers between devices, exchanged(): tiles = lax.all_to_all(tiles, TEAM, 0, 0, tiled=True)  5.12 us
    pallas_call x2, Pallas kernels, split(): pl.pallas_call(split_kernel, in_specs=[SCALARS, NEARBY], out_specs=[NEARB...  3.97 us
    all_to_all x1, starting transfers between devices, local(): lax.all_to_all(copies, FAR, 0, 0, tiled=True).reshape(-1, degrees)  3.54 us
  transfers between devices with their start and end apart: 5, of which 2 were waited for; matrix products, arithmetic and copies ran while one was open for 0% of the time, Pallas kernels for 3%

profile of v1, /device:TPU:1, one launch (start us, length us, event | category | flops | bytes accessed | tf_op | source)
XLA Modules:
  0.0 127.6 jit_solution(18112009752782565216)
XLA Ops:
  0.0 0.1 pad_add_fusion
  0.1 0.0 copy-start
  0.1 1.8 %copy-done = bf16[40,48,768]{2,1,0:T(8,128)(2,1)S(1)} copy-done((bf16[40,48,768]{2,1,0:T(8,128)(2,1)S(1)}, bf16[40,48,768]{2,1,0:T(8,128)(2,1)}, u32[]{:S(2)}) %copy-start) | copy-done | bytes 2949144
  1.9 0.0 copy-start.1
  1.9 0.0 copy-start.11
  1.9 0.0 copy-start.4
  1.9 0.0 copy-start.6
  1.9 0.0 copy-start.8
  1.9 1.9 %split.2 = (bf16[12,40,768]{2,1,0:T(8,128)(2,1)S(1)}, bf16[12,40,768]{2,1,0:T(8,128)(2,1)}) custom-call(s32[2]{0:T(128)S(1)} %get-tuple-element.13.spot_ref, bf16[40,48,768]{2,1,0:T(8,128)(2,1)S(1)} %copy-done), custom_call_target="tpu_custom_call" | custom-call | flops 1048576 | bytes 2949120 | tf_op jit(solution)/shard_map/split/pallas_call | solution.py:144
  3.8 8.7 %collective-permute-start = (bf16[12,40,768]{2,1,0:T(8,128)(2,1)}, bf16[12,40,768]{2,1,0:T(8,128)(2,1)S(1)}, u32[]{:S(2)}, u32[]{:S(2)}) collective-permute-start(bf16[12,40,768]{2,1,0:T(8,128)(2,1)} %get-tuple-element.10), channel_id=1, source_target_pairs={{0,1},{1,0},{16,17},{17,16},{2,3},{3,2},{18,19},{19,18},{4,5},{5,4... | collective-permute-start | bytes 2211848 | tf_op jit(solution)/shard_map/ppermute | solution.py:386
  12.5 0.0 copy-done.1
  12.5 0.0 copy-start.2
  12.6 2.1 %split.3 = (bf16[12,40,768]{2,1,0:T(8,128)(2,1)}, bf16[12,40,768]{2,1,0:T(8,128)(2,1)}) custom-call(s32[2]{0:T(128)S(1)} %get-tuple-element.14.spot_ref, bf16[40,48,768]{2,1,0:T(8,128)(2,1)S(1)} %copy-done.1), custom_call_target="tpu_custom_call" | custom-call | flops 1048576 | bytes 2949120 | tf_op jit(solution)/shard_map/split/pallas_call | solution.py:144
  14.7 1.9 %collective-permute-start.1 = (bf16[12,40,768]{2,1,0:T(8,128)(2,1)}, bf16[12,40,768]{2,1,0:T(8,128)(2,1)S(1)}, u32[]{:S(2)}, u32[]{:S(2)}) collective-permute-start(bf16[12,40,768]{2,1,0:T(8,128)(2,1)} %get-tuple-element.11), channel_id=1, source_target_pairs={{0,16},{1,17},{16,0},{17,1},{2,18},{3,19},{18,2},{19,3},{4,20},{5,... | collective-permute-start | bytes 2211848 | tf_op jit(solution)/shard_map/ppermute | solution.py:386
  16.6 5.0 %collective-permute-start.2 = (bf16[12,40,768]{2,1,0:T(8,128)(2,1)}, bf16[12,40,768]{2,1,0:T(8,128)(2,1)S(1)}, u32[]{:S(2)}, u32[]{:S(2)}) collective-permute-start(bf16[12,40,768]{2,1,0:T(8,128)(2,1)} %get-tuple-element.12), channel_id=1, source_target_pairs={{0,17},{1,16},{16,1},{17,0},{2,19},{3,18},{18,3},{19,2},{4,21},{5,... | collective-permute-start | bytes 2211848 | tf_op jit(solution)/shard_map/ppermute | solution.py:386
  21.6 0.0 copy-done.11
  21.6 0.1 copy.9.weight_ref
  21.7 0.0 copy-done.4
  21.7 0.0 copy-done.6
  21.7 0.0 copy-done.8
  21.8 0.0 copy-start.3
  21.8 1.0 copy-done.3
  22.8 2.2 %forward_dft.1 = bf16[512,128]{1,0:T(8,128)(2,1)} custom-call(bf16[40,6144]{1,0:T(8,128)(2,1)S(1)} %bitcast.19, f32[40,1]{1,0:T(8,128)S(1)} %copy.9.weight_ref, f32[2,16,768]{2,1,0:T(8,128)S(1)} %copy-done.8, f32[2,16,768]{2,1,0:T(8,128)S(1)} %copy-done.6, f32[2,24,768]{2,1,0:T(8,128)S(1)} %copy-done.4), custom_call_target="tpu_custom_call" | custom-call | flops 754974720 | bytes 1048576 | tf_op jit(solution)/shard_map/forward_dft/pallas_call | solution.py:109
  24.9 0.0 copy-start.10
  24.9 5.1 %all-to-all-start = ((bf16[64,8,128]{2,1,0:T(8,128)(2,1)}), bf16[64,8,128]{2,1,0:T(8,128)(2,1)S(1)}, u32[]{:S(2)}, u32[]{:S(2)}) async-start(bf16[64,8,128]{2,1,0:T(8,128)(2,1)} %bitcast.4), calls=%async_computation | async-start | bytes 262144 | tf_op jit(solution)/shard_map/all_to_all | solution.py:396
  30.1 23.9 %all-to-all-done = bf16[64,8,128]{2,1,0:T(8,128)(2,1)S(1)} async-done(((bf16[64,8,128]{2,1,0:T(8,128)(2,1)}), bf16[64,8,128]{2,1,0:T(8,128)(2,1)S(1)}, u32[]{:S(2)}, u32[]{:S(2)}) %all-to-all-start) | async-done | bytes 131104 | tf_op jit(solution)/shard_map/all_to_all | solution.py:396
  53.9 0.0 collective-permute-done.refs_3_.refs_2_
  54.0 0.0 collective-permute-done.1.refs_4_.refs_3_
  54.0 0.0 collective-permute-done.2.refs_5_.refs_4_
  54.0 0.0 copy-done.2
  54.0 1.4 %analysis.1 = bf16[384,768]{1,0:T(8,128)(2,1)S(1)} custom-call(s32[1]{0:T(128)} %bitcast.spot_ref, s32[16]{0:T(128)S(1)} %copy-done.2, bf16[512,128]{1,0:T(8,128)(2,1)S(1)} %bitcast.16, bf16[12,40,768]{2,1,0:T(8,128)(2,1)S(1)} %get-tuple-element.9.refs_2_.refs_1_, bf16[12,40,768]{2,1,0:T(8,128)(2,1)S(1)} %collective-permute-done.refs_3_.refs_2_, ...), custom_call_target="tpu_custom_call" | custom-call | flops 94371840 | bytes 4194304 | tf_op jit(solution)/shard_map/analysis/pallas_call | solution.py:202
  55.4 23.0 %all_to_all.20 = bf16[8,48,768]{2,1,0:T(8,128)(2,1)S(1)} all-to-all(bf16[8,48,768]{2,1,0:T(8,128)(2,1)S(1)} %bitcast.15), channel_id=1, replica_groups=mesh['cons'=16,'blk_0'=2,'blk_1'=8,'blk_2'=2] {'blk_1'}, dimensions={0} | all-to-all | bytes 1179648 | tf_op jit(solution)/shard_map/all_to_all | solution.py:404
  78.4 0.1 convert_reduce_fusion
  78.5 0.0 copy-done.10
  78.5 0.9 broadcast_in_dim.22
  79.4 3.5 %all-to-all-start.2 = ((bf16[8,48,768]{2,1,0:T(8,128)(2,1)}), bf16[8,48,768]{2,1,0:T(8,128)(2,1)S(1)}, u32[]{:S(2)}, u32[]{:S(2)}) async-start(bf16[8,48,768]{2,1,0:T(8,128)(2,1)} %broadcast_in_dim.22), calls=%async_computation.2 | async-start | bytes 1179648 | tf_op jit(solution)/shard_map/all_to_all | solution.py:408
  82.9 18.1 %all-to-all-done.2 = bf16[8,48,768]{2,1,0:T(8,128)(2,1)S(1)} async-done(((bf16[8,48,768]{2,1,0:T(8,128)(2,1)}), bf16[8,48,768]{2,1,0:T(8,128)(2,1)S(1)}, u32[]{:S(2)}, u32[]{:S(2)}) %all-to-all-start.2) | async-done | bytes 589856 | tf_op jit(solution)/shard_map/all_to_all | solution.py:408
  101.1 0.0 copy-start.5
  101.1 0.0 copy-start.7
  101.1 0.0 copy-start.9
  101.1 1.4 %synthesis.1 = bf16[512,128]{1,0:T(8,128)(2,1)S(1)} custom-call(s32[1]{0:T(128)} %bitcast.spot_ref, s32[1]{0:T(128)} %bitcast.1.first_ref, bf16[384,768]{1,0:T(8,128)(2,1)S(1)} %bitcast.14, bf16[12,40,768]{2,1,0:T(8,128)(2,1)S(1)} %get-tuple-element.9.refs_2_.refs_1_, bf16[12,40,768]{2,1,0:T(8,128)(2,1)S(1)} %collective-permute-done.refs_3_.refs_2_, ...), custom_call_target="tpu_custom_call" | custom-call | flops 94371840 | bytes 4194304 | tf_op jit(solution)/shard_map/synthesis/pallas_call | solution.py:266
  102.5 22.9 %all_to_all.21 = bf16[64,8,128]{2,1,0:T(8,128)(2,1)S(1)} all-to-all(bf16[64,8,128]{2,1,0:T(8,128)(2,1)S(1)} %bitcast.17), channel_id=1, replica_groups=mesh['cons'=16,'blk_0'=2,'blk_1'=8,'blk_2'=2] {'cons','blk_0','blk_2'}, dimensions={0} | all-to-all | bytes 262144 | tf_op jit(solution)/shard_map/all_to_all | solution.py:396
  125.3 0.0 copy-done.5
  125.3 0.0 copy-done.7
  125.3 0.0 copy-done.9
  125.3 2.2 %inverse_dft.1 = f32[40,6144]{1,0:T(8,128)} custom-call(bf16[512,128]{1,0:T(8,128)(2,1)S(1)} %bitcast.18, f32[2,16,768]{2,1,0:T(8,128)S(1)} %copy-done.9, f32[2,16,768]{2,1,0:T(8,128)S(1)} %copy-done.7, f32[2,24,768]{2,1,0:T(8,128)S(1)} %copy-done.5), custom_call_target="tpu_custom_call" | custom-call | flops 754974720 | bytes 1048576 | tf_op jit(solution)/shard_map/inverse_dft/pallas_call | solution.py:346
  (1 shorter events, 0.0 us)
Async XLA Ops:
  0.1 1.8 %copy-start = (bf16[40,48,768]{2,1,0:T(8,128)(2,1)S(1)}, bf16[40,48,768]{2,1,0:T(8,128)(2,1)}, u32[]{:S(2)}) copy-start(bf16[40,48,768]{2,1,0:T(8,128)(2,1)} %legendre_ref.3) | copy-start | bytes 8847364
  1.9 10.6 %copy-start.1 = (bf16[40,48,768]{2,1,0:T(8,128)(2,1)S(1)}, bf16[40,48,768]{2,1,0:T(8,128)(2,1)}, u32[]{:S(2)}) copy-start(bf16[40,48,768]{2,1,0:T(8,128)(2,1)} %legendre_ref.3) | copy-start | bytes 8847364
  1.9 19.7 %copy-start.11 = (f32[40]{0:T(128)S(1)}, f32[40]{0:T(128)}, u32[]{:S(2)}) copy-start(f32[40]{0:T(128)} %param.10) | copy-start | bytes 484
  1.9 19.8 %copy-start.4 = (f32[2,24,768]{2,1,0:T(8,128)S(1)}, f32[2,24,768]{2,1,0:T(8,128)}, u32[]{:S(2)}) copy-start(f32[2,24,768]{2,1,0:T(8,128)} %constant.31.clone.turn_ref) | copy-start | bytes 442372
  1.9 19.8 %copy-start.6 = (f32[2,16,768]{2,1,0:T(8,128)S(1)}, f32[2,16,768]{2,1,0:T(8,128)}, u32[]{:S(2)}) copy-start(f32[2,16,768]{2,1,0:T(8,128)} %constant.30.clone.fine_ref) | copy-start | bytes 294916
  1.9 19.8 %copy-start.8 = (f32[2,16,768]{2,1,0:T(8,128)S(1)}, f32[2,16,768]{2,1,0:T(8,128)}, u32[]{:S(2)}) copy-start(f32[2,16,768]{2,1,0:T(8,128)} %constant.29.clone.coarse_ref) | copy-start | bytes 294916
  3.8 50.2 %collective-permute-start = (bf16[12,40,768]{2,1,0:T(8,128)(2,1)}, bf16[12,40,768]{2,1,0:T(8,128)(2,1)S(1)}, u32[]{:S(2)}, u32[]{:S(2)}) collective-permute-start(bf16[12,40,768]{2,1,0:T(8,128)(2,1)} %get-tuple-element.10), channel_id=1, source_target_pairs={{0,1},{1,0},{16,17},{17,16},{2,3},{3,2},{18,19},{19,18},{4,5},{5,4... | collective-permute-start | bytes 2211848 | tf_op jit(solution)/shard_map/ppermute | solution.py:386
  12.5 41.4 %copy-start.2 = (s32[16]{0:T(128)S(1)}, s32[16]{0:T(128)}, u32[]{:S(2)}) copy-start(s32[16]{0:T(128)} %refs_0_.1) | copy-start | bytes 196
  14.7 39.3 %collective-permute-start.1 = (bf16[12,40,768]{2,1,0:T(8,128)(2,1)}, bf16[12,40,768]{2,1,0:T(8,128)(2,1)S(1)}, u32[]{:S(2)}, u32[]{:S(2)}) collective-permute-start(bf16[12,40,768]{2,1,0:T(8,128)(2,1)} %get-tuple-element.11), channel_id=1, source_target_pairs={{0,16},{1,17},{16,0},{17,1},{2,18},{3,19},{18,2},{19,3},{4,20},{5,... | collective-permute-start | bytes 2211848 | tf_op jit(solution)/shard_map/ppermute | solution.py:386
  16.6 37.4 %collective-permute-start.2 = (bf16[12,40,768]{2,1,0:T(8,128)(2,1)}, bf16[12,40,768]{2,1,0:T(8,128)(2,1)S(1)}, u32[]{:S(2)}, u32[]{:S(2)}) collective-permute-start(bf16[12,40,768]{2,1,0:T(8,128)(2,1)} %get-tuple-element.12), channel_id=1, source_target_pairs={{0,17},{1,16},{16,1},{17,0},{2,19},{3,18},{18,3},{19,2},{4,21},{5,... | collective-permute-start | bytes 2211848 | tf_op jit(solution)/shard_map/ppermute | solution.py:386
  21.8 1.0 copy-start.3
  24.9 53.5 %copy-start.10 = (f32[768]{0:T(1024)S(1)}, f32[768]{0:T(1024)}, u32[]{:S(2)}) copy-start(f32[768]{0:T(1024)} %param.11) | copy-start | bytes 9220
  24.9 29.0 %all-to-all-start = ((bf16[64,8,128]{2,1,0:T(8,128)(2,1)}), bf16[64,8,128]{2,1,0:T(8,128)(2,1)S(1)}, u32[]{:S(2)}, u32[]{:S(2)}) async-start(bf16[64,8,128]{2,1,0:T(8,128)(2,1)} %bitcast.4), calls=%async_computation | async-start | bytes 262144 | tf_op jit(solution)/shard_map/all_to_all | solution.py:396
  79.4 21.7 %all-to-all-start.2 = ((bf16[8,48,768]{2,1,0:T(8,128)(2,1)}), bf16[8,48,768]{2,1,0:T(8,128)(2,1)S(1)}, u32[]{:S(2)}, u32[]{:S(2)}) async-start(bf16[8,48,768]{2,1,0:T(8,128)(2,1)} %broadcast_in_dim.22), calls=%async_computation.2 | async-start | bytes 1179648 | tf_op jit(solution)/shard_map/all_to_all | solution.py:408
  101.1 24.3 %copy-start.5 = (f32[2,24,768]{2,1,0:T(8,128)S(1)}, f32[2,24,768]{2,1,0:T(8,128)}, u32[]{:S(2)}) copy-start(f32[2,24,768]{2,1,0:T(8,128)} %constant.31.clone.turn_ref) | copy-start | bytes 442372
  101.1 24.3 %copy-start.7 = (f32[2,16,768]{2,1,0:T(8,128)S(1)}, f32[2,16,768]{2,1,0:T(8,128)}, u32[]{:S(2)}) copy-start(f32[2,16,768]{2,1,0:T(8,128)} %constant.30.clone.fine_ref) | copy-start | bytes 294916
  101.1 24.3 %copy-start.9 = (f32[2,16,768]{2,1,0:T(8,128)S(1)}, f32[2,16,768]{2,1,0:T(8,128)}, u32[]{:S(2)}) copy-start(f32[2,16,768]{2,1,0:T(8,128)} %constant.29.clone.coarse_ref) | copy-start | bytes 294916

commit v2 on v0

--- a/solution.py
+++ b/solution.py
@@ -1,3 +1,6 @@
+import functools
+import math
+
 import jax
 import jax.numpy as jnp
 import numpy as np
@@ -7,17 +10,15 @@
 from jax.sharding import Mesh
 from jax.sharding import PartitionSpec as P
 
-BLK = ("blk_0", "blk_1", "blk_2", "blk_3")
-NEAR = ("blk_0", "blk_2", "blk_3")
-FAR = "blk_1"
-TEAM = ("cons", *NEAR)
+BLK = ("blk_0", "blk_1", "blk_2")
+NEAR = ("blk_2", "blk_0")
+CORE = "blk_2"
+DEEP = "blk_1"
+FAR = ("blk_0", "blk_1")
 FINE = 16
 INNER = FINE * FINE
 LANES = 128
-NEAR_SIZE = 8
-SHARE = 6
-EARLY = (6, 7)
-LATE = (4, 2, 5, 3, 1)
+TILE = 8
 ROOM = 24 << 20
 SCALARS = pl.BlockSpec(memory_space=pltpu.SMEM)
 NEARBY = pl.BlockSpec(memory_space=pltpu.VMEM)
@@ -55,6 +56,7 @@
 
 
 def forward_kernel(
+    peers,
     elevation_ref,
     weight_ref,
     coarse_ref,
@@ -91,23 +93,23 @@
         flip_ref[1, lanes, :cycles] = jnp.transpose(second * weight)
 
     beside = LANES // cycles
-    peers = orders // SHARE
     deep = out_ref.shape[0] // peers
+    share = orders // peers
     for row in range(deep):
         pieces = []
         for column in range(beside):
-            which, order = divmod(deep * column + row, SHARE)
-            pieces.append(flip_ref[which, pl.ds(order, peers, stride=SHARE), :])
+            which, order = divmod(deep * column + row, share)
+            pieces.append(flip_ref[which, pl.ds(order, peers, stride=share), :])
         pack_ref[pl.ds(row, peers, stride=deep), :] = side_by_side(pieces, cycles)
     out_ref[...] = pack_ref[...].astype(jnp.bfloat16)
 
 
-def forward(elevation, weight, coarse, fine, turn, lines):
+def forward(elevation, weight, coarse, fine, turn, lines, peers):
     cycles, longitudes = elevation.shape
     orders = coarse.shape[2]
     turns = longitudes // INNER
     return pl.pallas_call(
-        forward_kernel,
+        functools.partial(forward_kernel, peers),
         in_specs=[NEARBY] * 5,
         out_specs=NEARBY,
         out_shape=jax.ShapeDtypeStruct((lines, LANES), jnp.bfloat16),
@@ -125,8 +127,34 @@
     )(elevation, weight, coarse, fine, turn)
 
 
-def analysis_kernel(spot_ref, *refs):
-    near = NEAR_SIZE
+def split_kernel(place_ref, legendre_ref, half_ref):
+    orders = half_ref.shape[0]
+    for first in range(0, orders, TILE):
+        start = pl.multiple_of(place_ref[0] * orders + first, TILE)
+        half_ref[first : first + TILE] = jnp.swapaxes(
+            legendre_ref[:, pl.ds(start, TILE), :], 0, 1
+        )
+
+
+def part_kernel(place_ref, half_ref, part_ref):
+    share = part_ref.shape[0]
+    part_ref[...] = half_ref[pl.ds(place_ref[0] * share, share)]
+
+
+def halved(kernel, place, values, shape):
+    return pl.pallas_call(
+        kernel,
+        in_specs=[SCALARS, NEARBY],
+        out_specs=NEARBY,
+        out_shape=jax.ShapeDtypeStruct(shape, values.dtype),
+        cost_estimate=pl.CostEstimate(
+            flops=1 << 20, bytes_accessed=4 * math.prod(shape), transcendentals=0
+        ),
+        compiler_params=pltpu.CompilerParams(vmem_limit_bytes=ROOM),
+    )(place[None].astype(jnp.int32), values)
+
+
+def analysis_kernel(near, spot_ref, *refs):
     assignment_ref, moved_ref, *value_refs = refs[: near + 2]
     out_ref, row_ref, left_ref, joined_ref = refs[near + 2 :]
     share, _, two_fields, _ = left_ref.shape
@@ -170,7 +198,7 @@
     share, cycles, degrees = values[0].shape
     fields = assignment.shape[0]
     return pl.pallas_call(
-        analysis_kernel,
+        functools.partial(analysis_kernel, len(values)),
         in_specs=[SCALARS] * 2 + [NEARBY] * (1 + len(values)),
         out_specs=NEARBY,
         scratch_shapes=[
@@ -189,8 +217,7 @@
     )(spot, assignment, moved, *values)
 
 
-def synthesis_kernel(spot_ref, first_ref, *refs):
-    near = NEAR_SIZE
+def synthesis_kernel(near, spot_ref, first_ref, *refs):
     coefficient_ref, *value_refs = refs[: near + 1]
     out_ref, right_ref, row_ref, joined_ref = refs[near + 1 :]
     share, _, two_fields, _ = right_ref.shape
@@ -204,8 +231,9 @@
     for order in range(share):
         factor = jnp.where(first_ref[0] + order == 0, 1.0, 2.0).astype(jnp.float32)
         for other in range(near):
+            skip = 0 if value_refs[other].shape[0] == share else share * (spot_ref[0] % 2)
             joined_ref[order % 2, other * cycles : (other + 1) * cycles, :] = value_refs[other][
-                order
+                skip + order
             ]
         product = factor * lax.dot_general(
             coefficient_ref[2 * fields * order : 2 * fields * (order + 1), :],
@@ -231,10 +259,11 @@
 
 
 def synthesise(spot, first, coefficients, values, lines):
-    share, cycles, degrees = values[0].shape
+    share = min(value.shape[0] for value in values)
+    _, cycles, degrees = values[0].shape
     fields = coefficients.shape[0] // (2 * share)
     return pl.pallas_call(
-        synthesis_kernel,
+        functools.partial(synthesis_kernel, len(values)),
         in_specs=[SCALARS] * 2 + [NEARBY] * (1 + len(values)),
         out_specs=NEARBY,
         scratch_shapes=[
@@ -254,6 +283,7 @@
 
 
 def inverse_kernel(
+    peers,
     moved_ref,
     coarse_ref,
     fine_ref,
@@ -271,13 +301,13 @@
     orders = flip_ref.shape[1]
     inner_table(coarse_ref, fine_ref, table_ref, slice(None))
     row_ref[...] = moved_ref[...].astype(jnp.float32)
-    peers = orders // SHARE
     deep = moved_ref.shape[0] // peers
+    share = orders // peers
     for row in range(deep):
         taken = row_ref[pl.ds(row, peers, stride=deep), :]
         for column in range(LANES // cycles):
-            which, order = divmod(deep * column + row, SHARE)
-            flip_ref[which, pl.ds(order, peers, stride=SHARE), :] = shift(
+            which, order = divmod(deep * column + row, share)
+            flip_ref[which, pl.ds(order, peers, stride=share), :] = shift(
                 taken, -column * cycles
             )
     first = jnp.transpose(flip_ref[0])[:cycles]
@@ -309,12 +339,12 @@
         copy.wait()
 
 
-def inverse(moved, coarse, fine, turn, cycles, longitudes):
+def inverse(moved, coarse, fine, turn, cycles, longitudes, peers):
     orders = coarse.shape[2]
     count = 6
     parts = longitudes // INNER // count
     return pl.pallas_call(
-        inverse_kernel,
+        functools.partial(inverse_kernel, peers),
         in_specs=[NEARBY] * 4,
         out_specs=pl.BlockSpec(memory_space=pltpu.HBM),
         out_shape=jax.ShapeDtypeStruct((cycles, longitudes), jnp.float32),
@@ -338,54 +368,67 @@
     _, cycle_dev, longitudes = elevation.shape
     orders_dev, degrees = legendre.shape[1:]
     groups = lax.axis_size("cons")
-    near = lax.axis_size(NEAR)
-    far = lax.axis_size(FAR)
+    cores, near = lax.axis_size(CORE), lax.axis_size(NEAR)
+    deep, far = lax.axis_size(DEEP), lax.axis_size(FAR)
     orders = orders_dev * groups
-    share = orders_dev // near
-    spot = lax.axis_index(NEAR)
+    spot, core = lax.axis_index(NEAR), lax.axis_index(CORE)
+    side = lax.axis_index("blk_0")
     coarse = jnp.asarray(angle_tables(FINE, FINE, longitudes, orders))
     fine = jnp.asarray(angle_tables(FINE, 1, longitudes, orders))
     turn = jnp.asarray(angle_tables(longitudes // INNER, INNER, longitudes, orders))
 
-    by_order = legendre.transpose(1, 0, 2).reshape(near, share, cycle_dev, degrees)
-
-    def chunk(other):
-        return lax.dynamic_index_in_dim(by_order, spot ^ other, 0, keepdims=False)
-
-    values = [chunk(0)] + [None] * (near - 1)
-    for other in (*EARLY, *LATE):
-        values[other] = lax.ppermute(
-            chunk(other), NEAR, [(index, index ^ other) for index in range(near)]
-        )
-
-    deep = 2 * share // (LANES // cycle_dev)
-    peers = groups * near
-    lines = peers * deep
-
-    def exchanged(packed):
-        tiles = packed.reshape(peers, deep, LANES)
-        tiles = lax.all_to_all(tiles, TEAM, 0, 0, tiled=True)
-        return tiles.reshape(lines, LANES)
-
-    packed = forward(elevation[0], cycle_weight[:, None], coarse, fine, turn, lines)
-    moved = exchanged(packed)
-    spot_row = spot[None].astype(jnp.int32)
-    partial = analyse(spot_row, assignment, moved, values)
+    def swapped(values, other):
+        pairs = [(index, index ^ other) for index in range(near)]
+        return lax.ppermute(values, NEAR[::-1], pairs)
+
+    half, share = orders_dev // cores, orders_dev // near
+
+    def placed(which):
+        shape = (half, cycle_dev, degrees)
+        return halved(split_kernel, which, legendre, shape)
+
+    def part_of(values):
+        shape = (share, cycle_dev, degrees)
+        return halved(part_kernel, 1 - side, values, shape)
+
+    def exchanged(packed, axes):
+        peers = lax.axis_size(axes)
+        tiles = packed.reshape(peers, -1, LANES)
+        tiles = lax.all_to_all(tiles, axes, 0, 0, tiled=True)
+        return tiles.reshape(-1, LANES)
+
+    sent = placed(1 - core)
+    met = swapped(sent, 1)
+    own = placed(core)
+    lines = groups * orders_dev * 2 // (LANES // cycle_dev)
+    packed = forward(elevation[0], cycle_weight[:, None], coarse, fine, turn, lines, groups * cores)
+    moved = exchanged(packed, ("cons", CORE))
+    partial = analyse(core[None].astype(jnp.int32), assignment, moved, [own, met])
     rows = partial.shape[0] // far
     arrived = lax.all_to_all(partial.reshape(far, rows, degrees), FAR, 0, 0, tiled=True)
+    own_side = swapped(part_of(own), 2)
     analysis = jnp.sum(arrived.astype(jnp.float32), axis=0)
     scaled = (analysis * love_factor[None, :]).astype(jnp.bfloat16)
-    copies = jnp.broadcast_to(scaled[None], (far, rows, degrees))
-    coefficients = lax.all_to_all(copies, FAR, 0, 0, tiled=True).reshape(-1, degrees)
+    copies = jnp.broadcast_to(scaled[None], (deep, rows, degrees))
+    coefficients = lax.all_to_all(copies, DEEP, 0, 0, tiled=True)
+    met_side = swapped(part_of(sent), 3)
     first = ((lax.axis_index("cons") * near + spot) * share)[None].astype(jnp.int32)
-    synthesis = synthesise(spot_row, first, coefficients, values, lines)
-    returned = exchanged(synthesis)
-    return inverse(returned, coarse, fine, turn, cycle_dev, longitudes)[None]
+    synthesis = synthesise(
+        spot[None].astype(jnp.int32),
+        first,
+        coefficients.reshape(-1, degrees),
+        [own, own_side, met, met_side],
+        lines,
+    )
+    returned = exchanged(synthesis, ("cons", *NEAR))
+    return inverse(
+        returned, coarse, fine, turn, cycle_dev, longitudes, groups * near
+    )[None]
 
 
 def solution(mesh):
     torus = Mesh(
-        mesh.devices.reshape(mesh.shape["cons"], 2, 4, 2, 2), ("cons", *BLK)
+        mesh.devices.reshape(mesh.shape["cons"], 2, 8, 2), ("cons", *BLK)
     )
     placed = (P("cons", BLK, None), P(BLK, "cons", None), P(BLK), P(), P())
     return jax.shard_map(

time: 121 us -> 138 us (1.14)
  waiting for transfers between devices: 8.99 us -> 35.8 us
  starting transfers between devices: 33.3 us -> 26.1 us
  Pallas kernels: 6.49 us -> 13.6 us
  local copies, waits for them, and re-layouts: 11 us -> 4.65 us
  blocking collectives: 60.8 us -> 56.7 us
    ppermute x7 -> x3, waiting for transfers between devices: 0.02 us -> 28.7 us  [swapped(): return lax.ppermute(values, NEAR[::-1], pairs)]
    all_to_all x2 -> x1, blocking collectives: 43.4 us -> 15.4 us  [exchanged(): tiles = lax.all_to_all(tiles, axes, 0, 0, tiled=True)]
    all_to_all x1, blocking collectives: 17.4 us -> 41.3 us  [local(): lax.all_to_all(partial.reshape(far, rows, degrees), FAR, 0, 0, tiled=True)]
    ppermute x7 -> x3, starting transfers between devices: 29.4 us -> 17.4 us  [swapped(): return lax.ppermute(values, NEAR[::-1], pairs)]
    pallas_call x4 -> x8, Pallas kernels: 6.49 us -> 13.6 us  [the longest x4 5.08 us: halved(): pl.pallas_call(kernel, in_specs=[SCALARS, NEARBY], out_specs=NEARBY, out_...]
    all_to_all x1 -> x2, starting transfers between devices: 3.91 us -> 8.71 us  [the longest x1 5.06 us: local(): coefficients = lax.all_to_all(copies, DEEP, 0, 0, tiled=True)]
    unnamed x21 -> x24, local copies, waits for them, and re-layouts: 7.1 us -> 3.7 us
    squeeze x1 -> x0, local copies, waits for them, and re-layouts: 3.07 us -> none  [chunk(): return lax.dynamic_index_in_dim(by_order, spot ^ other, 0, keepdims=False)]
  transfers between devices with their start and end apart: 8 -> 5, of which waited for: 1 -> 3; matrix products, arithmetic and copies ran while one was open for 0% -> 0% of each run, Pallas kernels for 1% -> 4%
where the time goes in v2:
time: 138 us; the launch traced here: 137 us
  blocking collectives  56.7 us (41%)
  waiting for transfers between devices  35.8 us (26%)
  starting transfers between devices  26.1 us (19%)
  Pallas kernels  13.6 us (10%)
  local copies, waits for them, and re-layouts  4.65 us (3%)
    all_to_all x1, blocking collectives, local(): lax.all_to_all(partial.reshape(far, rows, degrees), FAR, 0, 0, tiled=True)  41.3 us
    ppermute x3, waiting for transfers between devices, swapped(): return lax.ppermute(values, NEAR[::-1], pairs)  28.7 us
    ppermute x3, starting transfers between devices, swapped(): return lax.ppermute(values, NEAR[::-1], pairs)  17.4 us
    all_to_all x1, blocking collectives, exchanged(): tiles = lax.all_to_all(tiles, axes, 0, 0, tiled=True)  15.4 us
    all_to_all x1, waiting for transfers between devices, exchanged(): tiles = lax.all_to_all(tiles, axes, 0, 0, tiled=True)  7.1 us
    pallas_call x4, Pallas kernels, halved(): pl.pallas_call(kernel, in_specs=[SCALARS, NEARBY], out_specs=NEARBY, out_...  5.08 us
    all_to_all x1, starting transfers between devices, local(): coefficients = lax.all_to_all(copies, DEEP, 0, 0, tiled=True)  5.06 us
    unnamed x24, local copies, waits for them, and re-layouts  3.7 us
  transfers between devices with their start and end apart: 5, of which 3 were waited for; matrix products, arithmetic and copies ran while one was open for 0% of the time, Pallas kernels for 4%

profile of v2, /device:TPU:1, one launch (start us, length us, event | category | flops | bytes accessed | tf_op | source)
XLA Modules:
  0.0 137.1 jit_solution(7824231635236702566)
XLA Ops:
  0.0 0.0 copy-start
  0.0 1.8 %copy-done = bf16[40,48,768]{2,1,0:T(8,128)(2,1)S(1)} copy-done((bf16[40,48,768]{2,1,0:T(8,128)(2,1)S(1)}, bf16[40,48,768]{2,1,0:T(8,128)(2,1)}, u32[]{:S(2)}) %copy-start) | copy-done | bytes 2949144
  1.8 0.0 copy-start.11
  1.8 0.0 copy-start.3
  1.8 0.0 copy-start.4
  1.8 0.0 copy-start.6
  1.8 0.0 copy-start.8
  1.9 1.5 %shard_map.83.half_ref = bf16[24,40,768]{2,1,0:T(8,128)(2,1)} custom-call(s32[1]{0:T(128)} %bitcast.7.place_ref, bf16[40,48,768]{2,1,0:T(8,128)(2,1)S(1)} %copy-done), custom_call_target="tpu_custom_call" | custom-call | flops 1048576 | bytes 2949120 | tf_op jit(solution)/shard_map/pallas_call | solution.py:145
  3.4 8.7 %collective-permute-start = (bf16[24,40,768]{2,1,0:T(8,128)(2,1)}, bf16[24,40,768]{2,1,0:T(8,128)(2,1)S(1)}, u32[]{:S(2)}, u32[]{:S(2)}) collective-permute-start(bf16[24,40,768]{2,1,0:T(8,128)(2,1)} %shard_map.83.half_ref), channel_id=1, source_target_pairs={{0,1},{1,0},{16,17},{17,16},{2,3},{3,2},{18,19},{19,18},{4,5},{5,4... | collective-permute-start | bytes 4423688 | tf_op jit(solution)/shard_map/ppermute | solution.py:382
  12.1 0.0 copy-done.11
  12.1 0.1 copy.9.weight_ref
  12.2 0.0 copy-done.3
  12.2 0.0 copy-done.4
  12.2 0.0 copy-done.6
  12.2 0.0 copy-done.8
  12.2 2.2 %forward_dft.1 = bf16[512,128]{1,0:T(8,128)(2,1)} custom-call(bf16[40,6144]{1,0:T(8,128)(2,1)S(1)} %bitcast.19, f32[40,1]{1,0:T(8,128)S(1)} %copy.9.weight_ref, f32[2,16,768]{2,1,0:T(8,128)S(1)} %copy-done.8, f32[2,16,768]{2,1,0:T(8,128)S(1)} %copy-done.6, f32[2,24,768]{2,1,0:T(8,128)S(1)} %copy-done.4), custom_call_target="tpu_custom_call" | custom-call | flops 754974720 | bytes 1048576 | tf_op jit(solution)/shard_map/forward_dft/pallas_call | solution.py:111
  14.4 3.6 %all-to-all-start = ((bf16[32,16,128]{2,1,0:T(8,128)(2,1)}), bf16[32,16,128]{2,1,0:T(8,128)(2,1)S(1)}, u32[]{:S(2)}, u32[]{:S(2)}) async-start(bf16[32,16,128]{2,1,0:T(8,128)(2,1)} %bitcast.5), calls=%async_computation | async-start | bytes 262144 | tf_op jit(solution)/shard_map/all_to_all | solution.py:397
  18.0 0.0 copy-start.1
  18.1 1.8 %copy-done.1 = bf16[40,48,768]{2,1,0:T(8,128)(2,1)S(1)} copy-done((bf16[40,48,768]{2,1,0:T(8,128)(2,1)S(1)}, bf16[40,48,768]{2,1,0:T(8,128)(2,1)}, u32[]{:S(2)}) %copy-start.1) | copy-done | bytes 2949144
  19.9 0.0 copy-start.2
  19.9 0.4 shard_map.82.refs_2_.half_ref.refs_1_
  20.3 7.1 %all-to-all-done = bf16[32,16,128]{2,1,0:T(8,128)(2,1)S(1)} async-done(((bf16[32,16,128]{2,1,0:T(8,128)(2,1)}), bf16[32,16,128]{2,1,0:T(8,128)(2,1)S(1)}, u32[]{:S(2)}, u32[]{:S(2)}) %all-to-all-start) | async-done | bytes 131104 | tf_op jit(solution)/shard_map/all_to_all | solution.py:397
  27.4 0.0 collective-permute-done.refs_3_
  27.4 0.0 copy-done.2
  27.4 1.3 analysis.1
  28.7 0.0 copy-start.10
  28.7 41.3 %all_to_all.20 = bf16[16,48,768]{2,1,0:T(8,128)(2,1)S(1)} all-to-all(bf16[16,48,768]{2,1,0:T(8,128)(2,1)S(1)} %bitcast.14), channel_id=1, replica_groups=mesh['cons'=16,'blk_0'=2,'blk_1'=8,'blk_2'=2] {'blk_0','blk_1'}, dimensions={0} | all-to-all | bytes 2359296 | tf_op jit(solution)/shard_map/all_to_all | solution.py:408
  70.0 0.2 convert_reduce_fusion
  70.1 0.0 copy-done.10
  70.2 0.9 broadcast_in_dim.35
  71.0 5.1 %all-to-all-start.2 = ((bf16[8,48,768]{2,1,0:T(8,128)(2,1)}), bf16[8,48,768]{2,1,0:T(8,128)(2,1)S(1)}, u32[]{:S(2)}, u32[]{:S(2)}) async-start(bf16[8,48,768]{2,1,0:T(8,128)(2,1)} %broadcast_in_dim.35), calls=%async_computation.2 | async-start | bytes 1179648 | tf_op jit(solution)/shard_map/all_to_all | solution.py:413
  76.1 2.3 %shard_map.85 = bf16[12,40,768]{2,1,0:T(8,128)(2,1)} custom-call(s32[1]{0:T(128)} %bitcast.10.place_ref, bf16[24,40,768]{2,1,0:T(8,128)(2,1)} %shard_map.83.half_ref), custom_call_target="tpu_custom_call" | custom-call | flops 1048576 | bytes 1474560 | tf_op jit(solution)/shard_map/pallas_call | solution.py:145
  78.4 4.5 %collective-permute-start.2 = (bf16[12,40,768]{2,1,0:T(8,128)(2,1)}, bf16[12,40,768]{2,1,0:T(8,128)(2,1)}, u32[]{:S(2)}, u32[]{:S(2)}) collective-permute-start(bf16[12,40,768]{2,1,0:T(8,128)(2,1)} %shard_map.85), channel_id=1, source_target_pairs={{0,17},{1,16},{16,1},{17,0},{2,19},{3,18},{18,3},{19,2},{4,21},{5,... | collective-permute-start | bytes 2211848 | tf_op jit(solution)/shard_map/ppermute | solution.py:382
  82.9 0.9 shard_map.84
  83.8 4.1 %collective-permute-start.1 = (bf16[12,40,768]{2,1,0:T(8,128)(2,1)}, bf16[12,40,768]{2,1,0:T(8,128)(2,1)}, u32[]{:S(2)}, u32[]{:S(2)}) collective-permute-start(bf16[12,40,768]{2,1,0:T(8,128)(2,1)} %shard_map.84), channel_id=1, source_target_pairs={{0,16},{1,17},{16,0},{17,1},{2,18},{3,19},{18,2},{19,3},{4,20},{5,... | collective-permute-start | bytes 2211848 | tf_op jit(solution)/shard_map/ppermute | solution.py:382
  88.0 11.9 %collective-permute-done.2.refs_4_ = bf16[12,40,768]{2,1,0:T(8,128)(2,1)} collective-permute-done((bf16[12,40,768]{2,1,0:T(8,128)(2,1)}, bf16[12,40,768]{2,1,0:T(8,128)(2,1)}, u32[]{:S(2)}, u32[]{:S(2)}) %collective-permute-start.2) | collective-permute-done | bytes 737312 | tf_op jit(solution)/shard_map/ppermute | solution.py:382
  99.9 16.8 %collective-permute-done.1.refs_2_ = bf16[12,40,768]{2,1,0:T(8,128)(2,1)} collective-permute-done((bf16[12,40,768]{2,1,0:T(8,128)(2,1)}, bf16[12,40,768]{2,1,0:T(8,128)(2,1)}, u32[]{:S(2)}, u32[]{:S(2)}) %collective-permute-start.1) | collective-permute-done | bytes 737312 | tf_op jit(solution)/shard_map/ppermute | solution.py:382
  116.7 0.0 all-to-all-done.2
  116.7 0.0 copy-start.5
  116.7 0.0 copy-start.7
  116.7 0.0 copy-start.9
  116.7 2.8 %synthesis.1 = bf16[512,128]{1,0:T(8,128)(2,1)S(1)} custom-call(s32[1]{0:T(128)} %bitcast.spot_ref, s32[1]{0:T(128)} %bitcast.1.first_ref, bf16[384,768]{1,0:T(8,128)(2,1)S(1)} %bitcast.15, bf16[24,40,768]{2,1,0:T(8,128)(2,1)S(1)} %shard_map.82.refs_2_.half_ref.refs_1_, bf16[12,40,768]{2,1,0:T(8,128)(2,1)} %collective-permute-done.1.refs_2_, ...), custom_call_target="tpu_custom_call" | custom-call | flops 94371840 | bytes 4194304 | tf_op jit(solution)/shard_map/synthesis/pallas_call | solution.py:265
  119.5 15.4 %all_to_all.21 = bf16[64,8,128]{2,1,0:T(8,128)(2,1)S(1)} all-to-all(bf16[64,8,128]{2,1,0:T(8,128)(2,1)S(1)} %bitcast.17), channel_id=1, replica_groups=mesh['cons'=16,'blk_0'=2,'blk_1'=8,'blk_2'=2] {'cons','blk_2','blk_0'}, dimensions={0} | all-to-all | bytes 262144 | tf_op jit(solution)/shard_map/all_to_all | solution.py:397
  134.8 0.0 copy-done.5
  134.8 0.0 copy-done.7
  134.8 0.0 copy-done.9
  134.9 2.2 %inverse_dft.1 = f32[40,6144]{1,0:T(8,128)} custom-call(bf16[512,128]{1,0:T(8,128)(2,1)S(1)} %bitcast.18, f32[2,16,768]{2,1,0:T(8,128)S(1)} %copy-done.9, f32[2,16,768]{2,1,0:T(8,128)S(1)} %copy-done.7, f32[2,24,768]{2,1,0:T(8,128)S(1)} %copy-done.5), custom_call_target="tpu_custom_call" | custom-call | flops 754974720 | bytes 1048576 | tf_op jit(solution)/shard_map/inverse_dft/pallas_call | solution.py:346
  (1 shorter events, 0.0 us)
Async XLA Ops:
  0.0 1.8 %copy-start = (bf16[40,48,768]{2,1,0:T(8,128)(2,1)S(1)}, bf16[40,48,768]{2,1,0:T(8,128)(2,1)}, u32[]{:S(2)}) copy-start(bf16[40,48,768]{2,1,0:T(8,128)(2,1)} %legendre_ref.3) | copy-start | bytes 8847364
  1.8 10.3 %copy-start.11 = (f32[40]{0:T(128)S(1)}, f32[40]{0:T(128)}, u32[]{:S(2)}) copy-start(f32[40]{0:T(128)} %param.10) | copy-start | bytes 484
  1.8 10.4 %copy-start.3 = (bf16[1,40,6144]{2,1,0:T(8,128)(2,1)S(1)}, bf16[1,40,6144]{2,1,0:T(8,128)(2,1)}, u32[]{:S(2)}) copy-start(bf16[1,40,6144]{2,1,0:T(8,128)(2,1)} %param.8) | copy-start | bytes 1474564
  1.8 10.4 %copy-start.4 = (f32[2,24,768]{2,1,0:T(8,128)S(1)}, f32[2,24,768]{2,1,0:T(8,128)}, u32[]{:S(2)}) copy-start(f32[2,24,768]{2,1,0:T(8,128)} %constant.31.clone.turn_ref) | copy-start | bytes 442372
  1.8 10.4 %copy-start.6 = (f32[2,16,768]{2,1,0:T(8,128)S(1)}, f32[2,16,768]{2,1,0:T(8,128)}, u32[]{:S(2)}) copy-start(f32[2,16,768]{2,1,0:T(8,128)} %constant.30.clone.fine_ref) | copy-start | bytes 294916
  1.8 10.4 %copy-start.8 = (f32[2,16,768]{2,1,0:T(8,128)S(1)}, f32[2,16,768]{2,1,0:T(8,128)}, u32[]{:S(2)}) copy-start(f32[2,16,768]{2,1,0:T(8,128)} %constant.29.clone.coarse_ref) | copy-start | bytes 294916
  3.4 24.0 %collective-permute-start = (bf16[24,40,768]{2,1,0:T(8,128)(2,1)}, bf16[24,40,768]{2,1,0:T(8,128)(2,1)S(1)}, u32[]{:S(2)}, u32[]{:S(2)}) collective-permute-start(bf16[24,40,768]{2,1,0:T(8,128)(2,1)} %shard_map.83.half_ref), channel_id=1, source_target_pairs={{0,1},{1,0},{16,17},{17,16},{2,3},{3,2},{18,19},{19,18},{4,5},{5,4... | collective-permute-start | bytes 4423688 | tf_op jit(solution)/shard_map/ppermute | solution.py:382
  14.4 13.0 %all-to-all-start = ((bf16[32,16,128]{2,1,0:T(8,128)(2,1)}), bf16[32,16,128]{2,1,0:T(8,128)(2,1)S(1)}, u32[]{:S(2)}, u32[]{:S(2)}) async-start(bf16[32,16,128]{2,1,0:T(8,128)(2,1)} %bitcast.5), calls=%async_computation | async-start | bytes 262144 | tf_op jit(solution)/shard_map/all_to_all | solution.py:397
  18.0 1.8 %copy-start.1 = (bf16[40,48,768]{2,1,0:T(8,128)(2,1)S(1)}, bf16[40,48,768]{2,1,0:T(8,128)(2,1)}, u32[]{:S(2)}) copy-start(bf16[40,48,768]{2,1,0:T(8,128)(2,1)} %legendre_ref.3) | copy-start | bytes 8847364
  19.9 7.5 %copy-start.2 = (s32[16]{0:T(128)S(1)}, s32[16]{0:T(128)}, u32[]{:S(2)}) copy-start(s32[16]{0:T(128)} %refs_0_.1) | copy-start | bytes 196
  28.7 41.5 %copy-start.10 = (f32[768]{0:T(1024)S(1)}, f32[768]{0:T(1024)}, u32[]{:S(2)}) copy-start(f32[768]{0:T(1024)} %param.11) | copy-start | bytes 9220
  71.0 45.6 %all-to-all-start.2 = ((bf16[8,48,768]{2,1,0:T(8,128)(2,1)}), bf16[8,48,768]{2,1,0:T(8,128)(2,1)S(1)}, u32[]{:S(2)}, u32[]{:S(2)}) async-start(bf16[8,48,768]{2,1,0:T(8,128)(2,1)} %broadcast_in_dim.35), calls=%async_computation.2 | async-start | bytes 1179648 | tf_op jit(solution)/shard_map/all_to_all | solution.py:413
  78.4 21.5 %collective-permute-start.2 = (bf16[12,40,768]{2,1,0:T(8,128)(2,1)}, bf16[12,40,768]{2,1,0:T(8,128)(2,1)}, u32[]{:S(2)}, u32[]{:S(2)}) collective-permute-start(bf16[12,40,768]{2,1,0:T(8,128)(2,1)} %shard_map.85), channel_id=1, source_target_pairs={{0,17},{1,16},{16,1},{17,0},{2,19},{3,18},{18,3},{19,2},{4,21},{5,... | collective-permute-start | bytes 2211848 | tf_op jit(solution)/shard_map/ppermute | solution.py:382
  83.8 32.9 %collective-permute-start.1 = (bf16[12,40,768]{2,1,0:T(8,128)(2,1)}, bf16[12,40,768]{2,1,0:T(8,128)(2,1)}, u32[]{:S(2)}, u32[]{:S(2)}) collective-permute-start(bf16[12,40,768]{2,1,0:T(8,128)(2,1)} %shard_map.84), channel_id=1, source_target_pairs={{0,16},{1,17},{16,0},{17,1},{2,18},{3,19},{18,2},{19,3},{4,20},{5,... | collective-permute-start | bytes 2211848 | tf_op jit(solution)/shard_map/ppermute | solution.py:382
  116.7 18.2 %copy-start.5 = (f32[2,24,768]{2,1,0:T(8,128)S(1)}, f32[2,24,768]{2,1,0:T(8,128)}, u32[]{:S(2)}) copy-start(f32[2,24,768]{2,1,0:T(8,128)} %constant.31.clone.turn_ref) | copy-start | bytes 442372
  116.7 18.2 %copy-start.7 = (f32[2,16,768]{2,1,0:T(8,128)S(1)}, f32[2,16,768]{2,1,0:T(8,128)}, u32[]{:S(2)}) copy-start(f32[2,16,768]{2,1,0:T(8,128)} %constant.30.clone.fine_ref) | copy-start | bytes 294916
  116.7 18.2 %copy-start.9 = (f32[2,16,768]{2,1,0:T(8,128)S(1)}, f32[2,16,768]{2,1,0:T(8,128)}, u32[]{:S(2)}) copy-start(f32[2,16,768]{2,1,0:T(8,128)} %constant.29.clone.coarse_ref) | copy-start | bytes 294916

commit v3 on v2

--- a/solution.py
+++ b/solution.py
@@ -122,36 +122,60 @@
         cost_estimate=pl.CostEstimate(
             flops=4 * cycles * longitudes * orders, bytes_accessed=1 << 20, transcendentals=0
         ),
-        compiler_params=pltpu.CompilerParams(vmem_limit_bytes=ROOM),
         name="forward_dft",
     )(elevation, weight, coarse, fine, turn)
 
 
-def split_kernel(place_ref, legendre_ref, half_ref):
-    orders = half_ref.shape[0]
-    for first in range(0, orders, TILE):
-        start = pl.multiple_of(place_ref[0] * orders + first, TILE)
-        half_ref[first : first + TILE] = jnp.swapaxes(
-            legendre_ref[:, pl.ds(start, TILE), :], 0, 1
-        )
+def split_kernel(place_ref, legendre_ref, sent_ref, own_ref, part_ref):
+    core, side = place_ref[0], place_ref[1]
+    orders, share = own_ref.shape[0], part_ref.shape[0]
+    for target, index in ((sent_ref, 1 - core), (own_ref, core)):
+        for first in range(0, orders, TILE):
+            start = pl.multiple_of(index * orders + first, TILE)
+            target[first : first + TILE] = jnp.swapaxes(
+                legendre_ref[:, pl.ds(start, TILE), :], 0, 1
+            )
+    part_ref[...] = own_ref[pl.ds((1 - side) * share, share)]
 
 
 def part_kernel(place_ref, half_ref, part_ref):
     share = part_ref.shape[0]
-    part_ref[...] = half_ref[pl.ds(place_ref[0] * share, share)]
-
-
-def halved(kernel, place, values, shape):
+    part_ref[...] = half_ref[pl.ds((1 - place_ref[1]) * share, share)]
+
+
+def divided(kernel, place, values, orders, cycles):
+    degrees = values.shape[2]
     return pl.pallas_call(
         kernel,
         in_specs=[SCALARS, NEARBY],
+        out_specs=[NEARBY] * len(orders),
+        out_shape=[
+            jax.ShapeDtypeStruct((count, cycles, degrees), values.dtype) for count in orders
+        ],
+        cost_estimate=pl.CostEstimate(
+            flops=1 << 20, bytes_accessed=4 * cycles * sum(orders) * degrees, transcendentals=0
+        ),
+        compiler_params=pltpu.CompilerParams(vmem_limit_bytes=ROOM),
+    )(place, values)
+
+
+def table_kernel(coarse_ref, fine_ref, table_ref):
+    inner_table(coarse_ref, fine_ref, table_ref, slice(None))
+
+
+def inner_tables(coarse, fine):
+    shape = (2, INNER, coarse.shape[2])
+    return pl.pallas_call(
+        table_kernel,
+        in_specs=[NEARBY] * 2,
         out_specs=NEARBY,
-        out_shape=jax.ShapeDtypeStruct(shape, values.dtype),
-        cost_estimate=pl.CostEstimate(
-            flops=1 << 20, bytes_accessed=4 * math.prod(shape), transcendentals=0
+        out_shape=jax.ShapeDtypeStruct(shape, jnp.bfloat16),
+        cost_estimate=pl.CostEstimate(
+            flops=1 << 20, bytes_accessed=2 * math.prod(shape), transcendentals=0
         ),
         compiler_params=pltpu.CompilerParams(vmem_limit_bytes=ROOM),
-    )(place[None].astype(jnp.int32), values)
+        name="tables",
+    )(coarse, fine)
 
 
 def analysis_kernel(near, spot_ref, *refs):
@@ -285,12 +309,10 @@
 def inverse_kernel(
     peers,
     moved_ref,
-    coarse_ref,
-    fine_ref,
+    table_ref,
     turn_ref,
     out_ref,
     rows_ref,
-    table_ref,
     row_ref,
     flip_ref,
     part_ref,
@@ -299,7 +321,6 @@
     parts, cycles, span = part_ref.shape
     count = span // INNER
     orders = flip_ref.shape[1]
-    inner_table(coarse_ref, fine_ref, table_ref, slice(None))
     row_ref[...] = moved_ref[...].astype(jnp.float32)
     deep = moved_ref.shape[0] // peers
     share = orders // peers
@@ -339,18 +360,17 @@
         copy.wait()
 
 
-def inverse(moved, coarse, fine, turn, cycles, longitudes, peers):
-    orders = coarse.shape[2]
+def inverse(moved, table, turn, cycles, longitudes, peers):
+    orders = turn.shape[2]
     count = 6
     parts = longitudes // INNER // count
     return pl.pallas_call(
         functools.partial(inverse_kernel, peers),
-        in_specs=[NEARBY] * 4,
+        in_specs=[NEARBY] * 3,
         out_specs=pl.BlockSpec(memory_space=pltpu.HBM),
         out_shape=jax.ShapeDtypeStruct((cycles, longitudes), jnp.float32),
         scratch_shapes=[
             pltpu.VMEM((2, 2, count * cycles, orders), jnp.bfloat16),
-            pltpu.VMEM((2, INNER, orders), jnp.bfloat16),
             pltpu.VMEM(moved.shape, jnp.float32),
             pltpu.VMEM((2, orders, LANES), jnp.float32),
             pltpu.VMEM((parts, cycles, count * INNER), jnp.float32),
@@ -361,7 +381,7 @@
         ),
         compiler_params=pltpu.CompilerParams(vmem_limit_bytes=ROOM),
         name="inverse_dft",
-    )(moved, coarse, fine, turn)
+    )(moved, table, turn)
 
 
 def local(elevation, legendre, cycle_weight, love_factor, assignment):
@@ -382,14 +402,7 @@
         return lax.ppermute(values, NEAR[::-1], pairs)
 
     half, share = orders_dev // cores, orders_dev // near
-
-    def placed(which):
-        shape = (half, cycle_dev, degrees)
-        return halved(split_kernel, which, legendre, shape)
-
-    def part_of(values):
-        shape = (share, cycle_dev, degrees)
-        return halved(part_kernel, 1 - side, values, shape)
+    place = jnp.stack([core, side]).astype(jnp.int32)
 
     def exchanged(packed, axes):
         peers = lax.axis_size(axes)
@@ -397,21 +410,22 @@
         tiles = lax.all_to_all(tiles, axes, 0, 0, tiled=True)
         return tiles.reshape(-1, LANES)
 
-    sent = placed(1 - core)
+    sent, own, own_part = divided(split_kernel, place, legendre, (half, half, share), cycle_dev)
     met = swapped(sent, 1)
-    own = placed(core)
+    own_side = swapped(own_part, 2)
+    (sent_part,) = divided(part_kernel, place, sent, (share,), cycle_dev)
+    met_side = swapped(sent_part, 3)
+    table = inner_tables(coarse, fine)
     lines = groups * orders_dev * 2 // (LANES // cycle_dev)
     packed = forward(elevation[0], cycle_weight[:, None], coarse, fine, turn, lines, groups * cores)
     moved = exchanged(packed, ("cons", CORE))
     partial = analyse(core[None].astype(jnp.int32), assignment, moved, [own, met])
     rows = partial.shape[0] // far
     arrived = lax.all_to_all(partial.reshape(far, rows, degrees), FAR, 0, 0, tiled=True)
-    own_side = swapped(part_of(own), 2)
     analysis = jnp.sum(arrived.astype(jnp.float32), axis=0)
     scaled = (analysis * love_factor[None, :]).astype(jnp.bfloat16)
     copies = jnp.broadcast_to(scaled[None], (deep, rows, degrees))
     coefficients = lax.all_to_all(copies, DEEP, 0, 0, tiled=True)
-    met_side = swapped(part_of(sent), 3)
     first = ((lax.axis_index("cons") * near + spot) * share)[None].astype(jnp.int32)
     synthesis = synthesise(
         spot[None].astype(jnp.int32),
@@ -421,9 +435,7 @@
         lines,
     )
     returned = exchanged(synthesis, ("cons", *NEAR))
-    return inverse(
-        returned, coarse, fine, turn, cycle_dev, longitudes, groups * near
-    )[None]
+    return inverse(returned, table, turn, cycle_dev, longitudes, groups * near)[None]
 
 
 def solution(mesh):

time: 138 us -> 139 us (level)
  local copies, waits for them, and re-layouts: 4.65 us -> 7.6 us
  blocking collectives: 56.7 us -> 54.3 us
    all_to_all x1, blocking collectives: 15.4 us -> 12.9 us  [exchanged(): tiles = lax.all_to_all(tiles, axes, 0, 0, tiled=True)]
    unnamed x24 -> x18, local copies, waits for them, and re-layouts: 3.7 us -> 6.05 us
    ppermute x3, waiting for transfers between devices: 28.7 us -> 26.4 us  [swapped(): return lax.ppermute(values, NEAR[::-1], pairs)]
    pallas_call x4 -> x3, Pallas kernels: 5.08 us -> 4.56 us  [the longest x2 4.32 us: divided(): pl.pallas_call(kernel, in_specs=[SCALARS, NEARBY], out_specs=[NEARBY] * l...]
  transfers between devices with their start and end apart: 5 -> 5, of which waited for: 3 -> 3; matrix products, arithmetic and copies ran while one was open for 0% -> 1% of each run, Pallas kernels for 4% -> 4%
where the time goes in v3:
time: 139 us; the launch traced here: 138 us
  blocking collectives  54.3 us (39%)
  waiting for transfers between devices  34.8 us (25%)
  starting transfers between devices  26.9 us (19%)
  Pallas kernels  14 us (10%)
  local copies, waits for them, and re-layouts  7.6 us (5%)
    all_to_all x1, blocking collectives, local(): lax.all_to_all(partial.reshape(far, rows, degrees), FAR, 0, 0, tiled=True)  41.3 us
    ppermute x3, waiting for transfers between devices, swapped(): return lax.ppermute(values, NEAR[::-1], pairs)  26.4 us
    ppermute x3, starting transfers between devices, swapped(): return lax.ppermute(values, NEAR[::-1], pairs)  17.7 us
    all_to_all x1, blocking collectives, exchanged(): tiles = lax.all_to_all(tiles, axes, 0, 0, tiled=True)  12.9 us
    all_to_all x1, waiting for transfers between devices, exchanged(): tiles = lax.all_to_all(tiles, axes, 0, 0, tiled=True)  8.4 us
    unnamed x18, local copies, waits for them, and re-layouts  6.05 us
    all_to_all x1, starting transfers between devices, local(): coefficients = lax.all_to_all(copies, DEEP, 0, 0, tiled=True)  5.06 us
    pallas_call x2, Pallas kernels, divided(): pl.pallas_call(kernel, in_specs=[SCALARS, NEARBY], out_specs=[NEARBY] * l...  4.32 us
  transfers between devices with their start and end apart: 5, of which 3 were waited for; matrix products, arithmetic and copies ran while one was open for 1% of the time, Pallas kernels for 4%

profile of v3, /device:TPU:1, one launch (start us, length us, event | category | flops | bytes accessed | tf_op | source)
XLA Modules:
  0.0 138.0 jit_solution(10866512335166022765)
XLA Ops:
  0.0 0.1 pad_add_fusion.place_ref
  0.1 0.0 copy-start
  0.1 1.8 %copy-done = bf16[40,48,768]{2,1,0:T(8,128)(2,1)S(1)} copy-done((bf16[40,48,768]{2,1,0:T(8,128)(2,1)S(1)}, bf16[40,48,768]{2,1,0:T(8,128)(2,1)}, u32[]{:S(2)}) %copy-start) | copy-done | bytes 2949144
  1.9 0.0 copy-start.8
  1.9 2.0 %shard_map.82 = (bf16[24,40,768]{2,1,0:T(8,128)(2,1)}, bf16[24,40,768]{2,1,0:T(8,128)(2,1)S(1)}, bf16[12,40,768]{2,1,0:T(8,128)(2,1)S(1)}) custom-call(s32[2]{0:T(128)S(1)} %pad_add_fusion.place_ref, bf16[40,48,768]{2,1,0:T(8,128)(2,1)S(1)} %copy-done), custom_call_target="tpu_custom_call" | custom-call | flops 1048576 | bytes 7372800 | tf_op jit(solution)/shard_map/pallas_call | solution.py:148
  3.9 0.0 copy-start.5
  3.9 0.9 copy-done.5
  4.8 8.7 %collective-permute-start = (bf16[24,40,768]{2,1,0:T(8,128)(2,1)}, bf16[24,40,768]{2,1,0:T(8,128)(2,1)S(1)}, u32[]{:S(2)}, u32[]{:S(2)}) collective-permute-start(bf16[24,40,768]{2,1,0:T(8,128)(2,1)} %get-tuple-element.9.half_ref), channel_id=1, source_target_pairs={{0,1},{1,0},{16,17},{17,16},{2,3},{3,2},{18,19},{19,18},{4,5},{5,4... | collective-permute-start | bytes 4423688 | tf_op jit(solution)/shard_map/ppermute | solution.py:402
  13.5 0.0 copy-done.8
  13.5 0.7 copy.9.weight_ref
  14.2 0.0 copy-start.4
  14.2 3.3 %forward_dft.1 = bf16[512,128]{1,0:T(8,128)(2,1)} custom-call(bf16[40,6144]{1,0:T(8,128)(2,1)} %bitcast.20, f32[40,1]{1,0:T(8,128)} %copy.9.weight_ref, f32[2,16,768]{2,1,0:T(8,128)} %constant.27.clone.coarse_ref, f32[2,16,768]{2,1,0:T(8,128)} %constant.28.clone.fine_ref, f32[2,24,768]{2,1,0:T(8,128)} %constant.29.clone.turn_ref), custom_call_target="tpu_custom_call" | custom-call | flops 754974720 | bytes 1048576 | tf_op jit(solution)/shard_map/forward_dft/pallas_call | solution.py:111
  17.6 12.9 %all_to_all.20 = bf16[32,16,128]{2,1,0:T(8,128)(2,1)S(1)} all-to-all(bf16[32,16,128]{2,1,0:T(8,128)(2,1)} %bitcast.18), channel_id=1, replica_groups=mesh['cons'=16,'blk_0'=2,'blk_1'=8,'blk_2'=2] {'cons','blk_2'}, dimensions={0} | all-to-all | bytes 262144 | tf_op jit(solution)/shard_map/all_to_all | solution.py:410
  30.5 0.0 collective-permute-done.refs_3_
  30.5 0.0 copy-done.4
  30.5 1.3 analysis.1
  31.8 0.0 copy-start.7
  31.8 41.3 %all_to_all.21 = bf16[16,48,768]{2,1,0:T(8,128)(2,1)S(1)} all-to-all(bf16[16,48,768]{2,1,0:T(8,128)(2,1)S(1)} %bitcast.13), channel_id=1, replica_groups=mesh['cons'=16,'blk_0'=2,'blk_1'=8,'blk_2'=2] {'blk_0','blk_1'}, dimensions={0} | all-to-all | bytes 2359296 | tf_op jit(solution)/shard_map/all_to_all | solution.py:424
  73.1 0.2 convert_reduce_fusion
  73.3 0.0 copy-done.7
  73.3 0.8 broadcast_in_dim.26
  74.2 5.1 %all-to-all-start.2 = ((bf16[8,48,768]{2,1,0:T(8,128)(2,1)}), bf16[8,48,768]{2,1,0:T(8,128)(2,1)S(1)}, u32[]{:S(2)}, u32[]{:S(2)}) async-start(bf16[8,48,768]{2,1,0:T(8,128)(2,1)} %broadcast_in_dim.26), calls=%async_computation.2 | async-start | bytes 1179648 | tf_op jit(solution)/shard_map/all_to_all | solution.py:428
  79.2 2.7 %collective-permute-start.1 = (bf16[12,40,768]{2,1,0:T(8,128)(2,1)}, bf16[12,40,768]{2,1,0:T(8,128)(2,1)}, u32[]{:S(2)}, u32[]{:S(2)}) collective-permute-start(bf16[12,40,768]{2,1,0:T(8,128)(2,1)} %copy-done.5), channel_id=1, source_target_pairs={{0,16},{1,17},{16,0},{17,1},{2,18},{3,19},{18,2},{19,3},{4,20},{5,... | collective-permute-start | bytes 2211848 | tf_op jit(solution)/shard_map/ppermute | solution.py:402
  82.0 2.3 %shard_map.83 = bf16[12,40,768]{2,1,0:T(8,128)(2,1)} custom-call(s32[2]{0:T(128)S(1)} %pad_add_fusion.place_ref, bf16[24,40,768]{2,1,0:T(8,128)(2,1)} %get-tuple-element.9.half_ref), custom_call_target="tpu_custom_call" | custom-call | flops 1048576 | bytes 1474560 | tf_op jit(solution)/shard_map/pallas_call | solution.py:148
  84.3 6.2 %collective-permute-start.2 = (bf16[12,40,768]{2,1,0:T(8,128)(2,1)}, bf16[12,40,768]{2,1,0:T(8,128)(2,1)}, u32[]{:S(2)}, u32[]{:S(2)}) collective-permute-start(bf16[12,40,768]{2,1,0:T(8,128)(2,1)} %shard_map.83), channel_id=1, source_target_pairs={{0,17},{1,16},{16,1},{17,0},{2,19},{3,18},{18,3},{19,2},{4,21},{5,... | collective-permute-start | bytes 2211848 | tf_op jit(solution)/shard_map/ppermute | solution.py:402
  90.5 8.5 %collective-permute-done.1.refs_2_ = bf16[12,40,768]{2,1,0:T(8,128)(2,1)} collective-permute-done((bf16[12,40,768]{2,1,0:T(8,128)(2,1)}, bf16[12,40,768]{2,1,0:T(8,128)(2,1)}, u32[]{:S(2)}, u32[]{:S(2)}) %collective-permute-start.1) | collective-permute-done | bytes 737312 | tf_op jit(solution)/shard_map/ppermute | solution.py:402
  99.0 18.0 %collective-permute-done.2.refs_4_ = bf16[12,40,768]{2,1,0:T(8,128)(2,1)} collective-permute-done((bf16[12,40,768]{2,1,0:T(8,128)(2,1)}, bf16[12,40,768]{2,1,0:T(8,128)(2,1)}, u32[]{:S(2)}, u32[]{:S(2)}) %collective-permute-start.2) | collective-permute-done | bytes 737312 | tf_op jit(solution)/shard_map/ppermute | solution.py:402
  117.0 0.0 all-to-all-done.2
  117.0 2.7 %synthesis.1 = bf16[512,128]{1,0:T(8,128)(2,1)S(1)} custom-call(s32[1]{0:T(128)} %bitcast.spot_ref, s32[1]{0:T(128)} %bitcast.1.first_ref, bf16[384,768]{1,0:T(8,128)(2,1)S(1)} %bitcast.14, bf16[24,40,768]{2,1,0:T(8,128)(2,1)S(1)} %get-tuple-element.8.refs_2_.refs_1_, bf16[12,40,768]{2,1,0:T(8,128)(2,1)} %collective-permute-done.1.refs_2_, ...), custom_call_target="tpu_custom_call" | custom-call | flops 94371840 | bytes 4194304 | tf_op jit(solution)/shard_map/synthesis/pallas_call | solution.py:289
  119.7 0.0 copy-start.1
  119.7 0.6 copy-done.1
  120.4 4.2 %all-to-all-start.3 = ((bf16[64,8,128]{2,1,0:T(8,128)(2,1)}), bf16[64,8,128]{2,1,0:T(8,128)(2,1)S(1)}, u32[]{:S(2)}, u32[]{:S(2)}) async-start(bf16[64,8,128]{2,1,0:T(8,128)(2,1)} %bitcast.15), calls=%async_computation.3 | async-start | bytes 262144 | tf_op jit(solution)/shard_map/all_to_all | solution.py:410
  124.6 0.0 copy-start.2
  124.6 0.9 copy-done.2
  125.5 0.0 copy-start.3
  125.5 0.9 copy-done.3
  126.4 0.2 tables.1.table_ref
  126.6 8.4 %all-to-all-done.3 = bf16[64,8,128]{2,1,0:T(8,128)(2,1)S(1)} async-done(((bf16[64,8,128]{2,1,0:T(8,128)(2,1)}), bf16[64,8,128]{2,1,0:T(8,128)(2,1)S(1)}, u32[]{:S(2)}, u32[]{:S(2)}) %all-to-all-start.3) | async-done | bytes 131104 | tf_op jit(solution)/shard_map/all_to_all | solution.py:410
  135.0 0.0 copy-start.6
  135.0 0.9 copy-done.6
  135.9 2.1 %inverse_dft.1 = f32[40,6144]{1,0:T(8,128)} custom-call(bf16[512,128]{1,0:T(8,128)(2,1)S(1)} %bitcast.17, bf16[2,256,768]{2,1,0:T(8,128)(2,1)S(1)} %tables.1.table_ref, f32[2,24,768]{2,1,0:T(8,128)S(1)} %copy-done.6), custom_call_target="tpu_custom_call" | custom-call | flops 754974720 | bytes 1048576 | tf_op jit(solution)/shard_map/inverse_dft/pallas_call | solution.py:367
  (1 shorter events, 0.0 us)
Async XLA Ops:
  0.1 1.8 %copy-start = (bf16[40,48,768]{2,1,0:T(8,128)(2,1)S(1)}, bf16[40,48,768]{2,1,0:T(8,128)(2,1)}, u32[]{:S(2)}) copy-start(bf16[40,48,768]{2,1,0:T(8,128)(2,1)} %legendre_ref.1) | copy-start | bytes 8847364
  1.9 11.6 %copy-start.8 = (f32[40]{0:T(128)S(1)}, f32[40]{0:T(128)}, u32[]{:S(2)}) copy-start(f32[40]{0:T(128)} %param.10) | copy-start | bytes 484
  3.9 0.9 copy-start.5
  4.8 25.7 %collective-permute-start = (bf16[24,40,768]{2,1,0:T(8,128)(2,1)}, bf16[24,40,768]{2,1,0:T(8,128)(2,1)S(1)}, u32[]{:S(2)}, u32[]{:S(2)}) collective-permute-start(bf16[24,40,768]{2,1,0:T(8,128)(2,1)} %get-tuple-element.9.half_ref), channel_id=1, source_target_pairs={{0,1},{1,0},{16,17},{17,16},{2,3},{3,2},{18,19},{19,18},{4,5},{5,4... | collective-permute-start | bytes 4423688 | tf_op jit(solution)/shard_map/ppermute | solution.py:402
  14.2 16.3 %copy-start.4 = (s32[16]{0:T(128)S(1)}, s32[16]{0:T(128)}, u32[]{:S(2)}) copy-start(s32[16]{0:T(128)} %refs_0_.1) | copy-start | bytes 196
  31.8 41.5 %copy-start.7 = (f32[768]{0:T(1024)S(1)}, f32[768]{0:T(1024)}, u32[]{:S(2)}) copy-start(f32[768]{0:T(1024)} %param.11) | copy-start | bytes 9220
  74.2 42.8 %all-to-all-start.2 = ((bf16[8,48,768]{2,1,0:T(8,128)(2,1)}), bf16[8,48,768]{2,1,0:T(8,128)(2,1)S(1)}, u32[]{:S(2)}, u32[]{:S(2)}) async-start(bf16[8,48,768]{2,1,0:T(8,128)(2,1)} %broadcast_in_dim.26), calls=%async_computation.2 | async-start | bytes 1179648 | tf_op jit(solution)/shard_map/all_to_all | solution.py:428
  79.2 19.7 %collective-permute-start.1 = (bf16[12,40,768]{2,1,0:T(8,128)(2,1)}, bf16[12,40,768]{2,1,0:T(8,128)(2,1)}, u32[]{:S(2)}, u32[]{:S(2)}) collective-permute-start(bf16[12,40,768]{2,1,0:T(8,128)(2,1)} %copy-done.5), channel_id=1, source_target_pairs={{0,16},{1,17},{16,0},{17,1},{2,18},{3,19},{18,2},{19,3},{4,20},{5,... | collective-permute-start | bytes 2211848 | tf_op jit(solution)/shard_map/ppermute | solution.py:402
  84.3 32.7 %collective-permute-start.2 = (bf16[12,40,768]{2,1,0:T(8,128)(2,1)}, bf16[12,40,768]{2,1,0:T(8,128)(2,1)}, u32[]{:S(2)}, u32[]{:S(2)}) collective-permute-start(bf16[12,40,768]{2,1,0:T(8,128)(2,1)} %shard_map.83), channel_id=1, source_target_pairs={{0,17},{1,16},{16,1},{17,0},{2,19},{3,18},{18,3},{19,2},{4,21},{5,... | collective-permute-start | bytes 2211848 | tf_op jit(solution)/shard_map/ppermute | solution.py:402
  119.7 0.7 copy-start.1
  120.4 14.6 %all-to-all-start.3 = ((bf16[64,8,128]{2,1,0:T(8,128)(2,1)}), bf16[64,8,128]{2,1,0:T(8,128)(2,1)S(1)}, u32[]{:S(2)}, u32[]{:S(2)}) async-start(bf16[64,8,128]{2,1,0:T(8,128)(2,1)} %bitcast.15), calls=%async_computation.3 | async-start | bytes 262144 | tf_op jit(solution)/shard_map/all_to_all | solution.py:410
  124.6 0.9 copy-start.2
  125.5 0.9 copy-start.3
  135.0 0.9 copy-start.6

commit v4 on v3

--- a/solution.py
+++ b/solution.py
@@ -89,8 +89,8 @@
             two = odd[rows] * cosine - even[rows] * sine
             first = one if first is None else first + one
             second = two if second is None else second + two
-        flip_ref[0, lanes, :cycles] = jnp.transpose(first * weight)
-        flip_ref[1, lanes, :cycles] = jnp.transpose(second * weight)
+        flip_ref[0, lanes, :cycles] = jnp.transpose(first) * weight
+        flip_ref[1, lanes, :cycles] = jnp.transpose(second) * weight
 
     beside = LANES // cycles
     deep = out_ref.shape[0] // peers
@@ -417,7 +417,7 @@
     met_side = swapped(sent_part, 3)
     table = inner_tables(coarse, fine)
     lines = groups * orders_dev * 2 // (LANES // cycle_dev)
-    packed = forward(elevation[0], cycle_weight[:, None], coarse, fine, turn, lines, groups * cores)
+    packed = forward(elevation[0], cycle_weight[None, :], coarse, fine, turn, lines, groups * cores)
     moved = exchanged(packed, ("cons", CORE))
     partial = analyse(core[None].astype(jnp.int32), assignment, moved, [own, met])
     rows = partial.shape[0] // far

time: 139 us -> 138 us (level)
    unnamed x18 -> x16, local copies, waits for them, and re-layouts: 6.05 us -> 6.05 us
  transfers between devices with their start and end apart: 5 -> 5, of which waited for: 3 -> 3; matrix products, arithmetic and copies ran while one was open for 1% -> 0% of each run, Pallas kernels for 4% -> 4%
where the time goes in v4:
time: 138 us; the launch traced here: 137 us
  blocking collectives  54.3 us (39%)
  waiting for transfers between devices  34.9 us (25%)
  starting transfers between devices  26.9 us (19%)
  Pallas kernels  14 us (10%)
  local copies, waits for them, and re-layouts  6.9 us (5%)
    all_to_all x1, blocking collectives, local(): lax.all_to_all(partial.reshape(far, rows, degrees), FAR, 0, 0, tiled=True)  41.3 us
    ppermute x3, waiting for transfers between devices, swapped(): return lax.ppermute(values, NEAR[::-1], pairs)  26.4 us
    ppermute x3, starting transfers between devices, swapped(): return lax.ppermute(values, NEAR[::-1], pairs)  17.7 us
    all_to_all x1, blocking collectives, exchanged(): tiles = lax.all_to_all(tiles, axes, 0, 0, tiled=True)  12.9 us
    all_to_all x1, waiting for transfers between devices, exchanged(): tiles = lax.all_to_all(tiles, axes, 0, 0, tiled=True)  8.4 us
    unnamed x16, local copies, waits for them, and re-layouts  6.05 us
    all_to_all x1, starting transfers between devices, local(): coefficients = lax.all_to_all(copies, DEEP, 0, 0, tiled=True)  5.06 us
    pallas_call x2, Pallas kernels, divided(): pl.pallas_call(kernel, in_specs=[SCALARS, NEARBY], out_specs=[NEARBY] * l...  4.32 us
  transfers between devices with their start and end apart: 5, of which 3 were waited for; matrix products, arithmetic and copies ran while one was open for 0% of the time, Pallas kernels for 4%

profile of v4, /device:TPU:1, one launch (start us, length us, event | category | flops | bytes accessed | tf_op | source)
XLA Modules:
  0.0 137.3 jit_solution(13431209739835951364)
XLA Ops:
  0.0 0.1 pad_add_fusion.place_ref
  0.1 0.0 copy-start
  0.1 1.8 %copy-done = bf16[40,48,768]{2,1,0:T(8,128)(2,1)S(1)} copy-done((bf16[40,48,768]{2,1,0:T(8,128)(2,1)S(1)}, bf16[40,48,768]{2,1,0:T(8,128)(2,1)}, u32[]{:S(2)}) %copy-start) | copy-done | bytes 2949144
  1.9 2.0 %shard_map.82 = (bf16[24,40,768]{2,1,0:T(8,128)(2,1)}, bf16[24,40,768]{2,1,0:T(8,128)(2,1)S(1)}, bf16[12,40,768]{2,1,0:T(8,128)(2,1)S(1)}) custom-call(s32[2]{0:T(128)S(1)} %pad_add_fusion.place_ref, bf16[40,48,768]{2,1,0:T(8,128)(2,1)S(1)} %copy-done), custom_call_target="tpu_custom_call" | custom-call | flops 1048576 | bytes 7372800 | tf_op jit(solution)/shard_map/pallas_call | solution.py:148
  3.9 0.0 copy-start.5
  3.9 0.9 copy-done.5
  4.8 8.7 %collective-permute-start = (bf16[24,40,768]{2,1,0:T(8,128)(2,1)}, bf16[24,40,768]{2,1,0:T(8,128)(2,1)S(1)}, u32[]{:S(2)}, u32[]{:S(2)}) collective-permute-start(bf16[24,40,768]{2,1,0:T(8,128)(2,1)} %get-tuple-element.9.half_ref), channel_id=1, source_target_pairs={{0,1},{1,0},{16,17},{17,16},{2,3},{3,2},{18,19},{19,18},{4,5},{5,4... | collective-permute-start | bytes 4423688 | tf_op jit(solution)/shard_map/ppermute | solution.py:402
  13.5 0.0 copy-start.4
  13.5 3.3 %forward_dft.1 = bf16[512,128]{1,0:T(8,128)(2,1)} custom-call(bf16[40,6144]{1,0:T(8,128)(2,1)} %bitcast.19, f32[1,40]{1,0:T(1,128)} %bitcast.20, f32[2,16,768]{2,1,0:T(8,128)} %constant.27.clone.coarse_ref, f32[2,16,768]{2,1,0:T(8,128)} %constant.28.clone.fine_ref, f32[2,24,768]{2,1,0:T(8,128)} %constant.29.clone.turn_ref), custom_call_target="tpu_custom_call" | custom-call | flops 754974720 | bytes 1048576 | tf_op jit(solution)/shard_map/forward_dft/pallas_call | solution.py:111
  16.9 12.9 %all_to_all.20 = bf16[32,16,128]{2,1,0:T(8,128)(2,1)S(1)} all-to-all(bf16[32,16,128]{2,1,0:T(8,128)(2,1)} %bitcast.18), channel_id=1, replica_groups=mesh['cons'=16,'blk_0'=2,'blk_1'=8,'blk_2'=2] {'cons','blk_2'}, dimensions={0} | all-to-all | bytes 262144 | tf_op jit(solution)/shard_map/all_to_all | solution.py:410
  29.8 0.0 collective-permute-done.refs_3_
  29.8 0.0 copy-done.4
  29.8 1.3 analysis.1
  31.1 0.0 copy-start.7
  31.1 41.3 %all_to_all.21 = bf16[16,48,768]{2,1,0:T(8,128)(2,1)S(1)} all-to-all(bf16[16,48,768]{2,1,0:T(8,128)(2,1)S(1)} %bitcast.13), channel_id=1, replica_groups=mesh['cons'=16,'blk_0'=2,'blk_1'=8,'blk_2'=2] {'blk_0','blk_1'}, dimensions={0} | all-to-all | bytes 2359296 | tf_op jit(solution)/shard_map/all_to_all | solution.py:424
  72.4 0.2 convert_reduce_fusion
  72.6 0.0 copy-done.7
  72.6 0.9 broadcast_in_dim.26
  73.5 5.1 %all-to-all-start.2 = ((bf16[8,48,768]{2,1,0:T(8,128)(2,1)}), bf16[8,48,768]{2,1,0:T(8,128)(2,1)S(1)}, u32[]{:S(2)}, u32[]{:S(2)}) async-start(bf16[8,48,768]{2,1,0:T(8,128)(2,1)} %broadcast_in_dim.26), calls=%async_computation.2 | async-start | bytes 1179648 | tf_op jit(solution)/shard_map/all_to_all | solution.py:428
  78.6 2.7 %collective-permute-start.1 = (bf16[12,40,768]{2,1,0:T(8,128)(2,1)}, bf16[12,40,768]{2,1,0:T(8,128)(2,1)}, u32[]{:S(2)}, u32[]{:S(2)}) collective-permute-start(bf16[12,40,768]{2,1,0:T(8,128)(2,1)} %copy-done.5), channel_id=1, source_target_pairs={{0,16},{1,17},{16,0},{17,1},{2,18},{3,19},{18,2},{19,3},{4,20},{5,... | collective-permute-start | bytes 2211848 | tf_op jit(solution)/shard_map/ppermute | solution.py:402
  81.3 2.3 %shard_map.83 = bf16[12,40,768]{2,1,0:T(8,128)(2,1)} custom-call(s32[2]{0:T(128)S(1)} %pad_add_fusion.place_ref, bf16[24,40,768]{2,1,0:T(8,128)(2,1)} %get-tuple-element.9.half_ref), custom_call_target="tpu_custom_call" | custom-call | flops 1048576 | bytes 1474560 | tf_op jit(solution)/shard_map/pallas_call | solution.py:148
  83.6 6.2 %collective-permute-start.2 = (bf16[12,40,768]{2,1,0:T(8,128)(2,1)}, bf16[12,40,768]{2,1,0:T(8,128)(2,1)}, u32[]{:S(2)}, u32[]{:S(2)}) collective-permute-start(bf16[12,40,768]{2,1,0:T(8,128)(2,1)} %shard_map.83), channel_id=1, source_target_pairs={{0,17},{1,16},{16,1},{17,0},{2,19},{3,18},{18,3},{19,2},{4,21},{5,... | collective-permute-start | bytes 2211848 | tf_op jit(solution)/shard_map/ppermute | solution.py:402
  89.8 8.5 %collective-permute-done.1.refs_2_ = bf16[12,40,768]{2,1,0:T(8,128)(2,1)} collective-permute-done((bf16[12,40,768]{2,1,0:T(8,128)(2,1)}, bf16[12,40,768]{2,1,0:T(8,128)(2,1)}, u32[]{:S(2)}, u32[]{:S(2)}) %collective-permute-start.1) | collective-permute-done | bytes 737312 | tf_op jit(solution)/shard_map/ppermute | solution.py:402
  98.3 18.0 %collective-permute-done.2.refs_4_ = bf16[12,40,768]{2,1,0:T(8,128)(2,1)} collective-permute-done((bf16[12,40,768]{2,1,0:T(8,128)(2,1)}, bf16[12,40,768]{2,1,0:T(8,128)(2,1)}, u32[]{:S(2)}, u32[]{:S(2)}) %collective-permute-start.2) | collective-permute-done | bytes 737312 | tf_op jit(solution)/shard_map/ppermute | solution.py:402
  116.3 0.0 all-to-all-done.2
  116.3 2.7 %synthesis.1 = bf16[512,128]{1,0:T(8,128)(2,1)S(1)} custom-call(s32[1]{0:T(128)} %bitcast.spot_ref, s32[1]{0:T(128)} %bitcast.1.first_ref, bf16[384,768]{1,0:T(8,128)(2,1)S(1)} %bitcast.14, bf16[24,40,768]{2,1,0:T(8,128)(2,1)S(1)} %get-tuple-element.8.refs_2_.refs_1_, bf16[12,40,768]{2,1,0:T(8,128)(2,1)} %collective-permute-done.1.refs_2_, ...), custom_call_target="tpu_custom_call" | custom-call | flops 94371840 | bytes 4194304 | tf_op jit(solution)/shard_map/synthesis/pallas_call | solution.py:289
  119.0 0.0 copy-start.1
  119.0 0.6 copy-done.1
  119.7 4.2 %all-to-all-start.3 = ((bf16[64,8,128]{2,1,0:T(8,128)(2,1)}), bf16[64,8,128]{2,1,0:T(8,128)(2,1)S(1)}, u32[]{:S(2)}, u32[]{:S(2)}) async-start(bf16[64,8,128]{2,1,0:T(8,128)(2,1)} %bitcast.15), calls=%async_computation.3 | async-start | bytes 262144 | tf_op jit(solution)/shard_map/all_to_all | solution.py:410
  123.9 0.0 copy-start.2
  123.9 0.9 copy-done.2
  124.8 0.0 copy-start.3
  124.8 0.9 copy-done.3
  125.7 0.2 tables.1.table_ref
  125.9 8.4 %all-to-all-done.3 = bf16[64,8,128]{2,1,0:T(8,128)(2,1)S(1)} async-done(((bf16[64,8,128]{2,1,0:T(8,128)(2,1)}), bf16[64,8,128]{2,1,0:T(8,128)(2,1)S(1)}, u32[]{:S(2)}, u32[]{:S(2)}) %all-to-all-start.3) | async-done | bytes 131104 | tf_op jit(solution)/shard_map/all_to_all | solution.py:410
  134.3 0.0 copy-start.6
  134.3 0.9 copy-done.6
  135.2 2.1 %inverse_dft.1 = f32[40,6144]{1,0:T(8,128)} custom-call(bf16[512,128]{1,0:T(8,128)(2,1)S(1)} %bitcast.17, bf16[2,256,768]{2,1,0:T(8,128)(2,1)S(1)} %tables.1.table_ref, f32[2,24,768]{2,1,0:T(8,128)S(1)} %copy-done.6), custom_call_target="tpu_custom_call" | custom-call | flops 754974720 | bytes 1048576 | tf_op jit(solution)/shard_map/inverse_dft/pallas_call | solution.py:367
  (1 shorter events, 0.0 us)
Async XLA Ops:
  0.1 1.8 %copy-start = (bf16[40,48,768]{2,1,0:T(8,128)(2,1)S(1)}, bf16[40,48,768]{2,1,0:T(8,128)(2,1)}, u32[]{:S(2)}) copy-start(bf16[40,48,768]{2,1,0:T(8,128)(2,1)} %legendre_ref.1) | copy-start | bytes 8847364
  3.9 0.9 copy-start.5
  4.8 25.0 %collective-permute-start = (bf16[24,40,768]{2,1,0:T(8,128)(2,1)}, bf16[24,40,768]{2,1,0:T(8,128)(2,1)S(1)}, u32[]{:S(2)}, u32[]{:S(2)}) collective-permute-start(bf16[24,40,768]{2,1,0:T(8,128)(2,1)} %get-tuple-element.9.half_ref), channel_id=1, source_target_pairs={{0,1},{1,0},{16,17},{17,16},{2,3},{3,2},{18,19},{19,18},{4,5},{5,4... | collective-permute-start | bytes 4423688 | tf_op jit(solution)/shard_map/ppermute | solution.py:402
  13.5 16.3 %copy-start.4 = (s32[16]{0:T(128)S(1)}, s32[16]{0:T(128)}, u32[]{:S(2)}) copy-start(s32[16]{0:T(128)} %refs_0_.1) | copy-start | bytes 196
  31.1 41.5 %copy-start.7 = (f32[768]{0:T(1024)S(1)}, f32[768]{0:T(1024)}, u32[]{:S(2)}) copy-start(f32[768]{0:T(1024)} %param.11) | copy-start | bytes 9220
  73.5 42.8 %all-to-all-start.2 = ((bf16[8,48,768]{2,1,0:T(8,128)(2,1)}), bf16[8,48,768]{2,1,0:T(8,128)(2,1)S(1)}, u32[]{:S(2)}, u32[]{:S(2)}) async-start(bf16[8,48,768]{2,1,0:T(8,128)(2,1)} %broadcast_in_dim.26), calls=%async_computation.2 | async-start | bytes 1179648 | tf_op jit(solution)/shard_map/all_to_all | solution.py:428
  78.6 19.7 %collective-permute-start.1 = (bf16[12,40,768]{2,1,0:T(8,128)(2,1)}, bf16[12,40,768]{2,1,0:T(8,128)(2,1)}, u32[]{:S(2)}, u32[]{:S(2)}) collective-permute-start(bf16[12,40,768]{2,1,0:T(8,128)(2,1)} %copy-done.5), channel_id=1, source_target_pairs={{0,16},{1,17},{16,0},{17,1},{2,18},{3,19},{18,2},{19,3},{4,20},{5,... | collective-permute-start | bytes 2211848 | tf_op jit(solution)/shard_map/ppermute | solution.py:402
  83.6 32.7 %collective-permute-start.2 = (bf16[12,40,768]{2,1,0:T(8,128)(2,1)}, bf16[12,40,768]{2,1,0:T(8,128)(2,1)}, u32[]{:S(2)}, u32[]{:S(2)}) collective-permute-start(bf16[12,40,768]{2,1,0:T(8,128)(2,1)} %shard_map.83), channel_id=1, source_target_pairs={{0,17},{1,16},{16,1},{17,0},{2,19},{3,18},{18,3},{19,2},{4,21},{5,... | collective-permute-start | bytes 2211848 | tf_op jit(solution)/shard_map/ppermute | solution.py:402
  119.0 0.7 copy-start.1
  119.7 14.6 %all-to-all-start.3 = ((bf16[64,8,128]{2,1,0:T(8,128)(2,1)}), bf16[64,8,128]{2,1,0:T(8,128)(2,1)S(1)}, u32[]{:S(2)}, u32[]{:S(2)}) async-start(bf16[64,8,128]{2,1,0:T(8,128)(2,1)} %bitcast.15), calls=%async_computation.3 | async-start | bytes 262144 | tf_op jit(solution)/shard_map/all_to_all | solution.py:410
  123.9 0.9 copy-start.2
  124.8 0.9 copy-start.3
  134.3 0.9 copy-start.6

commit v5 on v4

--- a/solution.py
+++ b/solution.py
@@ -159,14 +159,22 @@
     )(place, values)
 
 
-def table_kernel(coarse_ref, fine_ref, table_ref):
-    inner_table(coarse_ref, fine_ref, table_ref, slice(None))
-
-
-def inner_tables(coarse, fine):
-    shape = (2, INNER, coarse.shape[2])
-    return pl.pallas_call(
-        table_kernel,
+def table_kernel(which, coarse_ref, fine_ref, table_ref):
+    fine_cos, fine_sin = fine_ref[0], fine_ref[1]
+    for step in range(FINE):
+        coarse_cos = coarse_ref[0, step : step + 1, :]
+        coarse_sin = coarse_ref[1, step : step + 1, :]
+        if which == "cosine":
+            part = coarse_cos * fine_cos - coarse_sin * fine_sin
+        else:
+            part = -(coarse_sin * fine_cos + coarse_cos * fine_sin)
+        table_ref[step * FINE : (step + 1) * FINE, :] = part.astype(jnp.bfloat16)
+
+
+def table_of(which, coarse, fine):
+    shape = (INNER, coarse.shape[2])
+    return pl.pallas_call(
+        functools.partial(table_kernel, which),
         in_specs=[NEARBY] * 2,
         out_specs=NEARBY,
         out_shape=jax.ShapeDtypeStruct(shape, jnp.bfloat16),
@@ -174,7 +182,6 @@
             flops=1 << 20, bytes_accessed=2 * math.prod(shape), transcendentals=0
         ),
         compiler_params=pltpu.CompilerParams(vmem_limit_bytes=ROOM),
-        name="tables",
     )(coarse, fine)
 
 
@@ -309,7 +316,8 @@
 def inverse_kernel(
     peers,
     moved_ref,
-    table_ref,
+    cosine_ref,
+    sine_ref,
     turn_ref,
     out_ref,
     rows_ref,
@@ -343,9 +351,9 @@
             rows_ref[part % 2, 0, rows, :] = (first * cosine - second * sine).astype(jnp.bfloat16)
             rows_ref[part % 2, 1, rows, :] = (first * sine + second * cosine).astype(jnp.bfloat16)
         result = lax.dot_general(
-            rows_ref[part % 2, 0], table_ref[0], dims, preferred_element_type=jnp.float32
+            rows_ref[part % 2, 0], cosine_ref[...], dims, preferred_element_type=jnp.float32
         ) + lax.dot_general(
-            rows_ref[part % 2, 1], table_ref[1], dims, preferred_element_type=jnp.float32
+            rows_ref[part % 2, 1], sine_ref[...], dims, preferred_element_type=jnp.float32
         )
         for step in range(count):
             part_ref[part, :, step * INNER : (step + 1) * INNER] = result[
@@ -360,13 +368,13 @@
         copy.wait()
 
 
-def inverse(moved, table, turn, cycles, longitudes, peers):
+def inverse(moved, tables, turn, cycles, longitudes, peers):
     orders = turn.shape[2]
     count = 6
     parts = longitudes // INNER // count
     return pl.pallas_call(
         functools.partial(inverse_kernel, peers),
-        in_specs=[NEARBY] * 3,
+        in_specs=[NEARBY] * 4,
         out_specs=pl.BlockSpec(memory_space=pltpu.HBM),
         out_shape=jax.ShapeDtypeStruct((cycles, longitudes), jnp.float32),
         scratch_shapes=[
@@ -381,7 +389,7 @@
         ),
         compiler_params=pltpu.CompilerParams(vmem_limit_bytes=ROOM),
         name="inverse_dft",
-    )(moved, table, turn)
+    )(moved, *tables, turn)
 
 
 def local(elevation, legendre, cycle_weight, love_factor, assignment):
@@ -415,7 +423,7 @@
     own_side = swapped(own_part, 2)
     (sent_part,) = divided(part_kernel, place, sent, (share,), cycle_dev)
     met_side = swapped(sent_part, 3)
-    table = inner_tables(coarse, fine)
+    tables = [table_of(which, coarse, fine) for which in ("cosine", "sine")]
     lines = groups * orders_dev * 2 // (LANES // cycle_dev)
     packed = forward(elevation[0], cycle_weight[None, :], coarse, fine, turn, lines, groups * cores)
     moved = exchanged(packed, ("cons", CORE))
@@ -435,7 +443,7 @@
         lines,
     )
     returned = exchanged(synthesis, ("cons", *NEAR))
-    return inverse(returned, table, turn, cycle_dev, longitudes, groups * near)[None]
+    return inverse(returned, tables, turn, cycle_dev, longitudes, groups * near)[None]
 
 
 def solution(mesh):

time: 138 us -> 138 us (level)
  no operation moved by 1% of the time
where the time goes in v5:
time: 138 us; the launch traced here: 137 us
  blocking collectives  54.3 us (39%)
  waiting for transfers between devices  34.8 us (25%)
  starting transfers between devices  26.9 us (19%)
  Pallas kernels  14.1 us (10%)
  local copies, waits for them, and re-layouts  6.9 us (5%)
    all_to_all x1, blocking collectives, local(): lax.all_to_all(partial.reshape(far, rows, degrees), FAR, 0, 0, tiled=True)  41.3 us
    ppermute x3, waiting for transfers between devices, swapped(): return lax.ppermute(values, NEAR[::-1], pairs)  26.4 us
    ppermute x3, starting transfers between devices, swapped(): return lax.ppermute(values, NEAR[::-1], pairs)  17.7 us
    all_to_all x1, blocking collectives, exchanged(): tiles = lax.all_to_all(tiles, axes, 0, 0, tiled=True)  12.9 us
    all_to_all x1, waiting for transfers between devices, exchanged(): tiles = lax.all_to_all(tiles, axes, 0, 0, tiled=True)  8.36 us
    unnamed x16, local copies, waits for them, and re-layouts  6.05 us
    all_to_all x1, starting transfers between devices, local(): coefficients = lax.all_to_all(copies, DEEP, 0, 0, tiled=True)  5.06 us
    pallas_call x2, Pallas kernels, divided(): pl.pallas_call(kernel, in_specs=[SCALARS, NEARBY], out_specs=[NEARBY] * l...  4.32 us
  transfers between devices with their start and end apart: 5, of which 3 were waited for; matrix products, arithmetic and copies ran while one was open for 0% of the time, Pallas kernels for 4%

profile of v5, /device:TPU:1, one launch (start us, length us, event | category | flops | bytes accessed | tf_op | source)
XLA Modules:
  0.0 137.3 jit_solution(15338237490163988323)
XLA Ops:
  0.0 0.1 pad_add_fusion.place_ref
  0.1 0.0 copy-start
  0.1 1.8 %copy-done = bf16[40,48,768]{2,1,0:T(8,128)(2,1)S(1)} copy-done((bf16[40,48,768]{2,1,0:T(8,128)(2,1)S(1)}, bf16[40,48,768]{2,1,0:T(8,128)(2,1)}, u32[]{:S(2)}) %copy-start) | copy-done | bytes 2949144
  1.9 2.0 %shard_map.82 = (bf16[24,40,768]{2,1,0:T(8,128)(2,1)}, bf16[24,40,768]{2,1,0:T(8,128)(2,1)S(1)}, bf16[12,40,768]{2,1,0:T(8,128)(2,1)S(1)}) custom-call(s32[2]{0:T(128)S(1)} %pad_add_fusion.place_ref, bf16[40,48,768]{2,1,0:T(8,128)(2,1)S(1)} %copy-done), custom_call_target="tpu_custom_call" | custom-call | flops 1048576 | bytes 7372800 | tf_op jit(solution)/shard_map/pallas_call | solution.py:148
  3.9 0.0 copy-start.5
  3.9 0.9 copy-done.5
  4.8 8.7 %collective-permute-start = (bf16[24,40,768]{2,1,0:T(8,128)(2,1)}, bf16[24,40,768]{2,1,0:T(8,128)(2,1)S(1)}, u32[]{:S(2)}, u32[]{:S(2)}) collective-permute-start(bf16[24,40,768]{2,1,0:T(8,128)(2,1)} %get-tuple-element.9.half_ref), channel_id=1, source_target_pairs={{0,1},{1,0},{16,17},{17,16},{2,3},{3,2},{18,19},{19,18},{4,5},{5,4... | collective-permute-start | bytes 4423688 | tf_op jit(solution)/shard_map/ppermute | solution.py:410
  13.5 0.0 copy-start.4
  13.5 3.3 %forward_dft.1 = bf16[512,128]{1,0:T(8,128)(2,1)} custom-call(bf16[40,6144]{1,0:T(8,128)(2,1)} %bitcast.19, f32[1,40]{1,0:T(1,128)} %bitcast.20, f32[2,16,768]{2,1,0:T(8,128)} %constant.27.clone.coarse_ref, f32[2,16,768]{2,1,0:T(8,128)} %constant.28.clone.fine_ref, f32[2,24,768]{2,1,0:T(8,128)} %constant.29.clone.turn_ref), custom_call_target="tpu_custom_call" | custom-call | flops 754974720 | bytes 1048576 | tf_op jit(solution)/shard_map/forward_dft/pallas_call | solution.py:111
  16.9 12.9 %all_to_all.20 = bf16[32,16,128]{2,1,0:T(8,128)(2,1)S(1)} all-to-all(bf16[32,16,128]{2,1,0:T(8,128)(2,1)} %bitcast.18), channel_id=1, replica_groups=mesh['cons'=16,'blk_0'=2,'blk_1'=8,'blk_2'=2] {'cons','blk_2'}, dimensions={0} | all-to-all | bytes 262144 | tf_op jit(solution)/shard_map/all_to_all | solution.py:418
  29.8 0.0 collective-permute-done.refs_3_
  29.8 0.0 copy-done.4
  29.8 1.3 analysis.1
  31.1 0.0 copy-start.7
  31.1 41.3 %all_to_all.21 = bf16[16,48,768]{2,1,0:T(8,128)(2,1)S(1)} all-to-all(bf16[16,48,768]{2,1,0:T(8,128)(2,1)S(1)} %bitcast.13), channel_id=1, replica_groups=mesh['cons'=16,'blk_0'=2,'blk_1'=8,'blk_2'=2] {'blk_0','blk_1'}, dimensions={0} | all-to-all | bytes 2359296 | tf_op jit(solution)/shard_map/all_to_all | solution.py:432
  72.4 0.2 convert_reduce_fusion
  72.6 0.0 copy-done.7
  72.6 0.9 broadcast_in_dim.26
  73.5 5.1 %all-to-all-start.2 = ((bf16[8,48,768]{2,1,0:T(8,128)(2,1)}), bf16[8,48,768]{2,1,0:T(8,128)(2,1)S(1)}, u32[]{:S(2)}, u32[]{:S(2)}) async-start(bf16[8,48,768]{2,1,0:T(8,128)(2,1)} %broadcast_in_dim.26), calls=%async_computation.2 | async-start | bytes 1179648 | tf_op jit(solution)/shard_map/all_to_all | solution.py:436
  78.6 2.7 %collective-permute-start.1 = (bf16[12,40,768]{2,1,0:T(8,128)(2,1)}, bf16[12,40,768]{2,1,0:T(8,128)(2,1)}, u32[]{:S(2)}, u32[]{:S(2)}) collective-permute-start(bf16[12,40,768]{2,1,0:T(8,128)(2,1)} %copy-done.5), channel_id=1, source_target_pairs={{0,16},{1,17},{16,0},{17,1},{2,18},{3,19},{18,2},{19,3},{4,20},{5,... | collective-permute-start | bytes 2211848 | tf_op jit(solution)/shard_map/ppermute | solution.py:410
  81.3 2.3 %shard_map.83 = bf16[12,40,768]{2,1,0:T(8,128)(2,1)} custom-call(s32[2]{0:T(128)S(1)} %pad_add_fusion.place_ref, bf16[24,40,768]{2,1,0:T(8,128)(2,1)} %get-tuple-element.9.half_ref), custom_call_target="tpu_custom_call" | custom-call | flops 1048576 | bytes 1474560 | tf_op jit(solution)/shard_map/pallas_call | solution.py:148
  83.6 6.2 %collective-permute-start.2 = (bf16[12,40,768]{2,1,0:T(8,128)(2,1)}, bf16[12,40,768]{2,1,0:T(8,128)(2,1)}, u32[]{:S(2)}, u32[]{:S(2)}) collective-permute-start(bf16[12,40,768]{2,1,0:T(8,128)(2,1)} %shard_map.83), channel_id=1, source_target_pairs={{0,17},{1,16},{16,1},{17,0},{2,19},{3,18},{18,3},{19,2},{4,21},{5,... | collective-permute-start | bytes 2211848 | tf_op jit(solution)/shard_map/ppermute | solution.py:410
  89.8 8.5 %collective-permute-done.1.refs_2_ = bf16[12,40,768]{2,1,0:T(8,128)(2,1)} collective-permute-done((bf16[12,40,768]{2,1,0:T(8,128)(2,1)}, bf16[12,40,768]{2,1,0:T(8,128)(2,1)}, u32[]{:S(2)}, u32[]{:S(2)}) %collective-permute-start.1) | collective-permute-done | bytes 737312 | tf_op jit(solution)/shard_map/ppermute | solution.py:410
  98.3 18.0 %collective-permute-done.2.refs_4_ = bf16[12,40,768]{2,1,0:T(8,128)(2,1)} collective-permute-done((bf16[12,40,768]{2,1,0:T(8,128)(2,1)}, bf16[12,40,768]{2,1,0:T(8,128)(2,1)}, u32[]{:S(2)}, u32[]{:S(2)}) %collective-permute-start.2) | collective-permute-done | bytes 737312 | tf_op jit(solution)/shard_map/ppermute | solution.py:410
  116.3 0.0 all-to-all-done.2
  116.3 2.7 %synthesis.1 = bf16[512,128]{1,0:T(8,128)(2,1)S(1)} custom-call(s32[1]{0:T(128)} %bitcast.spot_ref, s32[1]{0:T(128)} %bitcast.1.first_ref, bf16[384,768]{1,0:T(8,128)(2,1)S(1)} %bitcast.14, bf16[24,40,768]{2,1,0:T(8,128)(2,1)S(1)} %get-tuple-element.8.refs_2_.refs_1_, bf16[12,40,768]{2,1,0:T(8,128)(2,1)} %collective-permute-done.1.refs_2_, ...), custom_call_target="tpu_custom_call" | custom-call | flops 94371840 | bytes 4194304 | tf_op jit(solution)/shard_map/synthesis/pallas_call | solution.py:296
  119.0 0.0 copy-start.1
  119.0 0.6 copy-done.1
  119.7 4.2 %all-to-all-start.3 = ((bf16[64,8,128]{2,1,0:T(8,128)(2,1)}), bf16[64,8,128]{2,1,0:T(8,128)(2,1)S(1)}, u32[]{:S(2)}, u32[]{:S(2)}) async-start(bf16[64,8,128]{2,1,0:T(8,128)(2,1)} %bitcast.15), calls=%async_computation.3 | async-start | bytes 262144 | tf_op jit(solution)/shard_map/all_to_all | solution.py:418
  123.9 0.0 copy-start.2
  123.9 0.9 copy-done.2
  124.8 0.0 copy-start.3
  124.8 0.9 copy-done.3
  125.7 0.1 shard_map.84.cosine_ref
  125.8 0.2 shard_map.85.sine_ref
  126.0 8.4 %all-to-all-done.3 = bf16[64,8,128]{2,1,0:T(8,128)(2,1)S(1)} async-done(((bf16[64,8,128]{2,1,0:T(8,128)(2,1)}), bf16[64,8,128]{2,1,0:T(8,128)(2,1)S(1)}, u32[]{:S(2)}, u32[]{:S(2)}) %all-to-all-start.3) | async-done | bytes 131104 | tf_op jit(solution)/shard_map/all_to_all | solution.py:418
  134.3 0.0 copy-start.6
  134.3 0.9 copy-done.6
  135.2 2.1 %inverse_dft.1 = f32[40,6144]{1,0:T(8,128)} custom-call(bf16[512,128]{1,0:T(8,128)(2,1)S(1)} %bitcast.17, bf16[256,768]{1,0:T(8,128)(2,1)S(1)} %shard_map.84.cosine_ref, bf16[256,768]{1,0:T(8,128)(2,1)S(1)} %shard_map.85.sine_ref, f32[2,24,768]{2,1,0:T(8,128)S(1)} %copy-done.6), custom_call_target="tpu_custom_call" | custom-call | flops 754974720 | bytes 1048576 | tf_op jit(solution)/shard_map/inverse_dft/pallas_call | solution.py:375
  (1 shorter events, 0.0 us)
Async XLA Ops:
  0.1 1.8 %copy-start = (bf16[40,48,768]{2,1,0:T(8,128)(2,1)S(1)}, bf16[40,48,768]{2,1,0:T(8,128)(2,1)}, u32[]{:S(2)}) copy-start(bf16[40,48,768]{2,1,0:T(8,128)(2,1)} %legendre_ref.1) | copy-start | bytes 8847364
  3.9 0.9 copy-start.5
  4.8 25.0 %collective-permute-start = (bf16[24,40,768]{2,1,0:T(8,128)(2,1)}, bf16[24,40,768]{2,1,0:T(8,128)(2,1)S(1)}, u32[]{:S(2)}, u32[]{:S(2)}) collective-permute-start(bf16[24,40,768]{2,1,0:T(8,128)(2,1)} %get-tuple-element.9.half_ref), channel_id=1, source_target_pairs={{0,1},{1,0},{16,17},{17,16},{2,3},{3,2},{18,19},{19,18},{4,5},{5,4... | collective-permute-start | bytes 4423688 | tf_op jit(solution)/shard_map/ppermute | solution.py:410
  13.5 16.3 %copy-start.4 = (s32[16]{0:T(128)S(1)}, s32[16]{0:T(128)}, u32[]{:S(2)}) copy-start(s32[16]{0:T(128)} %refs_0_.1) | copy-start | bytes 196
  31.1 41.5 %copy-start.7 = (f32[768]{0:T(1024)S(1)}, f32[768]{0:T(1024)}, u32[]{:S(2)}) copy-start(f32[768]{0:T(1024)} %param.11) | copy-start | bytes 9220
  73.5 42.8 %all-to-all-start.2 = ((bf16[8,48,768]{2,1,0:T(8,128)(2,1)}), bf16[8,48,768]{2,1,0:T(8,128)(2,1)S(1)}, u32[]{:S(2)}, u32[]{:S(2)}) async-start(bf16[8,48,768]{2,1,0:T(8,128)(2,1)} %broadcast_in_dim.26), calls=%async_computation.2 | async-start | bytes 1179648 | tf_op jit(solution)/shard_map/all_to_all | solution.py:436
  78.6 19.7 %collective-permute-start.1 = (bf16[12,40,768]{2,1,0:T(8,128)(2,1)}, bf16[12,40,768]{2,1,0:T(8,128)(2,1)}, u32[]{:S(2)}, u32[]{:S(2)}) collective-permute-start(bf16[12,40,768]{2,1,0:T(8,128)(2,1)} %copy-done.5), channel_id=1, source_target_pairs={{0,16},{1,17},{16,0},{17,1},{2,18},{3,19},{18,2},{19,3},{4,20},{5,... | collective-permute-start | bytes 2211848 | tf_op jit(solution)/shard_map/ppermute | solution.py:410
  83.6 32.7 %collective-permute-start.2 = (bf16[12,40,768]{2,1,0:T(8,128)(2,1)}, bf16[12,40,768]{2,1,0:T(8,128)(2,1)}, u32[]{:S(2)}, u32[]{:S(2)}) collective-permute-start(bf16[12,40,768]{2,1,0:T(8,128)(2,1)} %shard_map.83), channel_id=1, source_target_pairs={{0,17},{1,16},{16,1},{17,0},{2,19},{3,18},{18,3},{19,2},{4,21},{5,... | collective-permute-start | bytes 2211848 | tf_op jit(solution)/shard_map/ppermute | solution.py:410
  119.0 0.7 copy-start.1
  119.7 14.6 %all-to-all-start.3 = ((bf16[64,8,128]{2,1,0:T(8,128)(2,1)}), bf16[64,8,128]{2,1,0:T(8,128)(2,1)S(1)}, u32[]{:S(2)}, u32[]{:S(2)}) async-start(bf16[64,8,128]{2,1,0:T(8,128)(2,1)} %bitcast.15), calls=%async_computation.3 | async-start | bytes 262144 | tf_op jit(solution)/shard_map/all_to_all | solution.py:418
  123.9 0.9 copy-start.2
  124.8 0.9 copy-start.3
  134.3 0.9 copy-start.6

commit v6 on v5

--- a/solution.py
+++ b/solution.py
@@ -126,16 +126,15 @@
     )(elevation, weight, coarse, fine, turn)
 
 
-def split_kernel(place_ref, legendre_ref, sent_ref, own_ref, part_ref):
-    core, side = place_ref[0], place_ref[1]
-    orders, share = own_ref.shape[0], part_ref.shape[0]
+def split_kernel(place_ref, legendre_ref, sent_ref, own_ref):
+    core = place_ref[0]
+    orders = own_ref.shape[0]
     for target, index in ((sent_ref, 1 - core), (own_ref, core)):
         for first in range(0, orders, TILE):
             start = pl.multiple_of(index * orders + first, TILE)
             target[first : first + TILE] = jnp.swapaxes(
                 legendre_ref[:, pl.ds(start, TILE), :], 0, 1
             )
-    part_ref[...] = own_ref[pl.ds((1 - side) * share, share)]
 
 
 def part_kernel(place_ref, half_ref, part_ref):
@@ -418,11 +417,14 @@
         tiles = lax.all_to_all(tiles, axes, 0, 0, tiled=True)
         return tiles.reshape(-1, LANES)
 
-    sent, own, own_part = divided(split_kernel, place, legendre, (half, half, share), cycle_dev)
+    sent, own = divided(split_kernel, place, legendre, (half, half), cycle_dev)
+
+    def part_of(values):
+        return divided(part_kernel, place, values, (share,), cycle_dev)[0]
+
     met = swapped(sent, 1)
-    own_side = swapped(own_part, 2)
-    (sent_part,) = divided(part_kernel, place, sent, (share,), cycle_dev)
-    met_side = swapped(sent_part, 3)
+    own_side = swapped(part_of(own), 2)
+    met_side = swapped(part_of(sent), 3)
     tables = [table_of(which, coarse, fine) for which in ("cosine", "sine")]
     lines = groups * orders_dev * 2 // (LANES // cycle_dev)
     packed = forward(elevation[0], cycle_weight[None, :], coarse, fine, turn, lines, groups * cores)

time: 138 us -> 139 us (level)
  Pallas kernels: 14.1 us -> 15.6 us
    pallas_call x2 -> x3, Pallas kernels: 4.32 us -> 5.86 us  [divided(): pl.pallas_call(kernel, in_specs=[SCALARS, NEARBY], out_specs=[NEARBY] * l...]
    unnamed x16 -> x14, local copies, waits for them, and re-layouts: 6.05 us -> 5.19 us
  transfers between devices with their start and end apart: 5 -> 5, of which waited for: 3 -> 3; matrix products, arithmetic and copies ran while one was open for 0% -> 0% of each run, Pallas kernels for 4% -> 5%
where the time goes in v6:
time: 139 us; the launch traced here: 138 us
  blocking collectives  54.3 us (39%)
  waiting for transfers between devices  34.8 us (25%)
  starting transfers between devices  26.9 us (19%)
  Pallas kernels  15.6 us (11%)
  local copies, waits for them, and re-layouts  6.03 us (4%)
    all_to_all x1, blocking collectives, local(): lax.all_to_all(partial.reshape(far, rows, degrees), FAR, 0, 0, tiled=True)  41.3 us
    ppermute x3, waiting for transfers between devices, swapped(): return lax.ppermute(values, NEAR[::-1], pairs)  26.5 us
    ppermute x3, starting transfers between devices, swapped(): return lax.ppermute(values, NEAR[::-1], pairs)  17.7 us
    all_to_all x1, blocking collectives, exchanged(): tiles = lax.all_to_all(tiles, axes, 0, 0, tiled=True)  12.9 us
    all_to_all x1, waiting for transfers between devices, exchanged(): tiles = lax.all_to_all(tiles, axes, 0, 0, tiled=True)  8.35 us
    pallas_call x3, Pallas kernels, divided(): pl.pallas_call(kernel, in_specs=[SCALARS, NEARBY], out_specs=[NEARBY] * l...  5.86 us
    unnamed x14, local copies, waits for them, and re-layouts  5.19 us
    all_to_all x1, starting transfers between devices, local(): coefficients = lax.all_to_all(copies, DEEP, 0, 0, tiled=True)  5.06 us
  transfers between devices with their start and end apart: 5, of which 3 were waited for; matrix products, arithmetic and copies ran while one was open for 0% of the time, Pallas kernels for 5%

profile of v6, /device:TPU:1, one launch (start us, length us, event | category | flops | bytes accessed | tf_op | source)
XLA Modules:
  0.0 138.0 jit_solution(14193932021673319321)
XLA Ops:
  0.0 0.1 pad_add_fusion.place_ref
  0.1 0.0 copy-start
  0.1 1.8 %copy-done = bf16[40,48,768]{2,1,0:T(8,128)(2,1)S(1)} copy-done((bf16[40,48,768]{2,1,0:T(8,128)(2,1)S(1)}, bf16[40,48,768]{2,1,0:T(8,128)(2,1)}, u32[]{:S(2)}) %copy-start) | copy-done | bytes 2949144
  1.9 2.1 %shard_map.82 = (bf16[24,40,768]{2,1,0:T(8,128)(2,1)}, bf16[24,40,768]{2,1,0:T(8,128)(2,1)S(1)}) custom-call(s32[2]{0:T(128)S(1)} %pad_add_fusion.place_ref, bf16[40,48,768]{2,1,0:T(8,128)(2,1)S(1)} %copy-done), custom_call_target="tpu_custom_call" | custom-call | flops 1048576 | bytes 5898240 | tf_op jit(solution)/shard_map/pallas_call | solution.py:147
  4.0 8.7 %collective-permute-start = (bf16[24,40,768]{2,1,0:T(8,128)(2,1)}, bf16[24,40,768]{2,1,0:T(8,128)(2,1)S(1)}, u32[]{:S(2)}, u32[]{:S(2)}) collective-permute-start(bf16[24,40,768]{2,1,0:T(8,128)(2,1)} %get-tuple-element.8.half_ref), channel_id=1, source_target_pairs={{0,1},{1,0},{16,17},{17,16},{2,3},{3,2},{18,19},{19,18},{4,5},{5,4... | collective-permute-start | bytes 4423688 | tf_op jit(solution)/shard_map/ppermute | solution.py:409
  12.7 0.0 copy-start.4
  12.8 3.3 %forward_dft.1 = bf16[512,128]{1,0:T(8,128)(2,1)} custom-call(bf16[40,6144]{1,0:T(8,128)(2,1)} %bitcast.19, f32[1,40]{1,0:T(1,128)} %bitcast.20, f32[2,16,768]{2,1,0:T(8,128)} %constant.27.clone.coarse_ref, f32[2,16,768]{2,1,0:T(8,128)} %constant.28.clone.fine_ref, f32[2,24,768]{2,1,0:T(8,128)} %constant.29.clone.turn_ref), custom_call_target="tpu_custom_call" | custom-call | flops 754974720 | bytes 1048576 | tf_op jit(solution)/shard_map/forward_dft/pallas_call | solution.py:111
  16.1 12.9 %all_to_all.20 = bf16[32,16,128]{2,1,0:T(8,128)(2,1)S(1)} all-to-all(bf16[32,16,128]{2,1,0:T(8,128)(2,1)} %bitcast.18), channel_id=1, replica_groups=mesh['cons'=16,'blk_0'=2,'blk_1'=8,'blk_2'=2] {'cons','blk_2'}, dimensions={0} | all-to-all | bytes 262144 | tf_op jit(solution)/shard_map/all_to_all | solution.py:417
  29.0 0.0 collective-permute-done.refs_3_
  29.0 0.0 copy-done.4
  29.0 1.3 analysis.1
  30.3 0.0 copy-start.6
  30.4 41.3 %all_to_all.21 = bf16[16,48,768]{2,1,0:T(8,128)(2,1)S(1)} all-to-all(bf16[16,48,768]{2,1,0:T(8,128)(2,1)S(1)} %bitcast.13), channel_id=1, replica_groups=mesh['cons'=16,'blk_0'=2,'blk_1'=8,'blk_2'=2] {'blk_0','blk_1'}, dimensions={0} | all-to-all | bytes 2359296 | tf_op jit(solution)/shard_map/all_to_all | solution.py:434
  71.7 0.2 convert_reduce_fusion
  71.8 0.0 copy-done.6
  71.9 0.8 broadcast_in_dim.26
  72.7 5.1 %all-to-all-start.2 = ((bf16[8,48,768]{2,1,0:T(8,128)(2,1)}), bf16[8,48,768]{2,1,0:T(8,128)(2,1)S(1)}, u32[]{:S(2)}, u32[]{:S(2)}) async-start(bf16[8,48,768]{2,1,0:T(8,128)(2,1)} %broadcast_in_dim.26), calls=%async_computation.2 | async-start | bytes 1179648 | tf_op jit(solution)/shard_map/all_to_all | solution.py:438
  77.8 1.5 %shard_map.83 = bf16[12,40,768]{2,1,0:T(8,128)(2,1)} custom-call(s32[2]{0:T(128)S(1)} %pad_add_fusion.place_ref, bf16[24,40,768]{2,1,0:T(8,128)(2,1)S(1)} %get-tuple-element.7.refs_2_.half_ref.refs_1_), custom_call_target="tpu_custom_call" | custom-call | flops 1048576 | bytes 1474560 | tf_op jit(solution)/shard_map/pallas_call | solution.py:147
  79.2 2.7 %collective-permute-start.1 = (bf16[12,40,768]{2,1,0:T(8,128)(2,1)}, bf16[12,40,768]{2,1,0:T(8,128)(2,1)}, u32[]{:S(2)}, u32[]{:S(2)}) collective-permute-start(bf16[12,40,768]{2,1,0:T(8,128)(2,1)} %shard_map.83), channel_id=1, source_target_pairs={{0,16},{1,17},{16,0},{17,1},{2,18},{3,19},{18,2},{19,3},{4,20},{5,... | collective-permute-start | bytes 2211848 | tf_op jit(solution)/shard_map/ppermute | solution.py:409
  82.0 2.3 %shard_map.84 = bf16[12,40,768]{2,1,0:T(8,128)(2,1)} custom-call(s32[2]{0:T(128)S(1)} %pad_add_fusion.place_ref, bf16[24,40,768]{2,1,0:T(8,128)(2,1)} %get-tuple-element.8.half_ref), custom_call_target="tpu_custom_call" | custom-call | flops 1048576 | bytes 1474560 | tf_op jit(solution)/shard_map/pallas_call | solution.py:147
  84.3 6.2 %collective-permute-start.2 = (bf16[12,40,768]{2,1,0:T(8,128)(2,1)}, bf16[12,40,768]{2,1,0:T(8,128)(2,1)}, u32[]{:S(2)}, u32[]{:S(2)}) collective-permute-start(bf16[12,40,768]{2,1,0:T(8,128)(2,1)} %shard_map.84), channel_id=1, source_target_pairs={{0,17},{1,16},{16,1},{17,0},{2,19},{3,18},{18,3},{19,2},{4,21},{5,... | collective-permute-start | bytes 2211848 | tf_op jit(solution)/shard_map/ppermute | solution.py:409
  90.5 8.5 %collective-permute-done.1.refs_2_ = bf16[12,40,768]{2,1,0:T(8,128)(2,1)} collective-permute-done((bf16[12,40,768]{2,1,0:T(8,128)(2,1)}, bf16[12,40,768]{2,1,0:T(8,128)(2,1)}, u32[]{:S(2)}, u32[]{:S(2)}) %collective-permute-start.1) | collective-permute-done | bytes 737312 | tf_op jit(solution)/shard_map/ppermute | solution.py:409
  99.0 18.0 %collective-permute-done.2.refs_4_ = bf16[12,40,768]{2,1,0:T(8,128)(2,1)} collective-permute-done((bf16[12,40,768]{2,1,0:T(8,128)(2,1)}, bf16[12,40,768]{2,1,0:T(8,128)(2,1)}, u32[]{:S(2)}, u32[]{:S(2)}) %collective-permute-start.2) | collective-permute-done | bytes 737312 | tf_op jit(solution)/shard_map/ppermute | solution.py:409
  116.9 0.0 all-to-all-done.2
  116.9 2.7 %synthesis.1 = bf16[512,128]{1,0:T(8,128)(2,1)S(1)} custom-call(s32[1]{0:T(128)} %bitcast.spot_ref, s32[1]{0:T(128)} %bitcast.1.first_ref, bf16[384,768]{1,0:T(8,128)(2,1)S(1)} %bitcast.14, bf16[24,40,768]{2,1,0:T(8,128)(2,1)S(1)} %get-tuple-element.7.refs_2_.half_ref.refs_1_, bf16[12,40,768]{2,1,0:T(8,128)(2,1)} %collective-permute-done.1.refs_2_, ...), custom_call_target="tpu_custom_call" | custom-call | flops 94371840 | bytes 4194304 | tf_op jit(solution)/shard_map/synthesis/pallas_call | solution.py:295
  119.7 0.0 copy-start.1
  119.7 0.6 copy-done.1
  120.4 4.2 %all-to-all-start.3 = ((bf16[64,8,128]{2,1,0:T(8,128)(2,1)}), bf16[64,8,128]{2,1,0:T(8,128)(2,1)S(1)}, u32[]{:S(2)}, u32[]{:S(2)}) async-start(bf16[64,8,128]{2,1,0:T(8,128)(2,1)} %bitcast.15), calls=%async_computation.3 | async-start | bytes 262144 | tf_op jit(solution)/shard_map/all_to_all | solution.py:417
  124.6 0.0 copy-start.2
  124.6 0.9 copy-done.2
  125.4 0.0 copy-start.3
  125.5 0.9 copy-done.3
  126.3 0.1 shard_map.85.cosine_ref
  126.5 0.2 shard_map.86.sine_ref
  126.6 8.4 %all-to-all-done.3 = bf16[64,8,128]{2,1,0:T(8,128)(2,1)S(1)} async-done(((bf16[64,8,128]{2,1,0:T(8,128)(2,1)}), bf16[64,8,128]{2,1,0:T(8,128)(2,1)S(1)}, u32[]{:S(2)}, u32[]{:S(2)}) %all-to-all-start.3) | async-done | bytes 131104 | tf_op jit(solution)/shard_map/all_to_all | solution.py:417
  135.0 0.0 copy-start.5
  135.0 0.9 copy-done.5
  135.9 2.1 %inverse_dft.1 = f32[40,6144]{1,0:T(8,128)} custom-call(bf16[512,128]{1,0:T(8,128)(2,1)S(1)} %bitcast.17, bf16[256,768]{1,0:T(8,128)(2,1)S(1)} %shard_map.85.cosine_ref, bf16[256,768]{1,0:T(8,128)(2,1)S(1)} %shard_map.86.sine_ref, f32[2,24,768]{2,1,0:T(8,128)S(1)} %copy-done.5), custom_call_target="tpu_custom_call" | custom-call | flops 754974720 | bytes 1048576 | tf_op jit(solution)/shard_map/inverse_dft/pallas_call | solution.py:374
  (1 shorter events, 0.0 us)
Async XLA Ops:
  0.1 1.8 %copy-start = (bf16[40,48,768]{2,1,0:T(8,128)(2,1)S(1)}, bf16[40,48,768]{2,1,0:T(8,128)(2,1)}, u32[]{:S(2)}) copy-start(bf16[40,48,768]{2,1,0:T(8,128)(2,1)} %legendre_ref.1) | copy-start | bytes 8847364
  4.0 25.0 %collective-permute-start = (bf16[24,40,768]{2,1,0:T(8,128)(2,1)}, bf16[24,40,768]{2,1,0:T(8,128)(2,1)S(1)}, u32[]{:S(2)}, u32[]{:S(2)}) collective-permute-start(bf16[24,40,768]{2,1,0:T(8,128)(2,1)} %get-tuple-element.8.half_ref), channel_id=1, source_target_pairs={{0,1},{1,0},{16,17},{17,16},{2,3},{3,2},{18,19},{19,18},{4,5},{5,4... | collective-permute-start | bytes 4423688 | tf_op jit(solution)/shard_map/ppermute | solution.py:409
  12.7 16.3 %copy-start.4 = (s32[16]{0:T(128)S(1)}, s32[16]{0:T(128)}, u32[]{:S(2)}) copy-start(s32[16]{0:T(128)} %refs_0_.1) | copy-start | bytes 196
  30.3 41.5 %copy-start.6 = (f32[768]{0:T(1024)S(1)}, f32[768]{0:T(1024)}, u32[]{:S(2)}) copy-start(f32[768]{0:T(1024)} %param.11) | copy-start | bytes 9220
  72.7 44.2 %all-to-all-start.2 = ((bf16[8,48,768]{2,1,0:T(8,128)(2,1)}), bf16[8,48,768]{2,1,0:T(8,128)(2,1)S(1)}, u32[]{:S(2)}, u32[]{:S(2)}) async-start(bf16[8,48,768]{2,1,0:T(8,128)(2,1)} %broadcast_in_dim.26), calls=%async_computation.2 | async-start | bytes 1179648 | tf_op jit(solution)/shard_map/all_to_all | solution.py:438
  79.2 19.8 %collective-permute-start.1 = (bf16[12,40,768]{2,1,0:T(8,128)(2,1)}, bf16[12,40,768]{2,1,0:T(8,128)(2,1)}, u32[]{:S(2)}, u32[]{:S(2)}) collective-permute-start(bf16[12,40,768]{2,1,0:T(8,128)(2,1)} %shard_map.83), channel_id=1, source_target_pairs={{0,16},{1,17},{16,0},{17,1},{2,18},{3,19},{18,2},{19,3},{4,20},{5,... | collective-permute-start | bytes 2211848 | tf_op jit(solution)/shard_map/ppermute | solution.py:409
  84.3 32.7 %collective-permute-start.2 = (bf16[12,40,768]{2,1,0:T(8,128)(2,1)}, bf16[12,40,768]{2,1,0:T(8,128)(2,1)}, u32[]{:S(2)}, u32[]{:S(2)}) collective-permute-start(bf16[12,40,768]{2,1,0:T(8,128)(2,1)} %shard_map.84), channel_id=1, source_target_pairs={{0,17},{1,16},{16,1},{17,0},{2,19},{3,18},{18,3},{19,2},{4,21},{5,... | collective-permute-start | bytes 2211848 | tf_op jit(solution)/shard_map/ppermute | solution.py:409
  119.7 0.7 copy-start.1
  120.4 14.6 %all-to-all-start.3 = ((bf16[64,8,128]{2,1,0:T(8,128)(2,1)}), bf16[64,8,128]{2,1,0:T(8,128)(2,1)S(1)}, u32[]{:S(2)}, u32[]{:S(2)}) async-start(bf16[64,8,128]{2,1,0:T(8,128)(2,1)} %bitcast.15), calls=%async_computation.3 | async-start | bytes 262144 | tf_op jit(solution)/shard_map/all_to_all | solution.py:417
  124.6 0.9 copy-start.2
  125.4 0.9 copy-start.3
  135.0 0.9 copy-start.5

commit v7 on v6

--- a/solution.py
+++ b/solution.py
@@ -126,20 +126,14 @@
     )(elevation, weight, coarse, fine, turn)
 
 
-def split_kernel(place_ref, legendre_ref, sent_ref, own_ref):
-    core = place_ref[0]
-    orders = own_ref.shape[0]
-    for target, index in ((sent_ref, 1 - core), (own_ref, core)):
-        for first in range(0, orders, TILE):
-            start = pl.multiple_of(index * orders + first, TILE)
-            target[first : first + TILE] = jnp.swapaxes(
-                legendre_ref[:, pl.ds(start, TILE), :], 0, 1
-            )
-
-
-def part_kernel(place_ref, half_ref, part_ref):
-    share = part_ref.shape[0]
-    part_ref[...] = half_ref[pl.ds((1 - place_ref[1]) * share, share)]
+def split_kernel(flip, place_ref, legendre_ref, half_ref):
+    orders = half_ref.shape[0]
+    index = jnp.bitwise_xor(place_ref[0], flip)
+    for first in range(0, orders, TILE):
+        start = pl.multiple_of(index * orders + first, TILE)
+        half_ref[first : first + TILE] = jnp.swapaxes(
+            legendre_ref[:, pl.ds(start, TILE), :], 0, 1
+        )
 
 
 def divided(kernel, place, values, orders, cycles):
@@ -417,10 +411,14 @@
         tiles = lax.all_to_all(tiles, axes, 0, 0, tiled=True)
         return tiles.reshape(-1, LANES)
 
-    sent, own = divided(split_kernel, place, legendre, (half, half), cycle_dev)
+    def half_of(flip):
+        kernel = functools.partial(split_kernel, flip)
+        return divided(kernel, place, legendre, (half,), cycle_dev)[0]
+
+    sent, own = half_of(1), half_of(0)
 
     def part_of(values):
-        return divided(part_kernel, place, values, (share,), cycle_dev)[0]
+        return lax.dynamic_slice_in_dim(values, (1 - side) * share, share, 0)
 
     met = swapped(sent, 1)
     own_side = swapped(part_of(own), 2)

time: 139 us -> 138 us (level)
  blocking collectives: 54.3 us -> 41.3 us
  waiting for transfers between devices: 34.8 us -> 41.6 us
  local copies, waits for them, and re-layouts: 6.03 us -> 10.8 us
  starting transfers between devices: 26.9 us -> 30.6 us
  Pallas kernels: 15.6 us -> 12.7 us
    all_to_all x1 -> x0, blocking collectives: 12.9 us -> none  [exchanged(): tiles = lax.all_to_all(tiles, axes, 0, 0, tiled=True)]
    all_to_all x1 -> x2, waiting for transfers between devices: 8.35 us -> 14.9 us  [exchanged(): tiles = lax.all_to_all(tiles, axes, 0, 0, tiled=True)]
    all_to_all x1 -> x2, starting transfers between devices: 4.19 us -> 7.83 us  [exchanged(): tiles = lax.all_to_all(tiles, axes, 0, 0, tiled=True)]
    dynamic_slice x0 -> x2, local copies, waits for them, and re-layouts: none -> 2.95 us  [part_of(): return lax.dynamic_slice_in_dim(values, (1 - side) * share, share, 0)]
    pallas_call x3 -> x2, Pallas kernels: 5.86 us -> 2.94 us  [divided(): pl.pallas_call(kernel, in_specs=[SCALARS, NEARBY], out_specs=[NEARBY] * l...]
    unnamed x14 -> x16, local copies, waits for them, and re-layouts: 5.19 us -> 7.01 us
  transfers between devices with their start and end apart: 5 -> 6, of which waited for: 3 -> 4; matrix products, arithmetic and copies ran while one was open for 0% -> 2% of each run, Pallas kernels for 5% -> 3%
where the time goes in v7:
time: 138 us; the launch traced here: 137 us
  waiting for transfers between devices  41.6 us (30%)
  blocking collectives  41.3 us (30%)
  starting transfers between devices  30.6 us (22%)
  Pallas kernels  12.7 us (9%)
  local copies, waits for them, and re-layouts  10.8 us (8%)
    all_to_all x1, blocking collectives, local(): lax.all_to_all(partial.reshape(far, rows, degrees), FAR, 0, 0, tiled=True)  41.3 us
    ppermute x3, waiting for transfers between devices, swapped(): return lax.ppermute(values, NEAR[::-1], pairs)  26.7 us
    ppermute x3, starting transfers between devices, swapped(): return lax.ppermute(values, NEAR[::-1], pairs)  17.7 us
    all_to_all x2, waiting for transfers between devices, exchanged(): tiles = lax.all_to_all(tiles, axes, 0, 0, tiled=True)  14.9 us
    all_to_all x2, starting transfers between devices, exchanged(): tiles = lax.all_to_all(tiles, axes, 0, 0, tiled=True)  7.83 us
    unnamed x16, local copies, waits for them, and re-layouts  7.01 us
    all_to_all x1, starting transfers between devices, local(): coefficients = lax.all_to_all(copies, DEEP, 0, 0, tiled=True)  5.06 us
    pallas_call x1, Pallas kernels, forward(): pl.pallas_call(functools.partial(forward_kernel, peers), in_specs=[NEARBY...  3.34 us
  transfers between devices with their start and end apart: 6, of which 4 were waited for; matrix products, arithmetic and copies ran while one was open for 2% of the time, Pallas kernels for 3%

profile of v7, /device:TPU:1, one launch (start us, length us, event | category | flops | bytes accessed | tf_op | source)
XLA Modules:
  0.0 137.4 jit_solution(12140433922163530400)
XLA Ops:
  0.0 0.1 pad_add_fusion.place_ref
  0.1 0.0 copy-start
  0.1 1.8 %copy-done = bf16[40,48,768]{2,1,0:T(8,128)(2,1)S(1)} copy-done((bf16[40,48,768]{2,1,0:T(8,128)(2,1)S(1)}, bf16[40,48,768]{2,1,0:T(8,128)(2,1)}, u32[]{:S(2)}) %copy-start) | copy-done | bytes 2949144
  1.9 2.0 %shard_map.83 = bf16[24,40,768]{2,1,0:T(8,128)(2,1)} custom-call(s32[2]{0:T(128)S(1)} %pad_add_fusion.place_ref, bf16[40,48,768]{2,1,0:T(8,128)(2,1)S(1)} %copy-done), custom_call_target="tpu_custom_call" | custom-call | flops 1048576 | bytes 2949120 | tf_op jit(solution)/shard_map/pallas_call | solution.py:141
  3.9 8.7 %collective-permute-start = (bf16[24,40,768]{2,1,0:T(8,128)(2,1)}, bf16[24,40,768]{2,1,0:T(8,128)(2,1)S(1)}, u32[]{:S(2)}, u32[]{:S(2)}) collective-permute-start(bf16[24,40,768]{2,1,0:T(8,128)(2,1)} %shard_map.83), channel_id=1, source_target_pairs={{0,1},{1,0},{16,17},{17,16},{2,3},{3,2},{18,19},{19,18},{4,5},{5,4... | collective-permute-start | bytes 4423688 | tf_op jit(solution)/shard_map/ppermute | solution.py:403
  12.7 3.3 %forward_dft.1 = bf16[512,128]{1,0:T(8,128)(2,1)} custom-call(bf16[40,6144]{1,0:T(8,128)(2,1)} %bitcast.19, f32[1,40]{1,0:T(1,128)} %bitcast.20, f32[2,16,768]{2,1,0:T(8,128)} %constant.33.clone.coarse_ref, f32[2,16,768]{2,1,0:T(8,128)} %constant.34.clone.fine_ref, f32[2,24,768]{2,1,0:T(8,128)} %constant.35.clone.turn_ref), custom_call_target="tpu_custom_call" | custom-call | flops 754974720 | bytes 1048576 | tf_op jit(solution)/shard_map/forward_dft/pallas_call | solution.py:111
  16.0 3.6 %all-to-all-start = ((bf16[32,16,128]{2,1,0:T(8,128)(2,1)}), bf16[32,16,128]{2,1,0:T(8,128)(2,1)S(1)}, u32[]{:S(2)}, u32[]{:S(2)}) async-start(bf16[32,16,128]{2,1,0:T(8,128)(2,1)} %bitcast.18), calls=%async_computation | async-start | bytes 262144 | tf_op jit(solution)/shard_map/all_to_all | solution.py:411
  19.7 0.0 copy-start.1
  19.7 1.8 %copy-done.1 = bf16[40,48,768]{2,1,0:T(8,128)(2,1)S(1)} copy-done((bf16[40,48,768]{2,1,0:T(8,128)(2,1)S(1)}, bf16[40,48,768]{2,1,0:T(8,128)(2,1)}, u32[]{:S(2)}) %copy-start.1) | copy-done | bytes 2949144
  21.5 0.0 copy-start.5
  21.5 0.9 shard_map.82.refs_2_.refs_1_
  22.4 6.5 %all-to-all-done = bf16[32,16,128]{2,1,0:T(8,128)(2,1)S(1)} async-done(((bf16[32,16,128]{2,1,0:T(8,128)(2,1)}), bf16[32,16,128]{2,1,0:T(8,128)(2,1)S(1)}, u32[]{:S(2)}, u32[]{:S(2)}) %all-to-all-start) | async-done | bytes 131104 | tf_op jit(solution)/shard_map/all_to_all | solution.py:411
  29.0 0.0 collective-permute-done.refs_3_
  29.0 0.0 copy-done.5
  29.0 1.3 analysis.1
  30.3 0.0 copy-start.7
  30.3 41.3 %all_to_all.20 = bf16[16,48,768]{2,1,0:T(8,128)(2,1)S(1)} all-to-all(bf16[16,48,768]{2,1,0:T(8,128)(2,1)S(1)} %bitcast.13), channel_id=1, replica_groups=mesh['cons'=16,'blk_0'=2,'blk_1'=8,'blk_2'=2] {'blk_0','blk_1'}, dimensions={0} | all-to-all | bytes 2359296 | tf_op jit(solution)/shard_map/all_to_all | solution.py:432
  71.6 0.2 convert_reduce_fusion
  71.8 0.0 copy-done.7
  71.8 0.8 broadcast_in_dim.26
  72.6 5.1 %all-to-all-start.2 = ((bf16[8,48,768]{2,1,0:T(8,128)(2,1)}), bf16[8,48,768]{2,1,0:T(8,128)(2,1)S(1)}, u32[]{:S(2)}, u32[]{:S(2)}) async-start(bf16[8,48,768]{2,1,0:T(8,128)(2,1)} %broadcast_in_dim.26), calls=%async_computation.2 | async-start | bytes 1179648 | tf_op jit(solution)/shard_map/all_to_all | solution.py:436
  77.7 0.9 constant_dynamic-slice_fusion.1
  78.6 2.7 %collective-permute-start.1 = (bf16[12,40,768]{2,1,0:T(8,128)(2,1)}, bf16[12,40,768]{2,1,0:T(8,128)(2,1)}, u32[]{:S(2)}, u32[]{:S(2)}) collective-permute-start(bf16[12,40,768]{2,1,0:T(8,128)(2,1)} %constant_dynamic-slice_fusion.1), channel_id=1, source_target_pairs={{0,16},{1,17},{16,0},{17,1},{2,18},{3,19},{18,2},{19,3},{4,20},{5,... | collective-permute-start | bytes 2211848 | tf_op jit(solution)/shard_map/ppermute | solution.py:403
  81.4 2.0 %constant_dynamic-slice_fusion = bf16[12,40,768]{2,1,0:T(8,128)(2,1)} fusion(bf16[24,40,768]{2,1,0:T(8,128)(2,1)} %shard_map.83, s32[]{:T(128)S(6)} %select_n.4), kind=kLoop, calls=%fused_computation.3 | loop fusion | bytes 1474564 | tf_op jit(solution)/shard_map/dynamic_slice | solution.py:421
  83.4 6.2 %collective-permute-start.2 = (bf16[12,40,768]{2,1,0:T(8,128)(2,1)}, bf16[12,40,768]{2,1,0:T(8,128)(2,1)}, u32[]{:S(2)}, u32[]{:S(2)}) collective-permute-start(bf16[12,40,768]{2,1,0:T(8,128)(2,1)} %constant_dynamic-slice_fusion), channel_id=1, source_target_pairs={{0,17},{1,16},{16,1},{17,0},{2,19},{3,18},{18,3},{19,2},{4,21},{5,... | collective-permute-start | bytes 2211848 | tf_op jit(solution)/shard_map/ppermute | solution.py:403
  89.6 8.7 %collective-permute-done.1.refs_2_ = bf16[12,40,768]{2,1,0:T(8,128)(2,1)} collective-permute-done((bf16[12,40,768]{2,1,0:T(8,128)(2,1)}, bf16[12,40,768]{2,1,0:T(8,128)(2,1)}, u32[]{:S(2)}, u32[]{:S(2)}) %collective-permute-start.1) | collective-permute-done | bytes 737312 | tf_op jit(solution)/shard_map/ppermute | solution.py:403
  98.4 18.0 %collective-permute-done.2.refs_4_ = bf16[12,40,768]{2,1,0:T(8,128)(2,1)} collective-permute-done((bf16[12,40,768]{2,1,0:T(8,128)(2,1)}, bf16[12,40,768]{2,1,0:T(8,128)(2,1)}, u32[]{:S(2)}, u32[]{:S(2)}) %collective-permute-start.2) | collective-permute-done | bytes 737312 | tf_op jit(solution)/shard_map/ppermute | solution.py:403
  116.3 0.0 all-to-all-done.2
  116.3 2.7 %synthesis.1 = bf16[512,128]{1,0:T(8,128)(2,1)S(1)} custom-call(s32[1]{0:T(128)} %bitcast.spot_ref, s32[1]{0:T(128)} %bitcast.1.first_ref, bf16[384,768]{1,0:T(8,128)(2,1)S(1)} %bitcast.14, bf16[24,40,768]{2,1,0:T(8,128)(2,1)S(1)} %shard_map.82.refs_2_.refs_1_, bf16[12,40,768]{2,1,0:T(8,128)(2,1)} %collective-permute-done.1.refs_2_, ...), custom_call_target="tpu_custom_call" | custom-call | flops 94371840 | bytes 4194304 | tf_op jit(solution)/shard_map/synthesis/pallas_call | solution.py:289
  119.1 0.0 copy-start.2
  119.1 0.6 copy-done.2
  119.7 4.2 %all-to-all-start.3 = ((bf16[64,8,128]{2,1,0:T(8,128)(2,1)}), bf16[64,8,128]{2,1,0:T(8,128)(2,1)S(1)}, u32[]{:S(2)}, u32[]{:S(2)}) async-start(bf16[64,8,128]{2,1,0:T(8,128)(2,1)} %bitcast.15), calls=%async_computation.3 | async-start | bytes 262144 | tf_op jit(solution)/shard_map/all_to_all | solution.py:411
  123.9 0.0 copy-start.3
  124.0 0.9 copy-done.3
  124.8 0.0 copy-start.4
  124.8 0.9 copy-done.4
  125.7 0.1 shard_map.84.cosine_ref
  125.9 0.2 shard_map.85.sine_ref
  126.0 8.4 %all-to-all-done.3 = bf16[64,8,128]{2,1,0:T(8,128)(2,1)S(1)} async-done(((bf16[64,8,128]{2,1,0:T(8,128)(2,1)}), bf16[64,8,128]{2,1,0:T(8,128)(2,1)S(1)}, u32[]{:S(2)}, u32[]{:S(2)}) %all-to-all-start.3) | async-done | bytes 131104 | tf_op jit(solution)/shard_map/all_to_all | solution.py:411
  134.4 0.0 copy-start.6
  134.4 0.9 copy-done.6
  135.3 2.1 %inverse_dft.1 = f32[40,6144]{1,0:T(8,128)} custom-call(bf16[512,128]{1,0:T(8,128)(2,1)S(1)} %bitcast.17, bf16[256,768]{1,0:T(8,128)(2,1)S(1)} %shard_map.84.cosine_ref, bf16[256,768]{1,0:T(8,128)(2,1)S(1)} %shard_map.85.sine_ref, f32[2,24,768]{2,1,0:T(8,128)S(1)} %copy-done.6), custom_call_target="tpu_custom_call" | custom-call | flops 754974720 | bytes 1048576 | tf_op jit(solution)/shard_map/inverse_dft/pallas_call | solution.py:368
  (1 shorter events, 0.0 us)
Async XLA Ops:
  0.1 1.8 %copy-start = (bf16[40,48,768]{2,1,0:T(8,128)(2,1)S(1)}, bf16[40,48,768]{2,1,0:T(8,128)(2,1)}, u32[]{:S(2)}) copy-start(bf16[40,48,768]{2,1,0:T(8,128)(2,1)} %legendre_ref.3) | copy-start | bytes 8847364
  3.9 25.0 %collective-permute-start = (bf16[24,40,768]{2,1,0:T(8,128)(2,1)}, bf16[24,40,768]{2,1,0:T(8,128)(2,1)S(1)}, u32[]{:S(2)}, u32[]{:S(2)}) collective-permute-start(bf16[24,40,768]{2,1,0:T(8,128)(2,1)} %shard_map.83), channel_id=1, source_target_pairs={{0,1},{1,0},{16,17},{17,16},{2,3},{3,2},{18,19},{19,18},{4,5},{5,4... | collective-permute-start | bytes 4423688 | tf_op jit(solution)/shard_map/ppermute | solution.py:403
  16.0 13.0 %all-to-all-start = ((bf16[32,16,128]{2,1,0:T(8,128)(2,1)}), bf16[32,16,128]{2,1,0:T(8,128)(2,1)S(1)}, u32[]{:S(2)}, u32[]{:S(2)}) async-start(bf16[32,16,128]{2,1,0:T(8,128)(2,1)} %bitcast.18), calls=%async_computation | async-start | bytes 262144 | tf_op jit(solution)/shard_map/all_to_all | solution.py:411
  19.7 1.8 %copy-start.1 = (bf16[40,48,768]{2,1,0:T(8,128)(2,1)S(1)}, bf16[40,48,768]{2,1,0:T(8,128)(2,1)}, u32[]{:S(2)}) copy-start(bf16[40,48,768]{2,1,0:T(8,128)(2,1)} %legendre_ref.3) | copy-start | bytes 8847364
  21.5 7.5 %copy-start.5 = (s32[16]{0:T(128)S(1)}, s32[16]{0:T(128)}, u32[]{:S(2)}) copy-start(s32[16]{0:T(128)} %refs_0_.1) | copy-start | bytes 196
  30.3 41.5 %copy-start.7 = (f32[768]{0:T(1024)S(1)}, f32[768]{0:T(1024)}, u32[]{:S(2)}) copy-start(f32[768]{0:T(1024)} %param.11) | copy-start | bytes 9220
  72.6 43.7 %all-to-all-start.2 = ((bf16[8,48,768]{2,1,0:T(8,128)(2,1)}), bf16[8,48,768]{2,1,0:T(8,128)(2,1)S(1)}, u32[]{:S(2)}, u32[]{:S(2)}) async-start(bf16[8,48,768]{2,1,0:T(8,128)(2,1)} %broadcast_in_dim.26), calls=%async_computation.2 | async-start | bytes 1179648 | tf_op jit(solution)/shard_map/all_to_all | solution.py:436
  78.6 19.7 %collective-permute-start.1 = (bf16[12,40,768]{2,1,0:T(8,128)(2,1)}, bf16[12,40,768]{2,1,0:T(8,128)(2,1)}, u32[]{:S(2)}, u32[]{:S(2)}) collective-permute-start(bf16[12,40,768]{2,1,0:T(8,128)(2,1)} %constant_dynamic-slice_fusion.1), channel_id=1, source_target_pairs={{0,16},{1,17},{16,0},{17,1},{2,18},{3,19},{18,2},{19,3},{4,20},{5,... | collective-permute-start | bytes 2211848 | tf_op jit(solution)/shard_map/ppermute | solution.py:403
  83.4 32.9 %collective-permute-start.2 = (bf16[12,40,768]{2,1,0:T(8,128)(2,1)}, bf16[12,40,768]{2,1,0:T(8,128)(2,1)}, u32[]{:S(2)}, u32[]{:S(2)}) collective-permute-start(bf16[12,40,768]{2,1,0:T(8,128)(2,1)} %constant_dynamic-slice_fusion), channel_id=1, source_target_pairs={{0,17},{1,16},{16,1},{17,0},{2,19},{3,18},{18,3},{19,2},{4,21},{5,... | collective-permute-start | bytes 2211848 | tf_op jit(solution)/shard_map/ppermute | solution.py:403
  119.1 0.7 copy-start.2
  119.7 14.6 %all-to-all-start.3 = ((bf16[64,8,128]{2,1,0:T(8,128)(2,1)}), bf16[64,8,128]{2,1,0:T(8,128)(2,1)S(1)}, u32[]{:S(2)}, u32[]{:S(2)}) async-start(bf16[64,8,128]{2,1,0:T(8,128)(2,1)} %bitcast.15), calls=%async_computation.3 | async-start | bytes 262144 | tf_op jit(solution)/shard_map/all_to_all | solution.py:411
  123.9 0.9 copy-start.3
  124.8 0.9 copy-start.4
  134.4 0.9 copy-start.6

commit v8 on v7

--- a/solution.py
+++ b/solution.py
@@ -134,6 +134,11 @@
         half_ref[first : first + TILE] = jnp.swapaxes(
             legendre_ref[:, pl.ds(start, TILE), :], 0, 1
         )
+
+
+def part_kernel(place_ref, half_ref, part_ref):
+    share = part_ref.shape[0]
+    part_ref[...] = half_ref[pl.ds((1 - place_ref[1]) * share, share)]
 
 
 def divided(kernel, place, values, orders, cycles):
@@ -418,11 +423,12 @@
     sent, own = half_of(1), half_of(0)
 
     def part_of(values):
-        return lax.dynamic_slice_in_dim(values, (1 - side) * share, share, 0)
+        return divided(part_kernel, place, values, (share,), cycle_dev)[0]
 
     met = swapped(sent, 1)
     own_side = swapped(part_of(own), 2)
-    met_side = swapped(part_of(sent), 3)
+    sent_part = lax.dynamic_slice_in_dim(sent, (1 - side) * share, share, 0)
+    met_side = swapped(sent_part, 3)
     tables = [table_of(which, coarse, fine) for which in ("cosine", "sine")]
     lines = groups * orders_dev * 2 // (LANES // cycle_dev)
     packed = forward(elevation[0], cycle_weight[None, :], coarse, fine, turn, lines, groups * cores)

time: 138 us -> 141 us (1.022)
  waiting for transfers between devices: 41.6 us -> 43.3 us
    pallas_call x2 -> x3, Pallas kernels: 2.94 us -> 4.4 us  [divided(): pl.pallas_call(kernel, in_specs=[SCALARS, NEARBY], out_specs=[NEARBY] * l...]
    ppermute x3, waiting for transfers between devices: 26.7 us -> 28.2 us  [swapped(): return lax.ppermute(values, NEAR[::-1], pairs)]
    dynamic_slice x2 -> x1, local copies, waits for them, and re-layouts: 2.95 us -> 2.04 us  [local(): sent_part = lax.dynamic_slice_in_dim(sent, (1 - side) * share, share, 0)]
  transfers between devices with their start and end apart: 6 -> 6, of which waited for: 4 -> 4; matrix products, arithmetic and copies ran while one was open for 2% -> 1% of each run, Pallas kernels for 3% -> 4%
where the time goes in v8:
time: 141 us; the launch traced here: 140 us
  waiting for transfers between devices  43.3 us (31%)
  blocking collectives  41.3 us (29%)
  starting transfers between devices  31 us (22%)
  Pallas kernels  14.1 us (10%)
  local copies, waits for them, and re-layouts  9.91 us (7%)
    all_to_all x1, blocking collectives, local(): lax.all_to_all(partial.reshape(far, rows, degrees), FAR, 0, 0, tiled=True)  41.3 us
    ppermute x3, waiting for transfers between devices, swapped(): return lax.ppermute(values, NEAR[::-1], pairs)  28.2 us
    ppermute x3, starting transfers between devices, swapped(): return lax.ppermute(values, NEAR[::-1], pairs)  17.4 us
    all_to_all x2, waiting for transfers between devices, exchanged(): tiles = lax.all_to_all(tiles, axes, 0, 0, tiled=True)  15.2 us
    all_to_all x2, starting transfers between devices, exchanged(): tiles = lax.all_to_all(tiles, axes, 0, 0, tiled=True)  8.53 us
    unnamed x16, local copies, waits for them, and re-layouts  7.01 us
    all_to_all x1, starting transfers between devices, local(): coefficients = lax.all_to_all(copies, DEEP, 0, 0, tiled=True)  5.06 us
    pallas_call x3, Pallas kernels, divided(): pl.pallas_call(kernel, in_specs=[SCALARS, NEARBY], out_specs=[NEARBY] * l...  4.4 us
  transfers between devices with their start and end apart: 6, of which 4 were waited for; matrix products, arithmetic and copies ran while one was open for 1% of the time, Pallas kernels for 4%

profile of v8, /device:TPU:1, one launch (start us, length us, event | category | flops | bytes accessed | tf_op | source)
XLA Modules:
  0.0 140.0 jit_solution(11486001582920405252)
XLA Ops:
  0.0 0.1 pad_add_fusion.place_ref
  0.1 0.0 copy-start
  0.1 1.8 %copy-done = bf16[40,48,768]{2,1,0:T(8,128)(2,1)S(1)} copy-done((bf16[40,48,768]{2,1,0:T(8,128)(2,1)S(1)}, bf16[40,48,768]{2,1,0:T(8,128)(2,1)}, u32[]{:S(2)}) %copy-start) | copy-done | bytes 2949144
  1.9 2.0 %shard_map.83 = bf16[24,40,768]{2,1,0:T(8,128)(2,1)} custom-call(s32[2]{0:T(128)S(1)} %pad_add_fusion.place_ref, bf16[40,48,768]{2,1,0:T(8,128)(2,1)S(1)} %copy-done), custom_call_target="tpu_custom_call" | custom-call | flops 1048576 | bytes 2949120 | tf_op jit(solution)/shard_map/pallas_call | solution.py:146
  3.9 8.7 %collective-permute-start = (bf16[24,40,768]{2,1,0:T(8,128)(2,1)}, bf16[24,40,768]{2,1,0:T(8,128)(2,1)S(1)}, u32[]{:S(2)}, u32[]{:S(2)}) collective-permute-start(bf16[24,40,768]{2,1,0:T(8,128)(2,1)} %shard_map.83), channel_id=1, source_target_pairs={{0,1},{1,0},{16,17},{17,16},{2,3},{3,2},{18,19},{19,18},{4,5},{5,4... | collective-permute-start | bytes 4423688 | tf_op jit(solution)/shard_map/ppermute | solution.py:408
  12.7 3.3 %forward_dft.1 = bf16[512,128]{1,0:T(8,128)(2,1)} custom-call(bf16[40,6144]{1,0:T(8,128)(2,1)} %bitcast.19, f32[1,40]{1,0:T(1,128)} %bitcast.20, f32[2,16,768]{2,1,0:T(8,128)} %constant.33.clone.coarse_ref, f32[2,16,768]{2,1,0:T(8,128)} %constant.34.clone.fine_ref, f32[2,24,768]{2,1,0:T(8,128)} %constant.35.clone.turn_ref), custom_call_target="tpu_custom_call" | custom-call | flops 754974720 | bytes 1048576 | tf_op jit(solution)/shard_map/forward_dft/pallas_call | solution.py:111
  16.0 3.6 %all-to-all-start = ((bf16[32,16,128]{2,1,0:T(8,128)(2,1)}), bf16[32,16,128]{2,1,0:T(8,128)(2,1)S(1)}, u32[]{:S(2)}, u32[]{:S(2)}) async-start(bf16[32,16,128]{2,1,0:T(8,128)(2,1)} %bitcast.18), calls=%async_computation | async-start | bytes 262144 | tf_op jit(solution)/shard_map/all_to_all | solution.py:416
  19.7 0.0 copy-start.1
  19.7 1.8 %copy-done.1 = bf16[40,48,768]{2,1,0:T(8,128)(2,1)S(1)} copy-done((bf16[40,48,768]{2,1,0:T(8,128)(2,1)S(1)}, bf16[40,48,768]{2,1,0:T(8,128)(2,1)}, u32[]{:S(2)}) %copy-start.1) | copy-done | bytes 2949144
  21.5 0.0 copy-start.5
  21.5 0.9 shard_map.82.refs_2_.half_ref.refs_1_
  22.4 6.5 %all-to-all-done = bf16[32,16,128]{2,1,0:T(8,128)(2,1)S(1)} async-done(((bf16[32,16,128]{2,1,0:T(8,128)(2,1)}), bf16[32,16,128]{2,1,0:T(8,128)(2,1)S(1)}, u32[]{:S(2)}, u32[]{:S(2)}) %all-to-all-start) | async-done | bytes 131104 | tf_op jit(solution)/shard_map/all_to_all | solution.py:416
  29.0 0.0 collective-permute-done.refs_3_
  29.0 0.0 copy-done.5
  29.0 1.3 analysis.1
  30.3 0.0 copy-start.7
  30.3 41.3 %all_to_all.20 = bf16[16,48,768]{2,1,0:T(8,128)(2,1)S(1)} all-to-all(bf16[16,48,768]{2,1,0:T(8,128)(2,1)S(1)} %bitcast.13), channel_id=1, replica_groups=mesh['cons'=16,'blk_0'=2,'blk_1'=8,'blk_2'=2] {'blk_0','blk_1'}, dimensions={0} | all-to-all | bytes 2359296 | tf_op jit(solution)/shard_map/all_to_all | solution.py:438
  71.6 0.2 convert_reduce_fusion
  71.8 0.0 copy-done.7
  71.8 0.9 broadcast_in_dim.26
  72.6 5.1 %all-to-all-start.2 = ((bf16[8,48,768]{2,1,0:T(8,128)(2,1)}), bf16[8,48,768]{2,1,0:T(8,128)(2,1)S(1)}, u32[]{:S(2)}, u32[]{:S(2)}) async-start(bf16[8,48,768]{2,1,0:T(8,128)(2,1)} %broadcast_in_dim.26), calls=%async_computation.2 | async-start | bytes 1179648 | tf_op jit(solution)/shard_map/all_to_all | solution.py:442
  77.7 2.0 %constant_dynamic-slice_fusion = bf16[12,40,768]{2,1,0:T(8,128)(2,1)} fusion(bf16[24,40,768]{2,1,0:T(8,128)(2,1)} %shard_map.83, s32[]{:T(128)S(6)} %select_n.3), kind=kLoop, calls=%fused_computation.3 | loop fusion | bytes 1474564 | tf_op jit(solution)/shard_map/dynamic_slice | solution.py:430
  79.8 4.5 %collective-permute-start.2 = (bf16[12,40,768]{2,1,0:T(8,128)(2,1)}, bf16[12,40,768]{2,1,0:T(8,128)(2,1)}, u32[]{:S(2)}, u32[]{:S(2)}) collective-permute-start(bf16[12,40,768]{2,1,0:T(8,128)(2,1)} %constant_dynamic-slice_fusion), channel_id=1, source_target_pairs={{0,17},{1,16},{16,1},{17,0},{2,19},{3,18},{18,3},{19,2},{4,21},{5,... | collective-permute-start | bytes 2211848 | tf_op jit(solution)/shard_map/ppermute | solution.py:408
  84.3 1.5 %shard_map.84 = bf16[12,40,768]{2,1,0:T(8,128)(2,1)} custom-call(s32[2]{0:T(128)S(1)} %pad_add_fusion.place_ref, bf16[24,40,768]{2,1,0:T(8,128)(2,1)S(1)} %shard_map.82.refs_2_.half_ref.refs_1_), custom_call_target="tpu_custom_call" | custom-call | flops 1048576 | bytes 1474560 | tf_op jit(solution)/shard_map/pallas_call | solution.py:146
  85.7 4.1 %collective-permute-start.1 = (bf16[12,40,768]{2,1,0:T(8,128)(2,1)}, bf16[12,40,768]{2,1,0:T(8,128)(2,1)}, u32[]{:S(2)}, u32[]{:S(2)}) collective-permute-start(bf16[12,40,768]{2,1,0:T(8,128)(2,1)} %shard_map.84), channel_id=1, source_target_pairs={{0,16},{1,17},{16,0},{17,1},{2,18},{3,19},{18,2},{19,3},{4,20},{5,... | collective-permute-start | bytes 2211848 | tf_op jit(solution)/shard_map/ppermute | solution.py:408
  89.9 11.3 %collective-permute-done.2.refs_4_ = bf16[12,40,768]{2,1,0:T(8,128)(2,1)} collective-permute-done((bf16[12,40,768]{2,1,0:T(8,128)(2,1)}, bf16[12,40,768]{2,1,0:T(8,128)(2,1)}, u32[]{:S(2)}, u32[]{:S(2)}) %collective-permute-start.2) | collective-permute-done | bytes 737312 | tf_op jit(solution)/shard_map/ppermute | solution.py:408
  101.2 16.8 %collective-permute-done.1.refs_2_ = bf16[12,40,768]{2,1,0:T(8,128)(2,1)} collective-permute-done((bf16[12,40,768]{2,1,0:T(8,128)(2,1)}, bf16[12,40,768]{2,1,0:T(8,128)(2,1)}, u32[]{:S(2)}, u32[]{:S(2)}) %collective-permute-start.1) | collective-permute-done | bytes 737312 | tf_op jit(solution)/shard_map/ppermute | solution.py:408
  118.0 0.0 all-to-all-done.2
  118.0 2.7 %synthesis.1 = bf16[512,128]{1,0:T(8,128)(2,1)S(1)} custom-call(s32[1]{0:T(128)} %bitcast.spot_ref, s32[1]{0:T(128)} %bitcast.1.first_ref, bf16[384,768]{1,0:T(8,128)(2,1)S(1)} %bitcast.14, bf16[24,40,768]{2,1,0:T(8,128)(2,1)S(1)} %shard_map.82.refs_2_.half_ref.refs_1_, bf16[12,40,768]{2,1,0:T(8,128)(2,1)} %collective-permute-done.1.refs_2_, ...), custom_call_target="tpu_custom_call" | custom-call | flops 94371840 | bytes 4194304 | tf_op jit(solution)/shard_map/synthesis/pallas_call | solution.py:294
  120.8 0.0 copy-start.2
  120.8 0.6 copy-done.2
  121.5 4.9 %all-to-all-start.3 = ((bf16[64,8,128]{2,1,0:T(8,128)(2,1)}), bf16[64,8,128]{2,1,0:T(8,128)(2,1)S(1)}, u32[]{:S(2)}, u32[]{:S(2)}) async-start(bf16[64,8,128]{2,1,0:T(8,128)(2,1)} %bitcast.15), calls=%async_computation.3 | async-start | bytes 262144 | tf_op jit(solution)/shard_map/all_to_all | solution.py:416
  126.3 0.0 copy-start.3
  126.4 0.9 copy-done.3
  127.2 0.0 copy-start.4
  127.2 0.9 copy-done.4
  128.1 0.1 shard_map.85.cosine_ref
  128.3 0.2 shard_map.86.sine_ref
  128.4 8.6 %all-to-all-done.3 = bf16[64,8,128]{2,1,0:T(8,128)(2,1)S(1)} async-done(((bf16[64,8,128]{2,1,0:T(8,128)(2,1)}), bf16[64,8,128]{2,1,0:T(8,128)(2,1)S(1)}, u32[]{:S(2)}, u32[]{:S(2)}) %all-to-all-start.3) | async-done | bytes 131104 | tf_op jit(solution)/shard_map/all_to_all | solution.py:416
  137.0 0.0 copy-start.6
  137.0 0.9 copy-done.6
  137.9 2.1 %inverse_dft.1 = f32[40,6144]{1,0:T(8,128)} custom-call(bf16[512,128]{1,0:T(8,128)(2,1)S(1)} %bitcast.17, bf16[256,768]{1,0:T(8,128)(2,1)S(1)} %shard_map.85.cosine_ref, bf16[256,768]{1,0:T(8,128)(2,1)S(1)} %shard_map.86.sine_ref, f32[2,24,768]{2,1,0:T(8,128)S(1)} %copy-done.6), custom_call_target="tpu_custom_call" | custom-call | flops 754974720 | bytes 1048576 | tf_op jit(solution)/shard_map/inverse_dft/pallas_call | solution.py:373
  (1 shorter events, 0.0 us)
Async XLA Ops:
  0.1 1.8 %copy-start = (bf16[40,48,768]{2,1,0:T(8,128)(2,1)S(1)}, bf16[40,48,768]{2,1,0:T(8,128)(2,1)}, u32[]{:S(2)}) copy-start(bf16[40,48,768]{2,1,0:T(8,128)(2,1)} %legendre_ref.3) | copy-start | bytes 8847364
  3.9 25.0 %collective-permute-start = (bf16[24,40,768]{2,1,0:T(8,128)(2,1)}, bf16[24,40,768]{2,1,0:T(8,128)(2,1)S(1)}, u32[]{:S(2)}, u32[]{:S(2)}) collective-permute-start(bf16[24,40,768]{2,1,0:T(8,128)(2,1)} %shard_map.83), channel_id=1, source_target_pairs={{0,1},{1,0},{16,17},{17,16},{2,3},{3,2},{18,19},{19,18},{4,5},{5,4... | collective-permute-start | bytes 4423688 | tf_op jit(solution)/shard_map/ppermute | solution.py:408
  16.0 13.0 %all-to-all-start = ((bf16[32,16,128]{2,1,0:T(8,128)(2,1)}), bf16[32,16,128]{2,1,0:T(8,128)(2,1)S(1)}, u32[]{:S(2)}, u32[]{:S(2)}) async-start(bf16[32,16,128]{2,1,0:T(8,128)(2,1)} %bitcast.18), calls=%async_computation | async-start | bytes 262144 | tf_op jit(solution)/shard_map/all_to_all | solution.py:416
  19.7 1.8 %copy-start.1 = (bf16[40,48,768]{2,1,0:T(8,128)(2,1)S(1)}, bf16[40,48,768]{2,1,0:T(8,128)(2,1)}, u32[]{:S(2)}) copy-start(bf16[40,48,768]{2,1,0:T(8,128)(2,1)} %legendre_ref.3) | copy-start | bytes 8847364
  21.5 7.5 %copy-start.5 = (s32[16]{0:T(128)S(1)}, s32[16]{0:T(128)}, u32[]{:S(2)}) copy-start(s32[16]{0:T(128)} %refs_0_.1) | copy-start | bytes 196
  30.3 41.5 %copy-start.7 = (f32[768]{0:T(1024)S(1)}, f32[768]{0:T(1024)}, u32[]{:S(2)}) copy-start(f32[768]{0:T(1024)} %param.11) | copy-start | bytes 9220
  72.6 45.4 %all-to-all-start.2 = ((bf16[8,48,768]{2,1,0:T(8,128)(2,1)}), bf16[8,48,768]{2,1,0:T(8,128)(2,1)S(1)}, u32[]{:S(2)}, u32[]{:S(2)}) async-start(bf16[8,48,768]{2,1,0:T(8,128)(2,1)} %broadcast_in_dim.26), calls=%async_computation.2 | async-start | bytes 1179648 | tf_op jit(solution)/shard_map/all_to_all | solution.py:442
  79.8 21.5 %collective-permute-start.2 = (bf16[12,40,768]{2,1,0:T(8,128)(2,1)}, bf16[12,40,768]{2,1,0:T(8,128)(2,1)}, u32[]{:S(2)}, u32[]{:S(2)}) collective-permute-start(bf16[12,40,768]{2,1,0:T(8,128)(2,1)} %constant_dynamic-slice_fusion), channel_id=1, source_target_pairs={{0,17},{1,16},{16,1},{17,0},{2,19},{3,18},{18,3},{19,2},{4,21},{5,... | collective-permute-start | bytes 2211848 | tf_op jit(solution)/shard_map/ppermute | solution.py:408
  85.7 32.3 %collective-permute-start.1 = (bf16[12,40,768]{2,1,0:T(8,128)(2,1)}, bf16[12,40,768]{2,1,0:T(8,128)(2,1)}, u32[]{:S(2)}, u32[]{:S(2)}) collective-permute-start(bf16[12,40,768]{2,1,0:T(8,128)(2,1)} %shard_map.84), channel_id=1, source_target_pairs={{0,16},{1,17},{16,0},{17,1},{2,18},{3,19},{18,2},{19,3},{4,20},{5,... | collective-permute-start | bytes 2211848 | tf_op jit(solution)/shard_map/ppermute | solution.py:408
  120.8 0.7 copy-start.2
  121.5 15.6 %all-to-all-start.3 = ((bf16[64,8,128]{2,1,0:T(8,128)(2,1)}), bf16[64,8,128]{2,1,0:T(8,128)(2,1)S(1)}, u32[]{:S(2)}, u32[]{:S(2)}) async-start(bf16[64,8,128]{2,1,0:T(8,128)(2,1)} %bitcast.15), calls=%async_computation.3 | async-start | bytes 262144 | tf_op jit(solution)/shard_map/all_to_all | solution.py:416
  126.3 0.9 copy-start.3
  127.2 0.9 copy-start.4
  137.0 0.9 copy-start.6
